TPU v7x, 32 devices: a whole 2x2x4 slice. The times are simulated.
32 devices in a mesh: seq: 8 (over z, x), tp: 4 (over y, core).
Axes of the slice: x: 2, y: 2, z: 4, core: 2. Of those that a mesh axis runs over, the one named last changes fastest.
Arguments:
- tokens: bfloat16 [1024, 4608], P('seq'), may hold values from -6 to 6
- counts: int32 [8], P('seq'), may hold values from 0 to 32, as said below
- selected: int32 [8, 32], P('seq'), may hold values from 0 to 127, as said below
- router_w: float32 [4608], replicated, may hold values from -0.09375 to 0.09375
- pre_gain: float32 [4608], replicated, may hold values from 0.25 to 1.75
- post_gain: float32 [4608], replicated, may hold values from 0.25 to 1.75
- gate_w: bfloat16 [4608, 36864], P(None, ('seq', 'tp')), may hold values from -0.09375 to 0.09375
- up_w: bfloat16 [4608, 36864], P(None, ('seq', 'tp')), may hold values from -0.09375 to 0.09375
- down_w: bfloat16 [36864, 4608], P(('seq', 'tp')), may hold values from -0.0625 to 0.0625
Outputs:
- layer_out: bfloat16 [1024, 4608], P('seq')
Inputs may be any that keep to these rules, and one draw needn't show every extreme that they name: The counts sum to 128. For every shard s, the sum of the counts of the shards before s differs from s * 16 by at most 32. Each shard's first counts entries are distinct token positions of that shard in increasing order; the entries after them are padding and name no selected token.
All inputs are finite; a program needn't handle non-finite values.
Results may differ from a plain program's by a relative error of at most 0.003.
Values may be sent and summed in bfloat16 or wider, within the bound.
No kernel may reach another device: no remote copies, remote signals or barrier semaphores. Data moves between devices by JAX's collectives and lax.ppermute only.
A program may use at most 128 MiB of HBM per device.

v0:
```python
import jax
import jax.numpy as jnp
from jax import lax
from jax.sharding import PartitionSpec as P

EPS = 1e-06


def norm_rows(values, scale_vec):
    return values * lax.rsqrt(jnp.mean(values * values, axis=-1, keepdims=True) + EPS) * scale_vec


def body(tokens, counts, selected, router_w, pre_gain, post_gain, gate_w, up_w, down_w):
    tok_rows = tokens.shape[0]
    capacity = selected.shape[1]
    pair_count = lax.axis_size("tp")
    own_count = counts[0]
    chosen = selected[0]
    is_live = jnp.arange(capacity) < own_count
    positions = jnp.arange(tok_rows)
    picker = ((chosen[:, None] == positions[None, :]) & is_live[:, None]).astype(jnp.bfloat16)
    compact = jnp.dot(picker, tokens, preferred_element_type=jnp.float32).astype(jnp.bfloat16)
    row_total = compact.shape[0]
    piece_rows = row_total // pair_count
    tp_index = lax.axis_index("tp")
    rows_float = compact.astype(jnp.float32)
    weight = jax.nn.sigmoid(jnp.dot(rows_float, router_w, precision=lax.Precision.HIGHEST))
    normed = norm_rows(rows_float, pre_gain).astype(jnp.bfloat16)
    segment = lax.all_gather(normed, "seq", axis=0, tiled=True)
    gate_part = jnp.dot(segment, gate_w, preferred_element_type=jnp.float32)
    up_part = jnp.dot(segment, up_w, preferred_element_type=jnp.float32)
    hidden = (jax.nn.gelu(gate_part, approximate=True) * up_part).astype(jnp.bfloat16)
    mixed = lax.psum_scatter(
        jnp.dot(hidden, down_w, preferred_element_type=jnp.float32),
        ("seq", "tp"),
        scatter_dimension=0,
        tiled=True,
    )
    own_weight = lax.dynamic_slice_in_dim(weight, tp_index * piece_rows, piece_rows, 0)
    finished = own_weight[:, None] * norm_rows(mixed, post_gain)
    updates = lax.all_gather(finished.astype(jnp.bfloat16), "tp", axis=0, tiled=True).astype(
        finished.dtype
    )
    scattered = jnp.einsum(
        "ct,cd->td", picker.astype(jnp.float32), updates, precision=lax.Precision.HIGHEST
    )
    return (tokens.astype(jnp.float32) + scattered).astype(jnp.bfloat16)


def solution(mesh):
    in_specs = (
        P("seq", None),
        P("seq"),
        P("seq", None),
        P(),
        P(),
        P(),
        P(None, ("seq", "tp")),
        P(None, ("seq", "tp")),
        P(("seq", "tp"), None),
    )
    out_specs = P("seq", None)
    return jax.shard_map(body, mesh=mesh, in_specs=in_specs, out_specs=out_specs, check_vma=False)
```

profile of v0, /device:TPU:0, one launch (start us, length us, event | category | flops | bytes accessed | tf_op | source)
XLA Modules:
  0.0 212.9 jit_solution(5580388380556058634)
XLA Ops:
  6.5 0.0 all-gather.2.cloned.1.call-start
  7.2 1.7 fusion.13
  8.9 1.6 fusion.15
  10.5 0.0 all-gather.2.cloned.1.call-update
  10.6 0.0 reduce-scatter.2.cloned.1.call-start
  10.6 54.6 %all-gather.2.cloned.1.call-done = bf16[256,4608]{1,0:T(8,128)(2,1)} async-done(((bf16[32,4608]{1,0:T(8,128)(2,1)}), bf16[256,4608]{1,0:T(8,128)(2,1)}) %all-gather.2.cloned.1.call-update) | async-done | bytes 2359312 | tf_op jit(solution)/shard_map/all_gather | solution.py:29
  65.3 0.0 copy-start.4
  65.3 9.1 %fusion.28 = f32[256,1152]{1,0:T(8,128)} fusion(bf16[256,4608]{1,0:T(8,128)(2,1)} %all-gather.2.cloned.1.call-done, bf16[4608,1152]{1,0:T(8,128)(2,1)} %param.15), kind=kOutput, calls=%fused_computation.39 | convolution fusion | flops 2717908992 | bytes 14155776 | tf_op jit(solution)/shard_map/dot_general | solution.py:30
  74.4 0.0 copy-done.4
  74.4 15.9 %fusion.16 = f32[256,4608]{1,0:T(8,128)} fusion(bf16[1152,4608]{1,0:T(8,128)(2,1)} %param.17, bf16[256,4608]{1,0:T(8,128)(2,1)S(1)} %copy-done.4, bf16[4608,1152]{1,0:T(8,128)(2,1)} %param.16, f32[256,1152]{1,0:T(8,128)} %fusion.28), kind=kOutput, calls=%fused_computation.23 | convolution fusion | flops 5438767104 | bytes 29491200 | tf_op jit(solution)/shard_map/dot_general | solution.py:34
  90.3 0.0 copy-start.1
  90.3 0.0 copy-start.2
  90.3 0.0 copy-start
  90.3 0.0 copy-start.3
  90.3 0.0 reduce-scatter.2.cloned.1.call-update
  90.3 0.7 copy-done.1
  91.0 0.3 fusion.12
  91.3 0.1 dynamic_slice.3
  91.4 105.1 %reduce-scatter.2.cloned.1.call-done = f32[8,4608]{1,0:T(8,128)} async-done(((f32[256,4608]{1,0:T(8,128)}), f32[8,4608]{1,0:T(8,128)}) %reduce-scatter.2.cloned.1.call-update) | async-done | bytes 147472 | tf_op jit(solution)/shard_map/reduce_scatter | solution.py:33
  196.5 1.1 multiply_reduce_fusion
  197.6 0.0 copy-done.2
  197.6 1.0 multiply_convert_fusion
  198.6 5.9 %all_gather.7 = bf16[32,4608]{1,0:T(8,128)(2,1)S(1)} all-gather(bf16[8,4608]{1,0:T(8,128)(2,1)S(1)} %multiply_convert_fusion), channel_id=1, replica_groups=mesh['seq'=8,'tp'=4] {'tp'}, dimensions={0}, use_global_device_ids=true | all-gather | bytes 368640 | tf_op jit(solution)/shard_map/all_gather | solution.py:41
  204.5 0.0 copy-done
  204.5 0.0 copy-done.3
  204.5 1.6 fusion
  (4 shorter events, 0.0 us)
Async XLA Ops:
  6.5 58.7 %all-gather.2.cloned.1.call-start = ((), (), s32[]{:S(2)}) async-start(), calls=%async_computation.1 | async-start | bytes 2654208 | tf_op jit(solution)/shard_map/all_gather | solution.py:29
  10.6 185.9 %reduce-scatter.2.cloned.1.call-start = ((), (), s32[]{:S(2)}) async-start(), calls=%async_computation.2 | async-start | bytes 4866048 | tf_op jit(solution)/shard_map/reduce_scatter | solution.py:33
  65.3 9.1 %copy-start.4 = (bf16[256,4608]{1,0:T(8,128)(2,1)S(1)}, bf16[256,4608]{1,0:T(8,128)(2,1)}, u32[]{:S(2)}) copy-start(bf16[256,4608]{1,0:T(8,128)(2,1)} %all-gather.2.cloned.1.call-done) | copy-start | bytes 7077892
  90.3 0.7 copy-start.1
  90.3 107.3 %copy-start.2 = (f32[4608]{0:T(1024)S(1)}, f32[4608]{0:T(1024)}, u32[]{:S(2)}) copy-start(f32[4608]{0:T(1024)} %param.14) | copy-start | bytes 55300
  90.3 114.2 %copy-start = (bf16[128,4608]{1,0:T(8,128)(2,1)S(1)}, bf16[128,4608]{1,0:T(8,128)(2,1)}, u32[]{:S(2)}) copy-start(bf16[128,4608]{1,0:T(8,128)(2,1)} %param.9) | copy-start | bytes 3538948
  90.3 114.2 %copy-start.3 = (s32[1,32]{1,0:T(1,128)S(1)}, s32[1,32]{1,0:T(1,128)}, u32[]{:S(2)}) copy-start(s32[1,32]{1,0:T(1,128)} %param.11) | copy-start | bytes 388
Sparse Core Ops, SparseCore 0:
  10.7 54.5 all-gather.1
  90.4 106.0 reduce-scatter.1
where the time goes:
time: 213 us
  waiting for transfers between devices  160 us (75%)
  matrix products  28.7 us (13%)
  between operations  14.1 us (7%)
  blocking collectives  5.91 us (3%)
  other arithmetic  3.67 us (2%)
    reduce_scatter x1, waiting for transfers between devices, body(): lax.psum_scatter(jnp.dot(hidden, down_w, preferred_element_type=jnp.float...  105 us
    all_gather x1, waiting for transfers between devices, body(): segment = lax.all_gather(normed, 'seq', axis=0, tiled=True)  54.6 us
    dot_general x1, matrix products, body(): jnp.dot(hidden, down_w, preferred_element_type=jnp.float32)  15.9 us
    dot_general x1, matrix products, body(): gate_part = jnp.dot(segment, gate_w, preferred_element_type=jnp.float32)  9.1 us
    all_gather x1, blocking collectives, body(): lax.all_gather(finished.astype(jnp.bfloat16), 'tp', axis=0, tiled=True)  5.91 us
  transfers between devices with their start and end apart: 2, of which 2 were waited for; matrix products, arithmetic and copies ran while one was open for 0% of the time, Pallas kernels for 0%

commit v1 on v0

v1 whole, which is shorter than its diff:
```python
from functools import partial

import jax
import jax.numpy as jnp
from jax import lax
from jax.experimental import pallas as pl
from jax.experimental.pallas import tpu as pltpu
from jax.sharding import PartitionSpec as P

EPS = 1e-06
DEAD = 16384.0
LANES = 128
BF16 = jnp.bfloat16
F32 = jnp.float32
VMEM = pl.BlockSpec(memory_space=pltpu.VMEM)
SMEM = pl.BlockSpec(memory_space=pltpu.SMEM)
HBM = pl.BlockSpec(memory_space=pltpu.HBM)
CHUNKS = 4


def swap(value, axis, bits):
    size = lax.axis_size(axis)
    return lax.ppermute(value, axis, [(i, i ^ bits) for i in range(size)])


def iota(shape, dim):
    return lax.broadcasted_iota(jnp.int32, shape, dim)


def dot_f32(left, right):
    return jnp.dot(left, right, preferred_element_type=F32)


def dot_rows(left, right):
    return lax.dot_general(left, right, (((0,), (0,)), ((), ())), preferred_element_type=F32)


def picker(chosen, count, tok_rows):
    shape = (tok_rows, chosen.shape[1])
    hit = (iota(shape, 0) == chosen) & (iota(shape, 1) < count)
    return jnp.where(hit, 1.0, 0.0).astype(BF16)


def chunks(width):
    step = width // CHUNKS
    return [(part, slice(part * step, (part + 1) * step)) for part in range(CHUNKS)]


def scaled(values, gain):
    parts = [values[:, i * LANES : (i + 1) * LANES] * gain[i : i + 1, :] for i in range(gain.shape[0])]
    return jnp.concatenate(parts, 1)


def prepare_kernel(counts, tp_at, seq_at, chosen, tokens, gain, own, rows, chosen_v, tokens_v, gain_v, done, sems):
    del seq_at
    capacity, piece = own.shape
    width = tokens.shape[1]
    copies = [
        pltpu.make_async_copy(tokens.at[:, at], tokens_v.at[:, at], sems.at[part]) for part, at in chunks(width)
    ]
    small = [
        pltpu.make_async_copy(chosen, chosen_v, done.at[0]),
        pltpu.make_async_copy(gain, gain_v, done.at[1]),
    ]
    for copy in small[:1] + copies + small[1:]:
        copy.start()
    small[0].wait()
    picked = picker(chosen_v[...], counts[0], tokens.shape[0])
    square = jnp.zeros((capacity, 1), F32)
    for part, at in chunks(width):
        copies[part].wait()
        values = dot_rows(picked, tokens_v[:, at])
        rows[:, at] = values.astype(BF16)
        square = square + jnp.sum(values * values, axis=1, keepdims=True)
    small[1].wait()
    scale = lax.rsqrt(square / width + EPS)
    live = iota((capacity, 1), 0) < counts[0]
    for i in range(piece // LANES):
        at = pl.multiple_of(tp_at[0] * piece + i * LANES, LANES)
        part = rows[:, pl.ds(at, LANES)].astype(F32) * scale
        part = part * gain_v[pl.ds(tp_at[0] * (piece // LANES) + i, 1), :]
        own[:, i * LANES : (i + 1) * LANES] = jnp.where(live, part, DEAD).astype(BF16)


def weight_kernel(rows, router_w, weight):
    logit = jnp.sum(scaled(rows[...].astype(F32), router_w[...]), axis=1, keepdims=True)
    weight[...] = jnp.broadcast_to(jax.nn.sigmoid(logit), weight.shape)


def pack_kernel(seq_at, *refs):
    pieces, (packed, places) = refs[:-2], refs[-2:]
    capacity = pieces[0].shape[0]
    held = jnp.concatenate([ref[...] for ref in pieces], 0)
    count = held.shape[0]
    live = held[:, :LANES].astype(F32) < DEAD / 2
    live_bf16 = jnp.where(live, 1.0, 0.0).astype(BF16)
    before = (seq_at[0] ^ (iota((count, count), 1) // capacity)) < (seq_at[0] ^ (iota((count, count), 0) // capacity))
    first = dot_f32(jnp.where(before, 1.0, 0.0).astype(BF16), live_bf16).astype(jnp.int32)
    target = first + (iota((count, LANES), 0) % capacity)
    for part in range(places.shape[1] // LANES):
        hit = (target == iota((count, LANES), 1) + part * LANES) & live
        places[:, part * LANES : (part + 1) * LANES] = jnp.where(hit, 1.0, 0.0).astype(BF16)
    packed[...] = dot_rows(places[...], held).astype(BF16)


def start_kernel(tp_at, first, second, gate_w, up_w, gate_out, up_out):
    deep = first.shape[1]
    for weights, result in ((gate_w, gate_out), (up_w, up_out)):
        total = None
        for far, rows in ((0, first), (1, second)):
            at = pl.multiple_of((tp_at[0] ^ far) * deep, LANES)
            part = dot_f32(rows[...], weights[pl.ds(at, deep), :])
            total = part if total is None else total + part
        result[...] = total


def finish_kernel(tp_at, third, fourth, gate_in, up_in, gate_w, up_w, hidden):
    deep = third.shape[1]
    sums = []
    for weights, before in ((gate_w, gate_in), (up_w, up_in)):
        total = before[...]
        for far, rows in ((2, third), (3, fourth)):
            at = pl.multiple_of((tp_at[0] ^ far) * deep, LANES)
            total = total + dot_f32(rows[...], weights[pl.ds(at, deep), :])
        sums.append(total)
    hidden[...] = (jax.nn.gelu(sums[0], approximate=True) * sums[1]).astype(BF16)


def down_kernel(far, tp_at, hidden, down_w, *refs):
    result = refs[-1]
    wide = result.shape[1]
    at = pl.multiple_of((tp_at[0] ^ far) * wide, LANES)
    total = dot_f32(hidden[...], down_w[:, pl.ds(at, wide)])
    for ref in refs[:-1]:
        total = total + ref[...].astype(F32)
    result[...] = total.astype(result.dtype)


def window_kernel(near, far, places, *windows):
    total = (near[...] + far[...].astype(F32)).astype(BF16)
    capacity = windows[0].shape[0]
    for slot, window in enumerate(windows):
        rows = places[slot * capacity : (slot + 1) * capacity, :]
        window[...] = dot_f32(rows, total).astype(BF16)


def sum_kernel(*refs):
    total = refs[0][...].astype(F32)
    for ref in refs[1:-1]:
        total = total + ref[...].astype(F32)
    refs[-1][...] = total.astype(BF16)


def finish_rows_kernel(counts, tp_at, chosen, tokens, weight, gain, *refs):
    parts, (out, joined, staged, sems) = refs[:-4], refs[-4:]
    width = tokens.shape[1]
    piece = width // len(parts)
    for far, part in enumerate(parts):
        joined[:, pl.ds(pl.multiple_of((tp_at[0] ^ far) * piece, LANES), piece)] = part[...].astype(F32)
    values = joined[...]
    scale = lax.rsqrt(jnp.mean(values * values, axis=1, keepdims=True) + EPS) * weight[:, :1]
    picked = picker(chosen[...], counts[0], tokens.shape[0])
    rows = gain.shape[0] // CHUNKS
    copies = []
    for part, at in chunks(width):
        update = scaled(values[:, at] * scale, gain[part * rows : (part + 1) * rows, :]).astype(BF16)
        staged[:, at] = (tokens[:, at].astype(F32) + dot_f32(picked, update)).astype(BF16)
        copies.append(pltpu.make_async_copy(staged.at[:, at], out.at[:, at], sems.at[part]))
        copies[-1].start()
    for copy in copies:
        copy.wait()


def call(kernel, shapes, scalars, operands, flops=0, scratch=(), spec=None, out_spec=None):
    return pl.pallas_call(
        kernel,
        out_shape=shapes,
        in_specs=[SMEM] * len(scalars) + [spec or VMEM] * len(operands),
        out_specs=jax.tree.map(lambda _: out_spec or VMEM, shapes),
        scratch_shapes=scratch,
        compiler_params=pltpu.CompilerParams(vmem_limit_bytes=8 << 20),
        cost_estimate=pl.CostEstimate(flops=flops, bytes_accessed=0, transcendentals=0),
    )(*scalars, *operands)


def array(rows, columns, kind=BF16):
    return jax.ShapeDtypeStruct((rows, columns), kind)


def layer(tokens, counts, selected, router_w, pre_gain, post_gain, gate_w, up_w, down_w):
    tok_rows, width = tokens.shape
    capacity = selected.shape[1]
    shards = lax.axis_size("seq")
    pair_count = lax.axis_size("tp")
    units = gate_w.shape[1]
    total = shards * capacity // 2
    piece = width // pair_count
    seq_at = lax.axis_index("seq").astype(jnp.int32).reshape(1)
    tp_at = lax.axis_index("tp").astype(jnp.int32).reshape(1)

    own, rows = call(
        prepare_kernel,
        (array(capacity, piece), array(capacity, width)),
        (counts, tp_at, seq_at),
        [
            pltpu.with_memory_space_constraint(value, pltpu.HBM)
            for value in (selected, tokens, pre_gain.reshape(-1, LANES))
        ],
        scratch=(
            pltpu.VMEM(selected.shape, jnp.int32),
            pltpu.VMEM(tokens.shape, BF16),
            pltpu.VMEM((width // LANES, LANES), F32),
            pltpu.SemaphoreType.DMA((2,)),
            pltpu.SemaphoreType.DMA((CHUNKS,)),
        ),
        spec=HBM,
    )
    weight = call(
        weight_kernel,
        array(capacity, LANES, F32),
        (),
        (rows, router_w.reshape(-1, LANES)),
        flops=64 * total * width * units,
    )

    held = {0: own}
    for far in range(2, shards, 2):
        held[far] = swap(own, "seq", far)
    beside, weight = lax.optimization_barrier((own, weight))
    for far in range(0, shards, 2):
        held[far + 1] = swap(held[far] if far else beside, "seq", 1)
    packed, places = call(
        pack_kernel,
        (array(total, piece), array(shards * capacity, total)),
        (seq_at,),
        [held[far] for far in range(shards)],
        flops=16 * total * piece * units,
    )

    flops = 2 * total * piece * units
    third = swap(packed, "tp", 2)
    second = swap(packed, "tp", 1)
    sums = call(
        start_kernel,
        (array(total, units, F32), array(total, units, F32)),
        (tp_at,),
        (packed, second, gate_w, up_w),
        4 * flops,
    )
    third, sums = lax.optimization_barrier((third, sums))
    fourth = swap(third, "tp", 1)
    hidden = call(
        finish_kernel, array(total, units), (tp_at,), (third, fourth, *sums, gate_w, up_w), 4 * flops
    )

    def down(far, kind, *extra):
        return call(partial(down_kernel, far), array(total, piece, kind), (tp_at,), (hidden, down_w, *extra), flops)

    far_away = swap(down(3, BF16), "tp", 1)
    near_away = swap(down(1, BF16), "tp", 1)
    far_sum = swap(down(2, BF16, far_away), "tp", 2)
    near_sum = down(0, F32, near_away)
    windows = call(
        window_kernel, [array(capacity, piece)] * shards, (), (near_sum, far_sum, places)
    )
    arrived = []
    for far in range(shards - 2, 0, -2):
        other = swap(windows[far + 1], "seq", 1)
        arrived.append(swap(call(sum_kernel, array(capacity, piece), (), (windows[far], other)), "seq", far))
    other = swap(windows[1], "seq", 1)
    final = call(sum_kernel, array(capacity, piece), (), (windows[0], other, *arrived))
    other_far = swap(final, "tp", 2)
    other_near = swap(final, "tp", 1)
    last = swap(other_far, "tp", 1)
    return call(
        finish_rows_kernel,
        array(tok_rows, width),
        (counts, tp_at),
        (selected, tokens, weight, post_gain.reshape(-1, LANES), final, other_near, other_far, last),
        scratch=(
            pltpu.VMEM((capacity, width), F32),
            pltpu.VMEM(tokens.shape, BF16),
            pltpu.SemaphoreType.DMA((CHUNKS,)),
        ),
        out_spec=HBM,
    )


def solution(mesh):
    in_specs = (
        P("seq", None),
        P("seq"),
        P("seq", None),
        P(),
        P(),
        P(),
        P(None, ("seq", "tp")),
        P(None, ("seq", "tp")),
        P(("seq", "tp"), None),
    )
    return jax.shard_map(layer, mesh=mesh, in_specs=in_specs, out_specs=P("seq", None), check_vma=False)
```

time: 213 us -> 67.5 us (0.32)
  waiting for transfers between devices: 160 us -> 28.8 us
  matrix products: 28.7 us -> 0 us
  starting transfers between devices: 0.04 us -> 25.1 us
  between operations: 14.1 us -> 0.88 us
  Pallas kernels: 0 us -> 11.1 us
  blocking collectives: 5.91 us -> 0 us
  other arithmetic: 3.67 us -> 0.01 us
    reduce_scatter x1 -> x0, waiting for transfers between devices: 105 us -> none  [body(): lax.psum_scatter(jnp.dot(hidden, down_w, preferred_element_type=jnp.float...]
    all_gather x1 -> x0, waiting for transfers between devices: 54.6 us -> none  [body(): segment = lax.all_gather(normed, 'seq', axis=0, tiled=True)]
    ppermute x0 -> x23, waiting for transfers between devices: none -> 28.8 us  [swap(): return lax.ppermute(value, axis, [(i, i ^ bits) for i in range(size)])]
    dot_general x5 -> x0, matrix products: 28.7 us -> none  [the longest x1 15.9 us: body(): jnp.dot(hidden, down_w, preferred_element_type=jnp.float32)]
    ppermute x0 -> x23, starting transfers between devices: none -> 25.1 us  [swap(): return lax.ppermute(value, axis, [(i, i ^ bits) for i in range(size)])]
    pallas_call x0 -> x15, Pallas kernels: none -> 11.1 us  [call(): pl.pallas_call(kernel, out_shape=shapes, in_specs=[SMEM] * len(scalars) +...]
    all_gather x1 -> x0, blocking collectives: 5.91 us -> none  [body(): lax.all_gather(finished.astype(jnp.bfloat16), 'tp', axis=0, tiled=True)]
    convert_element_type x2 -> x0, other arithmetic: 2.59 us -> none  [the longest x1 1.59 us: body(): normed = norm_rows(rows_float, pre_gain).astype(jnp.bfloat16)]
  transfers between devices with their start and end apart: 2 -> 23, of which waited for: 2 -> 13; matrix products, arithmetic and copies ran while one was open for 0% -> 0% of each run, Pallas kernels for 0% -> 6%
where the time goes in v1:
time: 67.5 us; the launch traced here: 67.4 us
  waiting for transfers between devices  28.8 us (43%)
  starting transfers between devices  25.1 us (37%)
  Pallas kernels  11.1 us (16%)
  local copies, waits for them, and re-layouts  1.46 us (2%)
  between operations  0.88 us (1%)
    ppermute x23, waiting for transfers between devices, swap(): return lax.ppermute(value, axis, [(i, i ^ bits) for i in range(size)])  28.8 us
    ppermute x23, starting transfers between devices, swap(): return lax.ppermute(value, axis, [(i, i ^ bits) for i in range(size)])  25.1 us
    pallas_call x15, Pallas kernels, call(): pl.pallas_call(kernel, out_shape=shapes, in_specs=[SMEM] * len(scalars) +...  11.1 us
    unnamed x26, local copies, waits for them, and re-layouts  1.46 us
  transfers between devices with their start and end apart: 23, of which 13 were waited for; matrix products, arithmetic and copies ran while one was open for 0% of the time, Pallas kernels for 6%

profile of v1, /device:TPU:0, one launch (start us, length us, event | category | flops | bytes accessed | tf_op | source)
XLA Modules:
  0.0 67.4 jit_solution(17938921227543994265)
XLA Ops:
  0.7 2.1 %shard_map.91 = (bf16[32,1152]{1,0:T(8,128)(2,1)S(1)}, bf16[32,4608]{1,0:T(8,128)(2,1)S(1)}) custom-call(s32[1]{0:T(128)S(6)} %copy.10.counts, s32[1]{0:T(128)} %bitcast.tp_at, s32[1]{0:T(128)} %bitcast.1.seq_at, s32[1,32]{1,0:T(1,128)} %chosen.3, bf16[128,4608]{1,0:T(8,128)(2,1)} %tokens.3, f32[36,128]{1,0:T(8,128)} %bitcast.13), custom_call_target="tpu_custom_call" | custom-call | tf_op jit(solution)/shard_map/pallas_call | solution.py:175
  2.8 5.1 %collective-permute-start.5 = (bf16[32,1152]{1,0:T(8,128)(2,1)S(1)}, bf16[32,1152]{1,0:T(8,128)(2,1)S(1)}, u32[]{:S(2)}, u32[]{:S(2)}) collective-permute-start(bf16[32,1152]{1,0:T(8,128)(2,1)S(1)} %get-tuple-element.27.refs_0_), channel_id=1, source_target_pairs={{0,24},{4,28},{8,16},{12,20},{16,8},{20,12},{24,0},{28,4},{1,25},{... | collective-permute-start | bytes 221192 | tf_op jit(solution)/shard_map/ppermute | solution.py:23
  7.9 0.0 collective-permute-start.3
  7.9 0.6 collective-permute-start.1
  8.6 0.9 %copy-done.3 = f32[4608]{0:T(1024)S(1)} copy-done((f32[4608]{0:T(1024)S(1)}, f32[4608]{0:T(1024)}, u32[]{:S(2)}) %copy-start.3) | copy-done | bytes 18456
  9.5 0.1 shard_map.92.weight
  9.6 1.7 %collective-permute-start = (bf16[32,1152]{1,0:T(8,128)(2,1)S(1)}, bf16[32,1152]{1,0:T(8,128)(2,1)S(1)}, u32[]{:S(2)}, u32[]{:S(2)}) collective-permute-start(bf16[32,1152]{1,0:T(8,128)(2,1)S(1)} %get-tuple-element.27.refs_0_), channel_id=1, source_target_pairs={{0,4},{4,0},{8,12},{12,8},{16,20},{20,16},{24,28},{28,24},{1,5},{5... | collective-permute-start | bytes 221192 | tf_op jit(solution)/shard_map/ppermute | solution.py:23
  11.3 0.0 collective-permute-done.5.refs_6_
  11.3 1.2 %collective-permute-start.6 = (bf16[32,1152]{1,0:T(8,128)(2,1)S(1)}, bf16[32,1152]{1,0:T(8,128)(2,1)S(1)}, u32[]{:S(2)}, u32[]{:S(2)}) collective-permute-start(bf16[32,1152]{1,0:T(8,128)(2,1)S(1)} %collective-permute-done.5.refs_6_), channel_id=1, source_target_pairs={{0,4},{4,0},{8,12},{12,8},{16,20},{20,16},{24,28},{28,24},{1,5},{5... | collective-permute-start | bytes 221192 | tf_op jit(solution)/shard_map/ppermute | solution.py:23
  12.5 1.6 %collective-permute-done.3.refs_4_ = bf16[32,1152]{1,0:T(8,128)(2,1)S(1)} collective-permute-done((bf16[32,1152]{1,0:T(8,128)(2,1)S(1)}, bf16[32,1152]{1,0:T(8,128)(2,1)S(1)}, u32[]{:S(2)}, u32[]{:S(2)}) %collective-permute-start.3) | collective-permute-done | bytes 73760 | tf_op jit(solution)/shard_map/ppermute | solution.py:23
  14.1 1.5 %collective-permute-start.4 = (bf16[32,1152]{1,0:T(8,128)(2,1)S(1)}, bf16[32,1152]{1,0:T(8,128)(2,1)S(1)}, u32[]{:S(2)}, u32[]{:S(2)}) collective-permute-start(bf16[32,1152]{1,0:T(8,128)(2,1)S(1)} %collective-permute-done.3.refs_4_), channel_id=1, source_target_pairs={{0,4},{4,0},{8,12},{12,8},{16,20},{20,16},{24,28},{28,24},{1,5},{5... | collective-permute-start | bytes 221192 | tf_op jit(solution)/shard_map/ppermute | solution.py:23
  15.6 0.0 collective-permute-done.1.refs_2_
  15.6 0.5 collective-permute-start.2
  16.2 0.0 collective-permute-done.refs_1_
  16.2 0.0 collective-permute-done.6.refs_7_
  16.2 3.0 %collective-permute-done.4.refs_5_ = bf16[32,1152]{1,0:T(8,128)(2,1)S(1)} collective-permute-done((bf16[32,1152]{1,0:T(8,128)(2,1)S(1)}, bf16[32,1152]{1,0:T(8,128)(2,1)S(1)}, u32[]{:S(2)}, u32[]{:S(2)}) %collective-permute-start.4) | collective-permute-done | bytes 73760 | tf_op jit(solution)/shard_map/ppermute | solution.py:23
  19.1 0.8 %collective-permute-done.2.refs_3_ = bf16[32,1152]{1,0:T(8,128)(2,1)S(1)} collective-permute-done((bf16[32,1152]{1,0:T(8,128)(2,1)S(1)}, bf16[32,1152]{1,0:T(8,128)(2,1)S(1)}, u32[]{:S(2)}, u32[]{:S(2)}) %collective-permute-start.2) | collective-permute-done | bytes 73760 | tf_op jit(solution)/shard_map/ppermute | solution.py:23
  20.0 0.5 shard_map.93
  20.5 0.1 collective-permute-start.8
  20.6 1.6 %collective-permute-start.7 = (bf16[128,1152]{1,0:T(8,128)(2,1)S(1)}, bf16[128,1152]{1,0:T(8,128)(2,1)S(1)}, u32[]{:S(2)}, u32[]{:S(2)}) collective-permute-start(bf16[128,1152]{1,0:T(8,128)(2,1)S(1)} %get-tuple-element.28.first), channel_id=1, source_target_pairs={{0,2},{1,3},{2,0},{3,1},{4,6},{5,7},{6,4},{7,5},{8,10},{9,11},{10,... | collective-permute-start | bytes 884744 | tf_op jit(solution)/shard_map/ppermute | solution.py:23
  22.2 0.0 collective-permute-done.8.second
  22.2 0.0 slice-done.6
  22.2 1.9 %shard_map.94 = (f32[128,1152]{1,0:T(8,128)S(1)}, f32[128,1152]{1,0:T(8,128)S(1)}) custom-call(s32[1]{0:T(128)} %bitcast.tp_at, bf16[128,1152]{1,0:T(8,128)(2,1)S(1)} %get-tuple-element.28.first, bf16[128,1152]{1,0:T(8,128)(2,1)S(1)} %collective-permute-done.8.second, bf16[4608,1152]{1,0:T(8,128)(2,1)S(1)} %bitcast.8, bf16[4608,1152]{1,0:T(8,128)(2,1)S(1)} %bitcast.10), custom_call_target="tpu_custom_call" | custom-call | flops 1358954496 | tf_op jit(solution)/shard_map/pallas_call | solution.py:175
  24.1 5.9 %collective-permute-done.7.third = bf16[128,1152]{1,0:T(8,128)(2,1)S(1)} collective-permute-done((bf16[128,1152]{1,0:T(8,128)(2,1)S(1)}, bf16[128,1152]{1,0:T(8,128)(2,1)S(1)}, u32[]{:S(2)}, u32[]{:S(2)}) %collective-permute-start.7) | collective-permute-done | bytes 294944 | tf_op jit(solution)/shard_map/ppermute | solution.py:23
  30.0 0.0 collective-permute-start.9
  30.0 1.6 %collective-permute-done.9.fourth = bf16[128,1152]{1,0:T(8,128)(2,1)S(1)} collective-permute-done((bf16[128,1152]{1,0:T(8,128)(2,1)S(1)}, bf16[128,1152]{1,0:T(8,128)(2,1)S(1)}, u32[]{:S(2)}, u32[]{:S(2)}) %collective-permute-start.9) | collective-permute-done | bytes 294944 | tf_op jit(solution)/shard_map/ppermute | solution.py:23
  31.6 2.0 %shard_map.95.hidden = bf16[128,1152]{1,0:T(8,128)(2,1)S(1)} custom-call(s32[1]{0:T(128)} %bitcast.tp_at, bf16[128,1152]{1,0:T(8,128)(2,1)S(1)} %collective-permute-done.7.third, bf16[128,1152]{1,0:T(8,128)(2,1)S(1)} %collective-permute-done.9.fourth, f32[128,1152]{1,0:T(8,128)S(1)} %get-tuple-element.32.gate_in, f32[128,1152]{1,0:T(8,128)S(1)} %get-tuple-element.33.up_in, ...), custom_call_target="tpu_custom_call" | custom-call | flops 1358954496 | tf_op jit(solution)/shard_map/pallas_call | solution.py:175
  33.6 0.5 slice-done.2
  34.1 0.6 shard_map.98
  34.7 0.1 collective-permute-start.11
  34.8 0.6 shard_map.96
  35.4 0.0 copy-start
  35.4 0.0 copy-start.1
  35.4 0.0 copy-start.2
  35.4 0.6 collective-permute-start.10
  36.0 0.4 collective-permute-done.11.refs_0_
  36.4 0.6 shard_map.99
  37.0 1.6 %collective-permute-start.12 = (bf16[128,1152]{1,0:T(8,128)(2,1)S(1)}, bf16[128,1152]{1,0:T(8,128)(2,1)S(1)}, u32[]{:S(2)}, u32[]{:S(2)}) collective-permute-start(bf16[128,1152]{1,0:T(8,128)(2,1)S(1)} %shard_map.99), channel_id=1, source_target_pairs={{0,2},{1,3},{2,0},{3,1},{4,6},{5,7},{6,4},{7,5},{8,10},{9,11},{10,... | collective-permute-start | bytes 884744 | tf_op jit(solution)/shard_map/ppermute | solution.py:23
  38.5 0.0 collective-permute-done.10.refs_0_
  38.5 0.6 shard_map.97.near
  39.1 6.9 %collective-permute-done.12.far = bf16[128,1152]{1,0:T(8,128)(2,1)S(1)} collective-permute-done((bf16[128,1152]{1,0:T(8,128)(2,1)S(1)}, bf16[128,1152]{1,0:T(8,128)(2,1)S(1)}, u32[]{:S(2)}, u32[]{:S(2)}) %collective-permute-start.12) | collective-permute-done | bytes 294944 | tf_op jit(solution)/shard_map/ppermute | solution.py:23
  46.1 0.5 shard_map.100
  46.6 1.1 %collective-permute-start.14 = (bf16[32,1152]{1,0:T(8,128)(2,1)S(1)}, bf16[32,1152]{1,0:T(8,128)(2,1)S(1)}, u32[]{:S(2)}, u32[]{:S(2)}) collective-permute-start(bf16[32,1152]{1,0:T(8,128)(2,1)S(1)} %get-tuple-element.38), channel_id=1, source_target_pairs={{0,4},{4,0},{8,12},{12,8},{16,20},{20,16},{24,28},{28,24},{1,5},{5... | collective-permute-start | bytes 221192 | tf_op jit(solution)/shard_map/ppermute | solution.py:23
  47.6 1.0 %collective-permute-start.16 = (bf16[32,1152]{1,0:T(8,128)(2,1)S(1)}, bf16[32,1152]{1,0:T(8,128)(2,1)S(1)}, u32[]{:S(2)}, u32[]{:S(2)}) collective-permute-start(bf16[32,1152]{1,0:T(8,128)(2,1)S(1)} %get-tuple-element.40), channel_id=1, source_target_pairs={{0,4},{4,0},{8,12},{12,8},{16,20},{20,16},{24,28},{28,24},{1,5},{5... | collective-permute-start | bytes 221192 | tf_op jit(solution)/shard_map/ppermute | solution.py:23
  48.6 1.0 %collective-permute-start.18 = (bf16[32,1152]{1,0:T(8,128)(2,1)S(1)}, bf16[32,1152]{1,0:T(8,128)(2,1)S(1)}, u32[]{:S(2)}, u32[]{:S(2)}) collective-permute-start(bf16[32,1152]{1,0:T(8,128)(2,1)S(1)} %get-tuple-element.42), channel_id=1, source_target_pairs={{0,4},{4,0},{8,12},{12,8},{16,20},{20,16},{24,28},{28,24},{1,5},{5... | collective-permute-start | bytes 221192 | tf_op jit(solution)/shard_map/ppermute | solution.py:23
  49.7 1.0 %collective-permute-start.13 = (bf16[32,1152]{1,0:T(8,128)(2,1)S(1)}, bf16[32,1152]{1,0:T(8,128)(2,1)S(1)}, u32[]{:S(2)}, u32[]{:S(2)}) collective-permute-start(bf16[32,1152]{1,0:T(8,128)(2,1)S(1)} %get-tuple-element.36), channel_id=1, source_target_pairs={{0,4},{4,0},{8,12},{12,8},{16,20},{20,16},{24,28},{28,24},{1,5},{5... | collective-permute-start | bytes 221192 | tf_op jit(solution)/shard_map/ppermute | solution.py:23
  50.7 1.1 %collective-permute-done.14.refs_1_ = bf16[32,1152]{1,0:T(8,128)(2,1)S(1)} collective-permute-done((bf16[32,1152]{1,0:T(8,128)(2,1)S(1)}, bf16[32,1152]{1,0:T(8,128)(2,1)S(1)}, u32[]{:S(2)}, u32[]{:S(2)}) %collective-permute-start.14) | collective-permute-done | bytes 73760 | tf_op jit(solution)/shard_map/ppermute | solution.py:23
  51.8 2.8 %collective-permute-start.15 = (bf16[32,1152]{1,0:T(8,128)(2,1)S(1)}, bf16[32,1152]{1,0:T(8,128)(2,1)S(1)}, u32[]{:S(2)}, u32[]{:S(2)}) collective-permute-start(bf16[32,1152]{1,0:T(8,128)(2,1)S(1)} %shard_map.101), channel_id=1, source_target_pairs={{0,24},{4,28},{8,16},{12,20},{16,8},{20,12},{24,0},{28,4},{1,25},{... | collective-permute-start | bytes 221192 | tf_op jit(solution)/shard_map/ppermute | solution.py:23
  54.6 0.0 collective-permute-done.16.refs_1_
  54.6 0.3 collective-permute-start.17
  54.9 0.0 collective-permute-done.18.refs_1_
  54.9 1.8 %collective-permute-start.19 = (bf16[32,1152]{1,0:T(8,128)(2,1)S(1)}, bf16[32,1152]{1,0:T(8,128)(2,1)S(1)}, u32[]{:S(2)}, u32[]{:S(2)}) collective-permute-start(bf16[32,1152]{1,0:T(8,128)(2,1)S(1)} %shard_map.103), channel_id=1, source_target_pairs={{0,8},{4,12},{8,0},{12,4},{16,24},{20,28},{24,16},{28,20},{1,9},{5... | collective-permute-start | bytes 221192 | tf_op jit(solution)/shard_map/ppermute | solution.py:23
  56.7 0.0 collective-permute-done.13.refs_1_
  56.7 1.4 %collective-permute-done.15.refs_2_ = bf16[32,1152]{1,0:T(8,128)(2,1)S(1)} collective-permute-done((bf16[32,1152]{1,0:T(8,128)(2,1)S(1)}, bf16[32,1152]{1,0:T(8,128)(2,1)S(1)}, u32[]{:S(2)}, u32[]{:S(2)}) %collective-permute-start.15) | collective-permute-done | bytes 73760 | tf_op jit(solution)/shard_map/ppermute | solution.py:23
  58.1 1.9 %collective-permute-done.17.refs_3_ = bf16[32,1152]{1,0:T(8,128)(2,1)S(1)} collective-permute-done((bf16[32,1152]{1,0:T(8,128)(2,1)S(1)}, bf16[32,1152]{1,0:T(8,128)(2,1)S(1)}, u32[]{:S(2)}, u32[]{:S(2)}) %collective-permute-start.17) | collective-permute-done | bytes 73760 | tf_op jit(solution)/shard_map/ppermute | solution.py:23
  60.0 0.1 collective-permute-done.19.refs_4_
  60.1 0.1 shard_map.104.refs_0_
  60.2 1.6 %collective-permute-start.21 = (bf16[32,1152]{1,0:T(8,128)(2,1)S(1)}, bf16[32,1152]{1,0:T(8,128)(2,1)S(1)}, u32[]{:S(2)}, u32[]{:S(2)}) collective-permute-start(bf16[32,1152]{1,0:T(8,128)(2,1)S(1)} %shard_map.104.refs_0_), channel_id=1, source_target_pairs={{0,2},{1,3},{2,0},{3,1},{4,6},{5,7},{6,4},{7,5},{8,10},{9,11},{10,... | collective-permute-start | bytes 221192 | tf_op jit(solution)/shard_map/ppermute | solution.py:23
  61.7 0.0 collective-permute-start.20
  61.8 2.8 %collective-permute-done.21.refs_2_ = bf16[32,1152]{1,0:T(8,128)(2,1)S(1)} collective-permute-done((bf16[32,1152]{1,0:T(8,128)(2,1)S(1)}, bf16[32,1152]{1,0:T(8,128)(2,1)S(1)}, u32[]{:S(2)}, u32[]{:S(2)}) %collective-permute-start.21) | collective-permute-done | bytes 73760 | tf_op jit(solution)/shard_map/ppermute | solution.py:23
  64.6 0.0 collective-permute-start.22
  64.6 0.0 collective-permute-done.20.refs_1_
  64.6 1.3 %collective-permute-done.22.refs_3_ = bf16[32,1152]{1,0:T(8,128)(2,1)S(1)} collective-permute-done((bf16[32,1152]{1,0:T(8,128)(2,1)S(1)}, bf16[32,1152]{1,0:T(8,128)(2,1)S(1)}, u32[]{:S(2)}, u32[]{:S(2)}) %collective-permute-start.22) | collective-permute-done | bytes 73760 | tf_op jit(solution)/shard_map/ppermute | solution.py:23
  65.9 1.5 %shard_map.105 = bf16[128,4608]{1,0:T(8,128)(2,1)} custom-call(s32[1]{0:T(128)S(6)} %copy.10.counts, s32[1]{0:T(128)} %bitcast.tp_at, s32[1,32]{1,0:T(1,128)S(1)} %copy-done.2, bf16[128,4608]{1,0:T(8,128)(2,1)S(1)} %copy-done, f32[32,128]{1,0:T(8,128)S(1)} %shard_map.92.weight, f32[36,128]{1,0:T(8,128)S(1)} %bitcast.11, ...), custom_call_target="tpu_custom_call" | custom-call | tf_op jit(solution)/shard_map/pallas_call | solution.py:175
  (26 shorter events, 0.1 us)
Async XLA Ops:
  2.8 8.5 %collective-permute-start.5 = (bf16[32,1152]{1,0:T(8,128)(2,1)S(1)}, bf16[32,1152]{1,0:T(8,128)(2,1)S(1)}, u32[]{:S(2)}, u32[]{:S(2)}) collective-permute-start(bf16[32,1152]{1,0:T(8,128)(2,1)S(1)} %get-tuple-element.27.refs_0_), channel_id=1, source_target_pairs={{0,24},{4,28},{8,16},{12,20},{16,8},{20,12},{24,0},{28,4},{1,25},{... | collective-permute-start | bytes 221192 | tf_op jit(solution)/shard_map/ppermute | solution.py:23
  7.9 6.2 %collective-permute-start.3 = (bf16[32,1152]{1,0:T(8,128)(2,1)S(1)}, bf16[32,1152]{1,0:T(8,128)(2,1)S(1)}, u32[]{:S(2)}, u32[]{:S(2)}) collective-permute-start(bf16[32,1152]{1,0:T(8,128)(2,1)S(1)} %get-tuple-element.27.refs_0_), channel_id=1, source_target_pairs={{0,16},{4,20},{8,24},{12,28},{16,0},{20,4},{24,8},{28,12},{1,17},{... | collective-permute-start | bytes 221192 | tf_op jit(solution)/shard_map/ppermute | solution.py:23
  7.9 7.7 %collective-permute-start.1 = (bf16[32,1152]{1,0:T(8,128)(2,1)S(1)}, bf16[32,1152]{1,0:T(8,128)(2,1)S(1)}, u32[]{:S(2)}, u32[]{:S(2)}) collective-permute-start(bf16[32,1152]{1,0:T(8,128)(2,1)S(1)} %get-tuple-element.27.refs_0_), channel_id=1, source_target_pairs={{0,8},{4,12},{8,0},{12,4},{16,24},{20,28},{24,16},{28,20},{1,9},{5... | collective-permute-start | bytes 221192 | tf_op jit(solution)/shard_map/ppermute | solution.py:23
  8.6 13.6 %slice-start.3 = ((s8[10616832]{0:T(1024)(128)(4,1)}), s8[4194304]{0:T(1024)(128)(4,1)S(1)}, s32[]{:S(2)}) async-start(s8[10616832]{0:T(1024)(128)(4,1)} %bitcast.7), calls=%async_computation.3 | async-start | bytes 8388608
  8.6 13.6 %slice-start.6 = ((s8[10616832]{0:T(1024)(128)(4,1)}), s8[4194304]{0:T(1024)(128)(4,1)S(1)}, s32[]{:S(2)}) async-start(s8[10616832]{0:T(1024)(128)(4,1)} %bitcast.9), calls=%async_computation.6 | async-start | bytes 8388608
  8.6 0.9 %copy-start.3 = (f32[4608]{0:T(1024)S(1)}, f32[4608]{0:T(1024)}, u32[]{:S(2)}) copy-start(f32[4608]{0:T(1024)} %param.12) | copy-start | bytes 55300
  9.4 12.7 %slice-start.4 = ((s8[10616832]{0:T(1024)(128)(4,1)}), s8[4194304]{0:T(1024)(128)(4,1)S(1)}, s32[]{:S(2)}) async-start(s8[10616832]{0:T(1024)(128)(4,1)} %bitcast.7), calls=%async_computation.4 | async-start | bytes 8388608
  9.4 12.8 %slice-start.5 = ((s8[10616832]{0:T(1024)(128)(4,1)}), s8[2228224]{0:T(1024)(128)(4,1)S(1)}, s32[]{:S(2)}) async-start(s8[10616832]{0:T(1024)(128)(4,1)} %bitcast.7), calls=%async_computation.5 | async-start | bytes 4456448
  9.4 12.8 %slice-start.7 = ((s8[10616832]{0:T(1024)(128)(4,1)}), s8[4194304]{0:T(1024)(128)(4,1)S(1)}, s32[]{:S(2)}) async-start(s8[10616832]{0:T(1024)(128)(4,1)} %bitcast.9), calls=%async_computation.7 | async-start | bytes 8388608
  9.4 12.8 %slice-start.8 = ((s8[10616832]{0:T(1024)(128)(4,1)}), s8[2228224]{0:T(1024)(128)(4,1)S(1)}, s32[]{:S(2)}) async-start(s8[10616832]{0:T(1024)(128)(4,1)} %bitcast.9), calls=%async_computation.8 | async-start | bytes 4456448
  9.6 6.6 %collective-permute-start = (bf16[32,1152]{1,0:T(8,128)(2,1)S(1)}, bf16[32,1152]{1,0:T(8,128)(2,1)S(1)}, u32[]{:S(2)}, u32[]{:S(2)}) collective-permute-start(bf16[32,1152]{1,0:T(8,128)(2,1)S(1)} %get-tuple-element.27.refs_0_), channel_id=1, source_target_pairs={{0,4},{4,0},{8,12},{12,8},{16,20},{20,16},{24,28},{28,24},{1,5},{5... | collective-permute-start | bytes 221192 | tf_op jit(solution)/shard_map/ppermute | solution.py:23
  11.3 4.9 %collective-permute-start.6 = (bf16[32,1152]{1,0:T(8,128)(2,1)S(1)}, bf16[32,1152]{1,0:T(8,128)(2,1)S(1)}, u32[]{:S(2)}, u32[]{:S(2)}) collective-permute-start(bf16[32,1152]{1,0:T(8,128)(2,1)S(1)} %collective-permute-done.5.refs_6_), channel_id=1, source_target_pairs={{0,4},{4,0},{8,12},{12,8},{16,20},{20,16},{24,28},{28,24},{1,5},{5... | collective-permute-start | bytes 221192 | tf_op jit(solution)/shard_map/ppermute | solution.py:23
  14.1 5.0 %collective-permute-start.4 = (bf16[32,1152]{1,0:T(8,128)(2,1)S(1)}, bf16[32,1152]{1,0:T(8,128)(2,1)S(1)}, u32[]{:S(2)}, u32[]{:S(2)}) collective-permute-start(bf16[32,1152]{1,0:T(8,128)(2,1)S(1)} %collective-permute-done.3.refs_4_), channel_id=1, source_target_pairs={{0,4},{4,0},{8,12},{12,8},{16,20},{20,16},{24,28},{28,24},{1,5},{5... | collective-permute-start | bytes 221192 | tf_op jit(solution)/shard_map/ppermute | solution.py:23
  15.6 4.4 %collective-permute-start.2 = (bf16[32,1152]{1,0:T(8,128)(2,1)S(1)}, bf16[32,1152]{1,0:T(8,128)(2,1)S(1)}, u32[]{:S(2)}, u32[]{:S(2)}) collective-permute-start(bf16[32,1152]{1,0:T(8,128)(2,1)S(1)} %collective-permute-done.1.refs_2_), channel_id=1, source_target_pairs={{0,4},{4,0},{8,12},{12,8},{16,20},{20,16},{24,28},{28,24},{1,5},{5... | collective-permute-start | bytes 221192 | tf_op jit(solution)/shard_map/ppermute | solution.py:23
  20.5 1.7 %collective-permute-start.8 = (bf16[128,1152]{1,0:T(8,128)(2,1)S(1)}, bf16[128,1152]{1,0:T(8,128)(2,1)S(1)}, u32[]{:S(2)}, u32[]{:S(2)}) collective-permute-start(bf16[128,1152]{1,0:T(8,128)(2,1)S(1)} %get-tuple-element.28.first), channel_id=1, source_target_pairs={{0,1},{1,0},{2,3},{3,2},{4,5},{5,4},{6,7},{7,6},{8,9},{9,8},{10,11... | collective-permute-start | bytes 884744 | tf_op jit(solution)/shard_map/ppermute | solution.py:23
  20.6 9.4 %collective-permute-start.7 = (bf16[128,1152]{1,0:T(8,128)(2,1)S(1)}, bf16[128,1152]{1,0:T(8,128)(2,1)S(1)}, u32[]{:S(2)}, u32[]{:S(2)}) collective-permute-start(bf16[128,1152]{1,0:T(8,128)(2,1)S(1)} %get-tuple-element.28.first), channel_id=1, source_target_pairs={{0,2},{1,3},{2,0},{3,1},{4,6},{5,7},{6,4},{7,5},{8,10},{9,11},{10,... | collective-permute-start | bytes 884744 | tf_op jit(solution)/shard_map/ppermute | solution.py:23
  30.0 3.5 %slice-start = ((s8[10616832]{0:T(1024)(128)(4,1)}), s8[4194304]{0:T(1024)(128)(4,1)S(1)}, s32[]{:S(2)}) async-start(s8[10616832]{0:T(1024)(128)(4,1)} %bitcast.5), calls=%async_computation | async-start | bytes 8388608
  30.0 3.6 %slice-start.1 = ((s8[10616832]{0:T(1024)(128)(4,1)}), s8[4194304]{0:T(1024)(128)(4,1)S(1)}, s32[]{:S(2)}) async-start(s8[10616832]{0:T(1024)(128)(4,1)} %bitcast.5), calls=%async_computation.1 | async-start | bytes 8388608
  30.0 4.1 %slice-start.2 = ((s8[10616832]{0:T(1024)(128)(4,1)}), s8[2228224]{0:T(1024)(128)(4,1)S(1)}, s32[]{:S(2)}) async-start(s8[10616832]{0:T(1024)(128)(4,1)} %bitcast.5), calls=%async_computation.2 | async-start | bytes 4456448
  30.0 1.6 %collective-permute-start.9 = (bf16[128,1152]{1,0:T(8,128)(2,1)S(1)}, bf16[128,1152]{1,0:T(8,128)(2,1)S(1)}, u32[]{:S(2)}, u32[]{:S(2)}) collective-permute-start(bf16[128,1152]{1,0:T(8,128)(2,1)S(1)} %collective-permute-done.7.third), channel_id=1, source_target_pairs={{0,1},{1,0},{2,3},{3,2},{4,5},{5,4},{6,7},{7,6},{8,9},{9,8},{10,11... | collective-permute-start | bytes 884744 | tf_op jit(solution)/shard_map/ppermute | solution.py:23
  34.7 1.6 %collective-permute-start.11 = (bf16[128,1152]{1,0:T(8,128)(2,1)S(1)}, bf16[128,1152]{1,0:T(8,128)(2,1)S(1)}, u32[]{:S(2)}, u32[]{:S(2)}) collective-permute-start(bf16[128,1152]{1,0:T(8,128)(2,1)S(1)} %shard_map.98), channel_id=1, source_target_pairs={{0,1},{1,0},{2,3},{3,2},{4,5},{5,4},{6,7},{7,6},{8,9},{9,8},{10,11... | collective-permute-start | bytes 884744 | tf_op jit(solution)/shard_map/ppermute | solution.py:23
  35.4 30.4 %copy-start = (bf16[128,4608]{1,0:T(8,128)(2,1)S(1)}, bf16[128,4608]{1,0:T(8,128)(2,1)}, u32[]{:S(2)}) copy-start(bf16[128,4608]{1,0:T(8,128)(2,1)} %tokens.3) | copy-start | bytes 3538948
  35.4 30.4 %copy-start.1 = (f32[4608]{0:T(1024)S(1)}, f32[4608]{0:T(1024)}, u32[]{:S(2)}) copy-start(f32[4608]{0:T(1024)} %param.14) | copy-start | bytes 55300
  35.4 30.4 %copy-start.2 = (s32[1,32]{1,0:T(1,128)S(1)}, s32[1,32]{1,0:T(1,128)}, u32[]{:S(2)}) copy-start(s32[1,32]{1,0:T(1,128)} %chosen.3) | copy-start | bytes 388
  35.4 3.1 %collective-permute-start.10 = (bf16[128,1152]{1,0:T(8,128)(2,1)S(1)}, bf16[128,1152]{1,0:T(8,128)(2,1)S(1)}, u32[]{:S(2)}, u32[]{:S(2)}) collective-permute-start(bf16[128,1152]{1,0:T(8,128)(2,1)S(1)} %shard_map.96), channel_id=1, source_target_pairs={{0,1},{1,0},{2,3},{3,2},{4,5},{5,4},{6,7},{7,6},{8,9},{9,8},{10,11... | collective-permute-start | bytes 884744 | tf_op jit(solution)/shard_map/ppermute | solution.py:23
  37.0 9.1 %collective-permute-start.12 = (bf16[128,1152]{1,0:T(8,128)(2,1)S(1)}, bf16[128,1152]{1,0:T(8,128)(2,1)S(1)}, u32[]{:S(2)}, u32[]{:S(2)}) collective-permute-start(bf16[128,1152]{1,0:T(8,128)(2,1)S(1)} %shard_map.99), channel_id=1, source_target_pairs={{0,2},{1,3},{2,0},{3,1},{4,6},{5,7},{6,4},{7,5},{8,10},{9,11},{10,... | collective-permute-start | bytes 884744 | tf_op jit(solution)/shard_map/ppermute | solution.py:23
  46.6 5.2 %collective-permute-start.14 = (bf16[32,1152]{1,0:T(8,128)(2,1)S(1)}, bf16[32,1152]{1,0:T(8,128)(2,1)S(1)}, u32[]{:S(2)}, u32[]{:S(2)}) collective-permute-start(bf16[32,1152]{1,0:T(8,128)(2,1)S(1)} %get-tuple-element.38), channel_id=1, source_target_pairs={{0,4},{4,0},{8,12},{12,8},{16,20},{20,16},{24,28},{28,24},{1,5},{5... | collective-permute-start | bytes 221192 | tf_op jit(solution)/shard_map/ppermute | solution.py:23
  47.6 6.9 %collective-permute-start.16 = (bf16[32,1152]{1,0:T(8,128)(2,1)S(1)}, bf16[32,1152]{1,0:T(8,128)(2,1)S(1)}, u32[]{:S(2)}, u32[]{:S(2)}) collective-permute-start(bf16[32,1152]{1,0:T(8,128)(2,1)S(1)} %get-tuple-element.40), channel_id=1, source_target_pairs={{0,4},{4,0},{8,12},{12,8},{16,20},{20,16},{24,28},{28,24},{1,5},{5... | collective-permute-start | bytes 221192 | tf_op jit(solution)/shard_map/ppermute | solution.py:23
  48.6 6.2 %collective-permute-start.18 = (bf16[32,1152]{1,0:T(8,128)(2,1)S(1)}, bf16[32,1152]{1,0:T(8,128)(2,1)S(1)}, u32[]{:S(2)}, u32[]{:S(2)}) collective-permute-start(bf16[32,1152]{1,0:T(8,128)(2,1)S(1)} %get-tuple-element.42), channel_id=1, source_target_pairs={{0,4},{4,0},{8,12},{12,8},{16,20},{20,16},{24,28},{28,24},{1,5},{5... | collective-permute-start | bytes 221192 | tf_op jit(solution)/shard_map/ppermute | solution.py:23
  49.7 7.0 %collective-permute-start.13 = (bf16[32,1152]{1,0:T(8,128)(2,1)S(1)}, bf16[32,1152]{1,0:T(8,128)(2,1)S(1)}, u32[]{:S(2)}, u32[]{:S(2)}) collective-permute-start(bf16[32,1152]{1,0:T(8,128)(2,1)S(1)} %get-tuple-element.36), channel_id=1, source_target_pairs={{0,4},{4,0},{8,12},{12,8},{16,20},{20,16},{24,28},{28,24},{1,5},{5... | collective-permute-start | bytes 221192 | tf_op jit(solution)/shard_map/ppermute | solution.py:23
  51.8 6.3 %collective-permute-start.15 = (bf16[32,1152]{1,0:T(8,128)(2,1)S(1)}, bf16[32,1152]{1,0:T(8,128)(2,1)S(1)}, u32[]{:S(2)}, u32[]{:S(2)}) collective-permute-start(bf16[32,1152]{1,0:T(8,128)(2,1)S(1)} %shard_map.101), channel_id=1, source_target_pairs={{0,24},{4,28},{8,16},{12,20},{16,8},{20,12},{24,0},{28,4},{1,25},{... | collective-permute-start | bytes 221192 | tf_op jit(solution)/shard_map/ppermute | solution.py:23
  54.6 5.4 %collective-permute-start.17 = (bf16[32,1152]{1,0:T(8,128)(2,1)S(1)}, bf16[32,1152]{1,0:T(8,128)(2,1)S(1)}, u32[]{:S(2)}, u32[]{:S(2)}) collective-permute-start(bf16[32,1152]{1,0:T(8,128)(2,1)S(1)} %shard_map.102), channel_id=1, source_target_pairs={{0,16},{4,20},{8,24},{12,28},{16,0},{20,4},{24,8},{28,12},{1,17},{... | collective-permute-start | bytes 221192 | tf_op jit(solution)/shard_map/ppermute | solution.py:23
  54.9 5.2 %collective-permute-start.19 = (bf16[32,1152]{1,0:T(8,128)(2,1)S(1)}, bf16[32,1152]{1,0:T(8,128)(2,1)S(1)}, u32[]{:S(2)}, u32[]{:S(2)}) collective-permute-start(bf16[32,1152]{1,0:T(8,128)(2,1)S(1)} %shard_map.103), channel_id=1, source_target_pairs={{0,8},{4,12},{8,0},{12,4},{16,24},{20,28},{24,16},{28,20},{1,9},{5... | collective-permute-start | bytes 221192 | tf_op jit(solution)/shard_map/ppermute | solution.py:23
  60.2 4.4 %collective-permute-start.21 = (bf16[32,1152]{1,0:T(8,128)(2,1)S(1)}, bf16[32,1152]{1,0:T(8,128)(2,1)S(1)}, u32[]{:S(2)}, u32[]{:S(2)}) collective-permute-start(bf16[32,1152]{1,0:T(8,128)(2,1)S(1)} %shard_map.104.refs_0_), channel_id=1, source_target_pairs={{0,2},{1,3},{2,0},{3,1},{4,6},{5,7},{6,4},{7,5},{8,10},{9,11},{10,... | collective-permute-start | bytes 221192 | tf_op jit(solution)/shard_map/ppermute | solution.py:23
  61.7 2.8 %collective-permute-start.20 = (bf16[32,1152]{1,0:T(8,128)(2,1)S(1)}, bf16[32,1152]{1,0:T(8,128)(2,1)S(1)}, u32[]{:S(2)}, u32[]{:S(2)}) collective-permute-start(bf16[32,1152]{1,0:T(8,128)(2,1)S(1)} %shard_map.104.refs_0_), channel_id=1, source_target_pairs={{0,1},{1,0},{2,3},{3,2},{4,5},{5,4},{6,7},{7,6},{8,9},{9,8},{10,11... | collective-permute-start | bytes 221192 | tf_op jit(solution)/shard_map/ppermute | solution.py:23
  64.6 1.3 %collective-permute-start.22 = (bf16[32,1152]{1,0:T(8,128)(2,1)S(1)}, bf16[32,1152]{1,0:T(8,128)(2,1)S(1)}, u32[]{:S(2)}, u32[]{:S(2)}) collective-permute-start(bf16[32,1152]{1,0:T(8,128)(2,1)S(1)} %collective-permute-done.21.refs_2_), channel_id=1, source_target_pairs={{0,1},{1,0},{2,3},{3,2},{4,5},{5,4},{6,7},{7,6},{8,9},{9,8},{10,11... | collective-permute-start | bytes 221192 | tf_op jit(solution)/shard_map/ppermute | solution.py:23

commit v2 on v1

v2 whole, which is shorter than its diff:
```python
from functools import partial

import jax
import jax.numpy as jnp
from jax import lax
from jax.experimental import pallas as pl
from jax.experimental.pallas import tpu as pltpu
from jax.sharding import PartitionSpec as P

EPS = 1e-06
DEAD = 16384.0
LANES = 128
BF16 = jnp.bfloat16
F32 = jnp.float32
VMEM = pl.BlockSpec(memory_space=pltpu.VMEM)
SMEM = pl.BlockSpec(memory_space=pltpu.SMEM)
HBM = pl.BlockSpec(memory_space=pltpu.HBM)
CHUNKS = 4
TP = 4


def swap(value, axis, bits):
    size = lax.axis_size(axis)
    return lax.ppermute(value, axis, [(i, i ^ bits) for i in range(size)])


def iota(shape, dim):
    return lax.broadcasted_iota(jnp.int32, shape, dim)


def dot_f32(left, right):
    return jnp.dot(left, right, preferred_element_type=F32)


def dot_rows(left, right):
    return lax.dot_general(left, right, (((0,), (0,)), ((), ())), preferred_element_type=F32)


def picker(chosen, count, tok_rows):
    shape = (tok_rows, chosen.shape[1])
    hit = (iota(shape, 0) == chosen) & (iota(shape, 1) < count)
    return jnp.where(hit, 1.0, 0.0).astype(BF16)


def chunks(width):
    step = width // CHUNKS
    return [(part, slice(part * step, (part + 1) * step)) for part in range(CHUNKS)]


def scaled(values, gain):
    parts = [values[:, i * LANES : (i + 1) * LANES] * gain[i : i + 1, :] for i in range(gain.shape[0])]
    return jnp.concatenate(parts, 1)


def prepare_kernel(
    counts, tp_at, seq_at, chosen, tokens, gain, router_w,
    own, rows, picked, router_v, chosen_v, tokens_v, gain_v, done, sems,
):
    del seq_at
    capacity, piece = own.shape
    width = tokens.shape[1]
    copies = [
        pltpu.make_async_copy(tokens.at[:, at], tokens_v.at[:, at], sems.at[part]) for part, at in chunks(width)
    ]
    small = [
        pltpu.make_async_copy(source, target, done.at[at])
        for at, (source, target) in enumerate(
            ((chosen, chosen_v), (gain, gain_v), (router_w, router_v))
        )
    ]
    for copy in small[:1] + copies + small[1:]:
        copy.start()
    small[0].wait()
    count = counts[0]
    picked[...] = picker(chosen_v[...], count, tokens.shape[0])
    hot = picked[...]
    square = jnp.zeros((capacity, 1), F32)
    for part, at in chunks(width):
        copies[part].wait()
        values = dot_rows(hot, tokens_v[:, at])
        rows[:, at] = values.astype(BF16)
        square = square + jnp.sum(values * values, axis=1, keepdims=True)
    small[1].wait()
    scale = lax.rsqrt(square / width + EPS)
    live = iota((capacity, 1), 0) < count
    for i in range(piece // LANES):
        at = pl.multiple_of(tp_at[0] * piece + i * LANES, LANES)
        part = rows[:, pl.ds(at, LANES)].astype(F32) * scale
        part = part * gain_v[pl.ds(tp_at[0] * (piece // LANES) + i, 1), :]
        own[:, i * LANES : (i + 1) * LANES] = jnp.where(live, part, DEAD).astype(BF16)
    small[2].wait()


def weight_kernel(rows, router_w, weight):
    logit = jnp.sum(scaled(rows[...].astype(F32), router_w[...]), axis=1, keepdims=True)
    weight[...] = jnp.broadcast_to(jax.nn.sigmoid(logit), weight.shape)


def pack_kernel(seq_at, *refs):
    pieces, (packed, places, *halves) = refs[:-4], refs[-4:]
    capacity = pieces[0].shape[0]
    held = jnp.concatenate([ref[...] for ref in pieces], 0)
    count = held.shape[0]
    live = held[:, :LANES].astype(F32) < DEAD / 2
    live_bf16 = jnp.where(live, 1.0, 0.0).astype(BF16)
    block = min(count, 2 * LANES)
    firsts = []
    for top in range(0, count, block):
        shard = seq_at[0] ^ ((iota((block, count), 0) + top) // capacity)
        before = (seq_at[0] ^ (iota((block, count), 1) // capacity)) < shard
        firsts.append(dot_f32(jnp.where(before, 1.0, 0.0).astype(BF16), live_bf16).astype(jnp.int32))
    first = jnp.concatenate(firsts, 0)
    target = first + (iota((count, LANES), 0) % capacity)
    for part in range(places.shape[1] // LANES):
        hit = (target == iota((count, LANES), 1) + part * LANES) & live
        places[:, part * LANES : (part + 1) * LANES] = jnp.where(hit, 1.0, 0.0).astype(BF16)
    packed[...] = dot_rows(places[...], held).astype(BF16)
    cut = halves[0].shape[1]
    halves[0][...] = packed[:, :cut]
    halves[1][...] = packed[:, cut:]


def gated(tp_at, far, rows, weights, at=0):
    deep = weights.shape[0] // TP
    start = pl.multiple_of((tp_at[0] ^ far) * deep + at, LANES)
    return dot_f32(rows[...], weights[pl.ds(start, rows.shape[1]), :])


def start_kernel(tp_at, first, second, gate_w, up_w, down_w, gate_out, up_out):
    del down_w
    for weights, result in ((gate_w, gate_out), (up_w, up_out)):
        result[...] = gated(tp_at, 0, first, weights) + gated(tp_at, 1, second, weights)


def middle_kernel(places, tp_at, *refs):
    rows, (gate_in, up_in, gate_w, up_w, gate_out, up_out) = refs[:-6], refs[-6:]
    for weights, before, result in ((gate_w, gate_in, gate_out), (up_w, up_in, up_out)):
        total = before[...]
        for (far, at), part in zip(places, rows):
            total = total + gated(tp_at, far, part, weights, at)
        result[...] = total


def finish_kernel(place, tp_at, rows, gate_in, up_in, gate_w, up_w, hidden):
    far, at = place
    gate = gate_in[...] + gated(tp_at, far, rows, gate_w, at)
    up = up_in[...] + gated(tp_at, far, rows, up_w, at)
    hidden[...] = (jax.nn.gelu(gate, approximate=True) * up).astype(BF16)


def down_kernel(far, offset, tp_at, hidden, down_w, *refs):
    result = refs[-1]
    wide = result.shape[1]
    at = pl.multiple_of((tp_at[0] ^ far) * (down_w.shape[1] // TP) + offset, LANES)
    total = dot_f32(hidden[...], down_w[:, pl.ds(at, wide)])
    for ref in refs[:-1]:
        total = total + ref[...].astype(F32)
    result[...] = total.astype(result.dtype)


def window_kernel(near, first, second, places, *windows):
    total = near[...] + jnp.concatenate([first[...], second[...]], 1).astype(F32)
    total = total.astype(BF16)
    first = 0
    for window in windows:
        count = window.shape[0]
        window[...] = dot_f32(places[first : first + count, :], total).astype(BF16)
        first += count


def add_up(values, refs):
    total = values.astype(F32)
    for ref in refs:
        total = total + ref[...].astype(F32)
    return total.astype(BF16)


def sum_kernel(first, *refs):
    refs[-1][...] = add_up(first[...], refs[:-1])


def late_kernel(pair, *refs):
    refs[-1][...] = add_up(pair[refs[-1].shape[0] :, :], refs[:-1])


def last_kernel(pair, *refs):
    refs[-1][...] = add_up(pair[: refs[-1].shape[0], :], refs[:-1])


def finish_rows_kernel(tp_at, picked, tokens, weight, gain, *refs):
    parts, (out, joined, staged, sems) = refs[:-4], refs[-4:]
    width = tokens.shape[1]
    piece = width // len(parts)
    for far, part in enumerate(parts):
        joined[:, pl.ds(pl.multiple_of((tp_at[0] ^ far) * piece, LANES), piece)] = part[...].astype(F32)
    values = joined[...]
    scale = lax.rsqrt(jnp.mean(values * values, axis=1, keepdims=True) + EPS) * weight[:, :1]
    hot = picked[...]
    rows = gain.shape[0] // CHUNKS
    copies = []
    for part, at in chunks(width):
        update = scaled(values[:, at] * scale, gain[part * rows : (part + 1) * rows, :]).astype(BF16)
        staged[:, at] = (tokens[:, at].astype(F32) + dot_f32(hot, update)).astype(BF16)
        copies.append(pltpu.make_async_copy(staged.at[:, at], out.at[:, at], sems.at[part]))
        copies[-1].start()
    for copy in copies:
        copy.wait()


def call(kernel, shapes, scalars, operands, flops=0, scratch=(), spec=None, out_spec=None):
    return pl.pallas_call(
        kernel,
        out_shape=shapes,
        in_specs=[SMEM] * len(scalars) + [spec or VMEM] * len(operands),
        out_specs=jax.tree.map(lambda _: out_spec or VMEM, shapes),
        scratch_shapes=scratch,
        compiler_params=pltpu.CompilerParams(vmem_limit_bytes=min(32, lax.axis_size("seq")) << 20),
        cost_estimate=pl.CostEstimate(flops=flops, bytes_accessed=0, transcendentals=0),
    )(*scalars, *operands)


def array(rows, columns, kind=BF16):
    return jax.ShapeDtypeStruct((rows, columns), kind)


def layer(tokens, counts, selected, router_w, pre_gain, post_gain, gate_w, up_w, down_w):
    tok_rows, width = tokens.shape
    capacity = selected.shape[1]
    shards = lax.axis_size("seq")
    pair_count = lax.axis_size("tp")
    units = gate_w.shape[1]
    total = shards * capacity // 2
    piece = width // pair_count
    seq_at = lax.axis_index("seq").astype(jnp.int32).reshape(1)
    tp_at = lax.axis_index("tp").astype(jnp.int32).reshape(1)

    own, rows, picked, router_v = call(
        prepare_kernel,
        (
            array(capacity, piece),
            array(capacity, width),
            array(tok_rows, capacity),
            array(width // LANES, LANES, F32),
        ),
        (counts, tp_at, seq_at),
        [
            pltpu.with_memory_space_constraint(value, pltpu.HBM)
            for value in (
                selected, tokens, pre_gain.reshape(-1, LANES), router_w.reshape(-1, LANES)
            )
        ],
        scratch=(
            pltpu.VMEM(selected.shape, jnp.int32),
            pltpu.VMEM(tokens.shape, BF16),
            pltpu.VMEM((width // LANES, LANES), F32),
            pltpu.SemaphoreType.DMA((3,)),
            pltpu.SemaphoreType.DMA((CHUNKS,)),
        ),
        spec=HBM,
    )
    weight = call(
        weight_kernel,
        array(capacity, LANES, F32),
        (),
        (rows, router_v),
        flops=64 * total * width * units,
    )

    held = {0: own}
    for far in range(2, shards, 2):
        held[far] = swap(own, "seq", far)
    held[1] = swap(own, "seq", 1)
    held[shards - 2], weight = lax.optimization_barrier((held[shards - 2], weight))
    held[3] = swap(held[1], "seq", 2)
    for far in range(4, shards, 2):
        held[far + 1] = swap(held[far], "seq", 1)
    assert pair_count == TP
    cut = (piece // LANES + 1) // 2 * LANES
    cuts = (0, cut), (cut, piece - cut)
    packed, places, *halves = call(
        pack_kernel,
        (array(total, piece), array(shards * capacity, total), *[array(total, wide) for _, wide in cuts]),
        (seq_at,),
        [held[far] for far in range(shards)],
        flops=16 * total * piece * units,
    )

    flops = 2 * total * piece * units
    part = (array(total, units, F32), array(total, units, F32))
    third = [swap(rows, "tp", 2) for rows in halves]
    second = swap(packed, "tp", 1)
    sums = call(start_kernel, part, (tp_at,), (packed, second, gate_w, up_w, down_w), 4 * flops)
    third[0], sums = lax.optimization_barrier((third[0], sums))
    fourth = [swap(third[0], "tp", 1)]
    sums = call(partial(middle_kernel, ((2, 0),)), part, (tp_at,), (third[0], *sums, gate_w, up_w), flops)
    third[1], sums = lax.optimization_barrier((third[1], sums))
    fourth.append(swap(third[1], "tp", 1))
    sums = call(
        partial(middle_kernel, ((3, 0), (2, cut))), part, (tp_at,), (fourth[0], third[1], *sums, gate_w, up_w), flops
    )
    fourth[1], sums = lax.optimization_barrier((fourth[1], sums))
    hidden = call(
        partial(finish_kernel, (3, cut)), array(total, units), (tp_at,), (fourth[1], *sums, gate_w, up_w), flops
    )

    def down(far, kind, at, wide, *extra):
        kernel = partial(down_kernel, far, at)
        return call(kernel, array(total, wide, kind), (tp_at,), (hidden, down_w, *extra), flops // 2)

    far_sums = []
    for at, wide in cuts:
        away = swap(down(3, BF16, at, wide), "tp", 1)
        mine = down(2, F32, at, wide)
        away, mine = lax.optimization_barrier((away, mine))
        far_sum = call(sum_kernel, array(total, wide), (), (mine, away))
        far_sums.append(swap(far_sum, "tp", 2))
    near_away = swap(down(1, BF16, 0, piece), "tp", 1)
    near_sum = down(0, F32, 0, piece, near_away)
    one = array(capacity, piece)
    shapes = [one, one, array(2 * capacity, piece)] + [one] * (shards - 4)
    windows = call(window_kernel, shapes, (), (near_sum, *far_sums, places))
    ready = []
    for far in range(shards - 2, 2, -2):
        other = swap(windows[far], "seq", 1)
        pair = call(sum_kernel, one, (), (windows[far - 1], other))
        ready.append(swap(pair, "seq", far))
    pair = swap(windows[2], "seq", 2)
    other = swap(call(late_kernel, one, (), (pair, windows[1])), "seq", 1)
    final = call(last_kernel, one, (), (pair, windows[0], other, *ready))
    other_far = swap(final, "tp", 2)
    other_near = swap(final, "tp", 1)
    last = swap(other_far, "tp", 1)
    return call(
        finish_rows_kernel,
        array(tok_rows, width),
        (tp_at,),
        (picked, tokens, weight, post_gain.reshape(-1, LANES), final, other_near, other_far, last),
        scratch=(
            pltpu.VMEM((capacity, width), F32),
            pltpu.VMEM(tokens.shape, BF16),
            pltpu.SemaphoreType.DMA((CHUNKS,)),
        ),
        out_spec=HBM,
    )


def solution(mesh):
    in_specs = (
        P("seq", None),
        P("seq"),
        P("seq", None),
        P(),
        P(),
        P(),
        P(None, ("seq", "tp")),
        P(None, ("seq", "tp")),
        P(("seq", "tp"), None),
    )
    return jax.shard_map(layer, mesh=mesh, in_specs=in_specs, out_specs=P("seq", None), check_vma=False)
```

time: 67.5 us -> 65 us (0.963)
  waiting for transfers between devices: 28.8 us -> 25.6 us
  local copies, waits for them, and re-layouts: 1.46 us -> 0.05 us
  starting transfers between devices: 25.1 us -> 26.5 us
  Pallas kernels: 11.1 us -> 11.9 us
    ppermute x23 -> x26, waiting for transfers between devices: 28.8 us -> 25.6 us  [swap(): return lax.ppermute(value, axis, [(i, i ^ bits) for i in range(size)])]
    unnamed x26 -> x22, local copies, waits for them, and re-layouts: 1.46 us -> 0.05 us
    ppermute x23 -> x26, starting transfers between devices: 25.1 us -> 26.5 us  [swap(): return lax.ppermute(value, axis, [(i, i ^ bits) for i in range(size)])]
    pallas_call x15 -> x21, Pallas kernels: 11.1 us -> 11.9 us  [call(): pl.pallas_call(kernel, out_shape=shapes, in_specs=[SMEM] * len(scalars) +...]
  transfers between devices with their start and end apart: 23 -> 26, of which waited for: 13 -> 13; matrix products, arithmetic and copies ran while one was open for 0% -> 0% of each run, Pallas kernels for 6% -> 9%
where the time goes in v2:
time: 65 us; the launch traced here: 64.9 us
  starting transfers between devices  26.5 us (41%)
  waiting for transfers between devices  25.6 us (39%)
  Pallas kernels  11.9 us (18%)
  between operations  0.95 us (1%)
    ppermute x26, starting transfers between devices, swap(): return lax.ppermute(value, axis, [(i, i ^ bits) for i in range(size)])  26.5 us
    ppermute x26, waiting for transfers between devices, swap(): return lax.ppermute(value, axis, [(i, i ^ bits) for i in range(size)])  25.6 us
    pallas_call x21, Pallas kernels, call(): pl.pallas_call(kernel, out_shape=shapes, in_specs=[SMEM] * len(scalars) +...  11.9 us
  transfers between devices with their start and end apart: 26, of which 13 were waited for; matrix products, arithmetic and copies ran while one was open for 0% of the time, Pallas kernels for 9%

profile of v2, /device:TPU:0, one launch (start us, length us, event | category | flops | bytes accessed | tf_op | source)
XLA Modules:
  0.0 64.9 jit_solution(5009566285459477044)
XLA Ops:
  0.7 2.1 %shard_map.91 = (bf16[32,1152]{1,0:T(8,128)(2,1)S(1)}, bf16[32,4608]{1,0:T(8,128)(2,1)S(1)}, bf16[128,32]{1,0:T(8,128)(2,1)S(1)}, f32[36,128]{1,0:T(8,128)S(1)}) custom-call(s32[1]{0:T(128)S(6)} %copy.10.counts, s32[1]{0:T(128)} %bitcast.tp_at, s32[1]{0:T(128)} %bitcast.1.seq_at, s32[1,32]{1,0:T(1,128)} %chosen.1, bf16[128,4608]{1,0:T(8,128)(2,1)} %tokens.3, ...), custom_call_target="tpu_custom_call" | custom-call | tf_op jit(solution)/shard_map/pallas_call | solution.py:211
  2.8 5.1 %collective-permute-start = (bf16[32,1152]{1,0:T(8,128)(2,1)S(1)}, bf16[32,1152]{1,0:T(8,128)(2,1)S(1)}, u32[]{:S(2)}, u32[]{:S(2)}) collective-permute-start(bf16[32,1152]{1,0:T(8,128)(2,1)S(1)} %get-tuple-element.42.refs_0_), channel_id=1, source_target_pairs={{0,24},{4,28},{8,16},{12,20},{16,8},{20,12},{24,0},{28,4},{1,25},{... | collective-permute-start | bytes 221192 | tf_op jit(solution)/shard_map/ppermute | solution.py:24
  7.9 1.5 %collective-permute-start.1 = (bf16[32,1152]{1,0:T(8,128)(2,1)S(1)}, bf16[32,1152]{1,0:T(8,128)(2,1)S(1)}, u32[]{:S(2)}, u32[]{:S(2)}) collective-permute-start(bf16[32,1152]{1,0:T(8,128)(2,1)S(1)} %get-tuple-element.42.refs_0_), channel_id=1, source_target_pairs={{0,4},{4,0},{8,12},{12,8},{16,20},{20,16},{24,28},{28,24},{1,5},{5... | collective-permute-start | bytes 221192 | tf_op jit(solution)/shard_map/ppermute | solution.py:24
  9.4 0.8 %collective-permute-start.2 = (bf16[32,1152]{1,0:T(8,128)(2,1)S(1)}, bf16[32,1152]{1,0:T(8,128)(2,1)S(1)}, u32[]{:S(2)}, u32[]{:S(2)}) collective-permute-start(bf16[32,1152]{1,0:T(8,128)(2,1)S(1)} %get-tuple-element.42.refs_0_), channel_id=1, source_target_pairs={{0,8},{4,12},{8,0},{12,4},{16,24},{20,28},{24,16},{28,20},{1,9},{5... | collective-permute-start | bytes 221192 | tf_op jit(solution)/shard_map/ppermute | solution.py:24
  10.2 0.0 slice-start.2
  10.2 0.0 slice-start.5
  10.3 0.0 slice-start.7
  10.3 0.1 shard_map.92.weight
  10.4 0.1 collective-permute-done.refs_6_
  10.5 1.7 %collective-permute-start.6 = (bf16[32,1152]{1,0:T(8,128)(2,1)S(1)}, bf16[32,1152]{1,0:T(8,128)(2,1)S(1)}, u32[]{:S(2)}, u32[]{:S(2)}) collective-permute-start(bf16[32,1152]{1,0:T(8,128)(2,1)S(1)} %collective-permute-done.refs_6_), channel_id=1, source_target_pairs={{0,4},{4,0},{8,12},{12,8},{16,20},{20,16},{24,28},{28,24},{1,5},{5... | collective-permute-start | bytes 221192 | tf_op jit(solution)/shard_map/ppermute | solution.py:24
  12.2 0.4 collective-permute-done.1.refs_1_
  12.6 2.5 %collective-permute-start.3 = (bf16[32,1152]{1,0:T(8,128)(2,1)S(1)}, bf16[32,1152]{1,0:T(8,128)(2,1)S(1)}, u32[]{:S(2)}, u32[]{:S(2)}) collective-permute-start(bf16[32,1152]{1,0:T(8,128)(2,1)S(1)} %collective-permute-done.1.refs_1_), channel_id=1, source_target_pairs={{0,8},{4,12},{8,0},{12,4},{16,24},{20,28},{24,16},{28,20},{1,9},{5... | collective-permute-start | bytes 221192 | tf_op jit(solution)/shard_map/ppermute | solution.py:24
  15.1 0.0 collective-permute-done.4.refs_4_
  15.1 0.6 collective-permute-start.5
  15.7 1.7 %collective-permute-done.3.refs_3_ = bf16[32,1152]{1,0:T(8,128)(2,1)S(1)} collective-permute-done((bf16[32,1152]{1,0:T(8,128)(2,1)S(1)}, bf16[32,1152]{1,0:T(8,128)(2,1)S(1)}, u32[]{:S(2)}, u32[]{:S(2)}) %collective-permute-start.3) | collective-permute-done | bytes 73760 | tf_op jit(solution)/shard_map/ppermute | solution.py:24
  17.5 2.0 %collective-permute-done.5.refs_5_ = bf16[32,1152]{1,0:T(8,128)(2,1)S(1)} collective-permute-done((bf16[32,1152]{1,0:T(8,128)(2,1)S(1)}, bf16[32,1152]{1,0:T(8,128)(2,1)S(1)}, u32[]{:S(2)}, u32[]{:S(2)}) %collective-permute-start.5) | collective-permute-done | bytes 73760 | tf_op jit(solution)/shard_map/ppermute | solution.py:24
  19.5 0.5 shard_map.93
  20.0 0.1 collective-permute-start.9
  20.1 1.6 %collective-permute-start.8 = (bf16[128,640]{1,0:T(8,128)(2,1)S(1)}, bf16[128,640]{1,0:T(8,128)(2,1)S(1)}, u32[]{:S(2)}, u32[]{:S(2)}) collective-permute-start(bf16[128,640]{1,0:T(8,128)(2,1)S(1)} %get-tuple-element.48), channel_id=1, source_target_pairs={{0,2},{1,3},{2,0},{3,1},{4,6},{5,7},{6,4},{7,5},{8,10},{9,11},{10,... | collective-permute-start | bytes 491528 | tf_op jit(solution)/shard_map/ppermute | solution.py:24
  21.7 0.5 collective-permute-start.7
  22.2 0.0 collective-permute-done.9.second
  22.3 1.9 %shard_map.94 = (f32[128,1152]{1,0:T(8,128)S(1)}, f32[128,1152]{1,0:T(8,128)S(1)}) custom-call(s32[1]{0:T(128)} %bitcast.tp_at, bf16[128,1152]{1,0:T(8,128)(2,1)S(1)} %get-tuple-element.49.first, bf16[128,1152]{1,0:T(8,128)(2,1)S(1)} %collective-permute-done.9.second, bf16[4608,1152]{1,0:T(8,128)(2,1)S(1)} %bitcast.8, bf16[4608,1152]{1,0:T(8,128)(2,1)S(1)} %bitcast.10, ...), custom_call_target="tpu_custom_call" | custom-call | flops 1358954496 | tf_op jit(solution)/shard_map/pallas_call | solution.py:211
  24.2 3.1 %collective-permute-done.8.refs_0_ = bf16[128,640]{1,0:T(8,128)(2,1)S(1)} collective-permute-done((bf16[128,640]{1,0:T(8,128)(2,1)S(1)}, bf16[128,640]{1,0:T(8,128)(2,1)S(1)}, u32[]{:S(2)}, u32[]{:S(2)}) %collective-permute-start.8) | collective-permute-done | bytes 163872 | tf_op jit(solution)/shard_map/ppermute | solution.py:24
  27.2 0.7 %shard_map.95 = (f32[128,1152]{1,0:T(8,128)S(1)}, f32[128,1152]{1,0:T(8,128)S(1)}) custom-call(s32[1]{0:T(128)} %bitcast.tp_at, bf16[128,640]{1,0:T(8,128)(2,1)S(1)} %collective-permute-done.8.refs_0_, f32[128,1152]{1,0:T(8,128)S(1)} %get-tuple-element.53.refs_1_, f32[128,1152]{1,0:T(8,128)S(1)} %get-tuple-element.54.refs_2_, ...), custom_call_target="tpu_custom_call" | custom-call | flops 339738624 | tf_op jit(solution)/shard_map/pallas_call | solution.py:211
  27.9 1.6 %collective-permute-done.7.refs_1_ = bf16[128,512]{1,0:T(8,128)(2,1)S(1)} collective-permute-done((bf16[128,512]{1,0:T(8,128)(2,1)S(1)}, bf16[128,512]{1,0:T(8,128)(2,1)S(1)}, u32[]{:S(2)}, u32[]{:S(2)}) %collective-permute-start.7) | collective-permute-done | bytes 131104 | tf_op jit(solution)/shard_map/ppermute | solution.py:24
  29.5 0.0 collective-permute-start.10
  29.5 0.0 collective-permute-done.11.refs_0_
  29.5 1.0 %shard_map.96 = (f32[128,1152]{1,0:T(8,128)S(1)}, f32[128,1152]{1,0:T(8,128)S(1)}) custom-call(s32[1]{0:T(128)} %bitcast.tp_at, bf16[128,640]{1,0:T(8,128)(2,1)S(1)} %collective-permute-done.11.refs_0_, bf16[128,512]{1,0:T(8,128)(2,1)S(1)} %collective-permute-done.7.refs_1_, f32[128,1152]{1,0:T(8,128)S(1)} %get-tuple-element.58.refs_2_, ...), custom_call_target="tpu_custom_call" | custom-call | flops 339738624 | tf_op jit(solution)/shard_map/pallas_call | solution.py:211
  30.5 0.3 collective-permute-done.10.rows
  30.9 0.6 shard_map.97.hidden
  31.4 0.4 shard_map.100
  31.9 0.3 collective-permute-start.13
  32.2 0.6 shard_map.98
  32.8 0.4 collective-permute-start.12
  33.1 0.3 shard_map.103
  33.5 0.3 collective-permute-start.15
  33.7 0.4 shard_map.101.first
  34.2 0.0 collective-permute-done.13.refs_0_
  34.2 0.0 copy-start
  34.2 0.0 copy-start.1
  34.2 1.6 %collective-permute-start.14 = (bf16[128,640]{1,0:T(8,128)(2,1)S(1)}, bf16[128,640]{1,0:T(8,128)(2,1)S(1)}, u32[]{:S(2)}, u32[]{:S(2)}) collective-permute-start(bf16[128,640]{1,0:T(8,128)(2,1)S(1)} %shard_map.102), channel_id=1, source_target_pairs={{0,2},{1,3},{2,0},{3,1},{4,6},{5,7},{6,4},{7,5},{8,10},{9,11},{10,... | collective-permute-start | bytes 491528 | tf_op jit(solution)/shard_map/ppermute | solution.py:24
  35.8 0.3 shard_map.104.first
  36.2 0.0 collective-permute-done.15.refs_0_
  36.2 0.6 collective-permute-start.16
  36.8 0.6 shard_map.99.near
  37.4 6.1 %collective-permute-done.16.second = bf16[128,512]{1,0:T(8,128)(2,1)S(1)} collective-permute-done((bf16[128,512]{1,0:T(8,128)(2,1)S(1)}, bf16[128,512]{1,0:T(8,128)(2,1)S(1)}, u32[]{:S(2)}, u32[]{:S(2)}) %collective-permute-start.16) | collective-permute-done | bytes 131104 | tf_op jit(solution)/shard_map/ppermute | solution.py:24
  43.5 0.0 collective-permute-done.14.first
  43.5 0.4 shard_map.106
  44.0 0.1 collective-permute-start.17
  44.1 1.0 %collective-permute-start.21 = (bf16[32,1152]{1,0:T(8,128)(2,1)S(1)}, bf16[32,1152]{1,0:T(8,128)(2,1)S(1)}, u32[]{:S(2)}, u32[]{:S(2)}) collective-permute-start(bf16[32,1152]{1,0:T(8,128)(2,1)S(1)} %get-tuple-element.76), channel_id=1, source_target_pairs={{0,4},{4,0},{8,12},{12,8},{16,20},{20,16},{24,28},{28,24},{1,5},{5... | collective-permute-start | bytes 221192 | tf_op jit(solution)/shard_map/ppermute | solution.py:24
  45.1 1.0 %collective-permute-start.19 = (bf16[32,1152]{1,0:T(8,128)(2,1)S(1)}, bf16[32,1152]{1,0:T(8,128)(2,1)S(1)}, u32[]{:S(2)}, u32[]{:S(2)}) collective-permute-start(bf16[32,1152]{1,0:T(8,128)(2,1)S(1)} %get-tuple-element.74), channel_id=1, source_target_pairs={{0,4},{4,0},{8,12},{12,8},{16,20},{20,16},{24,28},{28,24},{1,5},{5... | collective-permute-start | bytes 221192 | tf_op jit(solution)/shard_map/ppermute | solution.py:24
  46.2 2.4 %collective-permute-done.21.refs_0_ = bf16[32,1152]{1,0:T(8,128)(2,1)S(1)} collective-permute-done((bf16[32,1152]{1,0:T(8,128)(2,1)S(1)}, bf16[32,1152]{1,0:T(8,128)(2,1)S(1)}, u32[]{:S(2)}, u32[]{:S(2)}) %collective-permute-start.21) | collective-permute-done | bytes 73760 | tf_op jit(solution)/shard_map/ppermute | solution.py:24
  48.6 2.8 %collective-permute-start.22 = (bf16[32,1152]{1,0:T(8,128)(2,1)S(1)}, bf16[32,1152]{1,0:T(8,128)(2,1)S(1)}, u32[]{:S(2)}, u32[]{:S(2)}) collective-permute-start(bf16[32,1152]{1,0:T(8,128)(2,1)S(1)} %shard_map.109), channel_id=1, source_target_pairs={{0,16},{4,20},{8,24},{12,28},{16,0},{20,4},{24,8},{28,12},{1,17},{... | collective-permute-start | bytes 221192 | tf_op jit(solution)/shard_map/ppermute | solution.py:24
  51.4 1.6 %collective-permute-start.20 = (bf16[32,1152]{1,0:T(8,128)(2,1)S(1)}, bf16[32,1152]{1,0:T(8,128)(2,1)S(1)}, u32[]{:S(2)}, u32[]{:S(2)}) collective-permute-start(bf16[32,1152]{1,0:T(8,128)(2,1)S(1)} %shard_map.108), channel_id=1, source_target_pairs={{0,24},{4,28},{8,16},{12,20},{16,8},{20,12},{24,0},{28,4},{1,25},{... | collective-permute-start | bytes 221192 | tf_op jit(solution)/shard_map/ppermute | solution.py:24
  53.0 0.0 collective-permute-done.17.pair
  53.0 0.9 %collective-permute-start.18 = (bf16[32,1152]{1,0:T(8,128)(2,1)S(1)}, bf16[32,1152]{1,0:T(8,128)(2,1)S(1)}, u32[]{:S(2)}, u32[]{:S(2)}) collective-permute-start(bf16[32,1152]{1,0:T(8,128)(2,1)S(1)} %shard_map.107), channel_id=1, source_target_pairs={{0,4},{4,0},{8,12},{12,8},{16,20},{20,16},{24,28},{28,24},{1,5},{5... | collective-permute-start | bytes 221192 | tf_op jit(solution)/shard_map/ppermute | solution.py:24
  53.9 1.9 %collective-permute-done.22.refs_3_ = bf16[32,1152]{1,0:T(8,128)(2,1)S(1)} collective-permute-done((bf16[32,1152]{1,0:T(8,128)(2,1)S(1)}, bf16[32,1152]{1,0:T(8,128)(2,1)S(1)}, u32[]{:S(2)}, u32[]{:S(2)}) %collective-permute-start.22) | collective-permute-done | bytes 73760 | tf_op jit(solution)/shard_map/ppermute | solution.py:24
  55.7 1.9 %collective-permute-done.20.refs_2_ = bf16[32,1152]{1,0:T(8,128)(2,1)S(1)} collective-permute-done((bf16[32,1152]{1,0:T(8,128)(2,1)S(1)}, bf16[32,1152]{1,0:T(8,128)(2,1)S(1)}, u32[]{:S(2)}, u32[]{:S(2)}) %collective-permute-start.20) | collective-permute-done | bytes 73760 | tf_op jit(solution)/shard_map/ppermute | solution.py:24
  57.6 0.0 collective-permute-done.18.refs_1_
  57.6 0.1 shard_map.110.refs_0_
  57.6 1.6 %collective-permute-start.24 = (bf16[32,1152]{1,0:T(8,128)(2,1)S(1)}, bf16[32,1152]{1,0:T(8,128)(2,1)S(1)}, u32[]{:S(2)}, u32[]{:S(2)}) collective-permute-start(bf16[32,1152]{1,0:T(8,128)(2,1)S(1)} %shard_map.110.refs_0_), channel_id=1, source_target_pairs={{0,2},{1,3},{2,0},{3,1},{4,6},{5,7},{6,4},{7,5},{8,10},{9,11},{10,... | collective-permute-start | bytes 221192 | tf_op jit(solution)/shard_map/ppermute | solution.py:24
  59.2 2.8 %collective-permute-done.24.refs_2_ = bf16[32,1152]{1,0:T(8,128)(2,1)S(1)} collective-permute-done((bf16[32,1152]{1,0:T(8,128)(2,1)S(1)}, bf16[32,1152]{1,0:T(8,128)(2,1)S(1)}, u32[]{:S(2)}, u32[]{:S(2)}) %collective-permute-start.24) | collective-permute-done | bytes 73760 | tf_op jit(solution)/shard_map/ppermute | solution.py:24
  62.1 1.3 %collective-permute-done.25.refs_3_ = bf16[32,1152]{1,0:T(8,128)(2,1)S(1)} collective-permute-done((bf16[32,1152]{1,0:T(8,128)(2,1)S(1)}, bf16[32,1152]{1,0:T(8,128)(2,1)S(1)}, u32[]{:S(2)}, u32[]{:S(2)}) %collective-permute-start.25) | collective-permute-done | bytes 73760 | tf_op jit(solution)/shard_map/ppermute | solution.py:24
  63.3 1.6 %shard_map.111 = bf16[128,4608]{1,0:T(8,128)(2,1)} custom-call(s32[1]{0:T(128)} %bitcast.tp_at, bf16[128,32]{1,0:T(8,128)(2,1)S(1)} %get-tuple-element.41.picked, bf16[128,4608]{1,0:T(8,128)(2,1)S(1)} %copy-done, f32[32,128]{1,0:T(8,128)S(1)} %shard_map.92.weight, f32[36,128]{1,0:T(8,128)S(1)} %bitcast.11, bf16[32,1152]{1,0:T(8,128)(2,1)S(1)} %shard_map.110.refs_0_, ...), custom_call_target="tpu_custom_call" | custom-call | tf_op jit(solution)/shard_map/pallas_call | solution.py:211
  (34 shorter events, 0.2 us)
Async XLA Ops:
  2.8 7.7 %collective-permute-start = (bf16[32,1152]{1,0:T(8,128)(2,1)S(1)}, bf16[32,1152]{1,0:T(8,128)(2,1)S(1)}, u32[]{:S(2)}, u32[]{:S(2)}) collective-permute-start(bf16[32,1152]{1,0:T(8,128)(2,1)S(1)} %get-tuple-element.42.refs_0_), channel_id=1, source_target_pairs={{0,24},{4,28},{8,16},{12,20},{16,8},{20,12},{24,0},{28,4},{1,25},{... | collective-permute-start | bytes 221192 | tf_op jit(solution)/shard_map/ppermute | solution.py:24
  7.9 4.7 %collective-permute-start.1 = (bf16[32,1152]{1,0:T(8,128)(2,1)S(1)}, bf16[32,1152]{1,0:T(8,128)(2,1)S(1)}, u32[]{:S(2)}, u32[]{:S(2)}) collective-permute-start(bf16[32,1152]{1,0:T(8,128)(2,1)S(1)} %get-tuple-element.42.refs_0_), channel_id=1, source_target_pairs={{0,4},{4,0},{8,12},{12,8},{16,20},{20,16},{24,28},{28,24},{1,5},{5... | collective-permute-start | bytes 221192 | tf_op jit(solution)/shard_map/ppermute | solution.py:24
  9.4 5.7 %collective-permute-start.4 = (bf16[32,1152]{1,0:T(8,128)(2,1)S(1)}, bf16[32,1152]{1,0:T(8,128)(2,1)S(1)}, u32[]{:S(2)}, u32[]{:S(2)}) collective-permute-start(bf16[32,1152]{1,0:T(8,128)(2,1)S(1)} %get-tuple-element.42.refs_0_), channel_id=1, source_target_pairs={{0,16},{4,20},{8,24},{12,28},{16,0},{20,4},{24,8},{28,12},{1,17},{... | collective-permute-start | bytes 221192 | tf_op jit(solution)/shard_map/ppermute | solution.py:24
  9.4 6.3 %collective-permute-start.2 = (bf16[32,1152]{1,0:T(8,128)(2,1)S(1)}, bf16[32,1152]{1,0:T(8,128)(2,1)S(1)}, u32[]{:S(2)}, u32[]{:S(2)}) collective-permute-start(bf16[32,1152]{1,0:T(8,128)(2,1)S(1)} %get-tuple-element.42.refs_0_), channel_id=1, source_target_pairs={{0,8},{4,12},{8,0},{12,4},{16,24},{20,28},{24,16},{28,20},{1,9},{5... | collective-permute-start | bytes 221192 | tf_op jit(solution)/shard_map/ppermute | solution.py:24
  10.2 12.0 %slice-start = ((s8[10616832]{0:T(1024)(128)(4,1)}), s8[4194304]{0:T(1024)(128)(4,1)S(1)}, s32[]{:S(2)}) async-start(s8[10616832]{0:T(1024)(128)(4,1)} %bitcast.5), calls=%async_computation | async-start | bytes 8388608
  10.2 12.0 %slice-start.3 = ((s8[10616832]{0:T(1024)(128)(4,1)}), s8[4194304]{0:T(1024)(128)(4,1)S(1)}, s32[]{:S(2)}) async-start(s8[10616832]{0:T(1024)(128)(4,1)} %bitcast.7), calls=%async_computation.3 | async-start | bytes 8388608
  10.2 12.0 %slice-start.6 = ((s8[10616832]{0:T(1024)(128)(4,1)}), s8[4194304]{0:T(1024)(128)(4,1)S(1)}, s32[]{:S(2)}) async-start(s8[10616832]{0:T(1024)(128)(4,1)} %bitcast.9), calls=%async_computation.6 | async-start | bytes 8388608
  10.2 12.0 %slice-start.1 = ((s8[10616832]{0:T(1024)(128)(4,1)}), s8[4194304]{0:T(1024)(128)(4,1)S(1)}, s32[]{:S(2)}) async-start(s8[10616832]{0:T(1024)(128)(4,1)} %bitcast.5), calls=%async_computation.1 | async-start | bytes 8388608
  10.2 12.0 %slice-start.2 = ((s8[10616832]{0:T(1024)(128)(4,1)}), s8[2228224]{0:T(1024)(128)(4,1)S(1)}, s32[]{:S(2)}) async-start(s8[10616832]{0:T(1024)(128)(4,1)} %bitcast.5), calls=%async_computation.2 | async-start | bytes 4456448
  10.2 12.0 %slice-start.4 = ((s8[10616832]{0:T(1024)(128)(4,1)}), s8[4194304]{0:T(1024)(128)(4,1)S(1)}, s32[]{:S(2)}) async-start(s8[10616832]{0:T(1024)(128)(4,1)} %bitcast.7), calls=%async_computation.4 | async-start | bytes 8388608
  10.2 12.0 %slice-start.5 = ((s8[10616832]{0:T(1024)(128)(4,1)}), s8[2228224]{0:T(1024)(128)(4,1)S(1)}, s32[]{:S(2)}) async-start(s8[10616832]{0:T(1024)(128)(4,1)} %bitcast.7), calls=%async_computation.5 | async-start | bytes 4456448
  10.3 12.0 %slice-start.7 = ((s8[10616832]{0:T(1024)(128)(4,1)}), s8[4194304]{0:T(1024)(128)(4,1)S(1)}, s32[]{:S(2)}) async-start(s8[10616832]{0:T(1024)(128)(4,1)} %bitcast.9), calls=%async_computation.7 | async-start | bytes 8388608
  10.3 12.0 %slice-start.8 = ((s8[10616832]{0:T(1024)(128)(4,1)}), s8[2228224]{0:T(1024)(128)(4,1)S(1)}, s32[]{:S(2)}) async-start(s8[10616832]{0:T(1024)(128)(4,1)} %bitcast.9), calls=%async_computation.8 | async-start | bytes 4456448
  10.5 5.2 %collective-permute-start.6 = (bf16[32,1152]{1,0:T(8,128)(2,1)S(1)}, bf16[32,1152]{1,0:T(8,128)(2,1)S(1)}, u32[]{:S(2)}, u32[]{:S(2)}) collective-permute-start(bf16[32,1152]{1,0:T(8,128)(2,1)S(1)} %collective-permute-done.refs_6_), channel_id=1, source_target_pairs={{0,4},{4,0},{8,12},{12,8},{16,20},{20,16},{24,28},{28,24},{1,5},{5... | collective-permute-start | bytes 221192 | tf_op jit(solution)/shard_map/ppermute | solution.py:24
  12.6 4.8 %collective-permute-start.3 = (bf16[32,1152]{1,0:T(8,128)(2,1)S(1)}, bf16[32,1152]{1,0:T(8,128)(2,1)S(1)}, u32[]{:S(2)}, u32[]{:S(2)}) collective-permute-start(bf16[32,1152]{1,0:T(8,128)(2,1)S(1)} %collective-permute-done.1.refs_1_), channel_id=1, source_target_pairs={{0,8},{4,12},{8,0},{12,4},{16,24},{20,28},{24,16},{28,20},{1,9},{5... | collective-permute-start | bytes 221192 | tf_op jit(solution)/shard_map/ppermute | solution.py:24
  15.1 4.4 %collective-permute-start.5 = (bf16[32,1152]{1,0:T(8,128)(2,1)S(1)}, bf16[32,1152]{1,0:T(8,128)(2,1)S(1)}, u32[]{:S(2)}, u32[]{:S(2)}) collective-permute-start(bf16[32,1152]{1,0:T(8,128)(2,1)S(1)} %collective-permute-done.4.refs_4_), channel_id=1, source_target_pairs={{0,4},{4,0},{8,12},{12,8},{16,20},{20,16},{24,28},{28,24},{1,5},{5... | collective-permute-start | bytes 221192 | tf_op jit(solution)/shard_map/ppermute | solution.py:24
  20.0 2.2 %collective-permute-start.9 = (bf16[128,1152]{1,0:T(8,128)(2,1)S(1)}, bf16[128,1152]{1,0:T(8,128)(2,1)S(1)}, u32[]{:S(2)}, u32[]{:S(2)}) collective-permute-start(bf16[128,1152]{1,0:T(8,128)(2,1)S(1)} %get-tuple-element.49.first), channel_id=1, source_target_pairs={{0,1},{1,0},{2,3},{3,2},{4,5},{5,4},{6,7},{7,6},{8,9},{9,8},{10,11... | collective-permute-start | bytes 884744 | tf_op jit(solution)/shard_map/ppermute | solution.py:24
  20.1 7.1 %collective-permute-start.8 = (bf16[128,640]{1,0:T(8,128)(2,1)S(1)}, bf16[128,640]{1,0:T(8,128)(2,1)S(1)}, u32[]{:S(2)}, u32[]{:S(2)}) collective-permute-start(bf16[128,640]{1,0:T(8,128)(2,1)S(1)} %get-tuple-element.48), channel_id=1, source_target_pairs={{0,2},{1,3},{2,0},{3,1},{4,6},{5,7},{6,4},{7,5},{8,10},{9,11},{10,... | collective-permute-start | bytes 491528 | tf_op jit(solution)/shard_map/ppermute | solution.py:24
  21.7 7.8 %collective-permute-start.7 = (bf16[128,512]{1,0:T(8,128)(2,1)S(1)}, bf16[128,512]{1,0:T(8,128)(2,1)S(1)}, u32[]{:S(2)}, u32[]{:S(2)}) collective-permute-start(bf16[128,512]{1,0:T(8,128)(2,1)S(1)} %get-tuple-element.47), channel_id=1, source_target_pairs={{0,2},{1,3},{2,0},{3,1},{4,6},{5,7},{6,4},{7,5},{8,10},{9,11},{10,... | collective-permute-start | bytes 393224 | tf_op jit(solution)/shard_map/ppermute | solution.py:24
  27.2 2.3 %collective-permute-start.11 = (bf16[128,640]{1,0:T(8,128)(2,1)S(1)}, bf16[128,640]{1,0:T(8,128)(2,1)S(1)}, u32[]{:S(2)}, u32[]{:S(2)}) collective-permute-start(bf16[128,640]{1,0:T(8,128)(2,1)S(1)} %collective-permute-done.8.refs_0_), channel_id=1, source_target_pairs={{0,1},{1,0},{2,3},{3,2},{4,5},{5,4},{6,7},{7,6},{8,9},{9,8},{10,11... | collective-permute-start | bytes 491528 | tf_op jit(solution)/shard_map/ppermute | solution.py:24
  29.5 1.3 %collective-permute-start.10 = (bf16[128,512]{1,0:T(8,128)(2,1)S(1)}, bf16[128,512]{1,0:T(8,128)(2,1)S(1)}, u32[]{:S(2)}, u32[]{:S(2)}) collective-permute-start(bf16[128,512]{1,0:T(8,128)(2,1)S(1)} %collective-permute-done.7.refs_1_), channel_id=1, source_target_pairs={{0,1},{1,0},{2,3},{3,2},{4,5},{5,4},{6,7},{7,6},{8,9},{9,8},{10,11... | collective-permute-start | bytes 393224 | tf_op jit(solution)/shard_map/ppermute | solution.py:24
  31.9 2.3 %collective-permute-start.13 = (bf16[128,640]{1,0:T(8,128)(2,1)S(1)}, bf16[128,640]{1,0:T(8,128)(2,1)S(1)}, u32[]{:S(2)}, u32[]{:S(2)}) collective-permute-start(bf16[128,640]{1,0:T(8,128)(2,1)S(1)} %shard_map.100), channel_id=1, source_target_pairs={{0,1},{1,0},{2,3},{3,2},{4,5},{5,4},{6,7},{7,6},{8,9},{9,8},{10,11... | collective-permute-start | bytes 491528 | tf_op jit(solution)/shard_map/ppermute | solution.py:24
  32.8 4.0 %collective-permute-start.12 = (bf16[128,1152]{1,0:T(8,128)(2,1)S(1)}, bf16[128,1152]{1,0:T(8,128)(2,1)S(1)}, u32[]{:S(2)}, u32[]{:S(2)}) collective-permute-start(bf16[128,1152]{1,0:T(8,128)(2,1)S(1)} %shard_map.98), channel_id=1, source_target_pairs={{0,1},{1,0},{2,3},{3,2},{4,5},{5,4},{6,7},{7,6},{8,9},{9,8},{10,11... | collective-permute-start | bytes 884744 | tf_op jit(solution)/shard_map/ppermute | solution.py:24
  33.5 2.7 %collective-permute-start.15 = (bf16[128,512]{1,0:T(8,128)(2,1)S(1)}, bf16[128,512]{1,0:T(8,128)(2,1)S(1)}, u32[]{:S(2)}, u32[]{:S(2)}) collective-permute-start(bf16[128,512]{1,0:T(8,128)(2,1)S(1)} %shard_map.103), channel_id=1, source_target_pairs={{0,1},{1,0},{2,3},{3,2},{4,5},{5,4},{6,7},{7,6},{8,9},{9,8},{10,11... | collective-permute-start | bytes 393224 | tf_op jit(solution)/shard_map/ppermute | solution.py:24
  34.2 29.1 %copy-start = (bf16[128,4608]{1,0:T(8,128)(2,1)S(1)}, bf16[128,4608]{1,0:T(8,128)(2,1)}, u32[]{:S(2)}) copy-start(bf16[128,4608]{1,0:T(8,128)(2,1)} %tokens.3) | copy-start | bytes 3538948
  34.2 29.1 %copy-start.1 = (f32[4608]{0:T(1024)S(1)}, f32[4608]{0:T(1024)}, u32[]{:S(2)}) copy-start(f32[4608]{0:T(1024)} %param.14) | copy-start | bytes 55300
  34.2 9.3 %collective-permute-start.14 = (bf16[128,640]{1,0:T(8,128)(2,1)S(1)}, bf16[128,640]{1,0:T(8,128)(2,1)S(1)}, u32[]{:S(2)}, u32[]{:S(2)}) collective-permute-start(bf16[128,640]{1,0:T(8,128)(2,1)S(1)} %shard_map.102), channel_id=1, source_target_pairs={{0,2},{1,3},{2,0},{3,1},{4,6},{5,7},{6,4},{7,5},{8,10},{9,11},{10,... | collective-permute-start | bytes 491528 | tf_op jit(solution)/shard_map/ppermute | solution.py:24
  36.2 7.3 %collective-permute-start.16 = (bf16[128,512]{1,0:T(8,128)(2,1)S(1)}, bf16[128,512]{1,0:T(8,128)(2,1)S(1)}, u32[]{:S(2)}, u32[]{:S(2)}) collective-permute-start(bf16[128,512]{1,0:T(8,128)(2,1)S(1)} %shard_map.105), channel_id=1, source_target_pairs={{0,2},{1,3},{2,0},{3,1},{4,6},{5,7},{6,4},{7,5},{8,10},{9,11},{10,... | collective-permute-start | bytes 393224 | tf_op jit(solution)/shard_map/ppermute | solution.py:24
  44.0 9.0 %collective-permute-start.17 = (bf16[64,1152]{1,0:T(8,128)(2,1)S(1)}, bf16[64,1152]{1,0:T(8,128)(2,1)S(1)}, u32[]{:S(2)}, u32[]{:S(2)}) collective-permute-start(bf16[64,1152]{1,0:T(8,128)(2,1)S(1)} %get-tuple-element.70), channel_id=1, source_target_pairs={{0,8},{4,12},{8,0},{12,4},{16,24},{20,28},{24,16},{28,20},{1,9},{5... | collective-permute-start | bytes 442376 | tf_op jit(solution)/shard_map/ppermute | solution.py:24
  44.1 4.4 %collective-permute-start.21 = (bf16[32,1152]{1,0:T(8,128)(2,1)S(1)}, bf16[32,1152]{1,0:T(8,128)(2,1)S(1)}, u32[]{:S(2)}, u32[]{:S(2)}) collective-permute-start(bf16[32,1152]{1,0:T(8,128)(2,1)S(1)} %get-tuple-element.76), channel_id=1, source_target_pairs={{0,4},{4,0},{8,12},{12,8},{16,20},{20,16},{24,28},{28,24},{1,5},{5... | collective-permute-start | bytes 221192 | tf_op jit(solution)/shard_map/ppermute | solution.py:24
  45.1 6.2 %collective-permute-start.19 = (bf16[32,1152]{1,0:T(8,128)(2,1)S(1)}, bf16[32,1152]{1,0:T(8,128)(2,1)S(1)}, u32[]{:S(2)}, u32[]{:S(2)}) collective-permute-start(bf16[32,1152]{1,0:T(8,128)(2,1)S(1)} %get-tuple-element.74), channel_id=1, source_target_pairs={{0,4},{4,0},{8,12},{12,8},{16,20},{20,16},{24,28},{28,24},{1,5},{5... | collective-permute-start | bytes 221192 | tf_op jit(solution)/shard_map/ppermute | solution.py:24
  48.6 7.1 %collective-permute-start.22 = (bf16[32,1152]{1,0:T(8,128)(2,1)S(1)}, bf16[32,1152]{1,0:T(8,128)(2,1)S(1)}, u32[]{:S(2)}, u32[]{:S(2)}) collective-permute-start(bf16[32,1152]{1,0:T(8,128)(2,1)S(1)} %shard_map.109), channel_id=1, source_target_pairs={{0,16},{4,20},{8,24},{12,28},{16,0},{20,4},{24,8},{28,12},{1,17},{... | collective-permute-start | bytes 221192 | tf_op jit(solution)/shard_map/ppermute | solution.py:24
  51.4 6.2 %collective-permute-start.20 = (bf16[32,1152]{1,0:T(8,128)(2,1)S(1)}, bf16[32,1152]{1,0:T(8,128)(2,1)S(1)}, u32[]{:S(2)}, u32[]{:S(2)}) collective-permute-start(bf16[32,1152]{1,0:T(8,128)(2,1)S(1)} %shard_map.108), channel_id=1, source_target_pairs={{0,24},{4,28},{8,16},{12,20},{16,8},{20,12},{24,0},{28,4},{1,25},{... | collective-permute-start | bytes 221192 | tf_op jit(solution)/shard_map/ppermute | solution.py:24
  53.0 4.6 %collective-permute-start.18 = (bf16[32,1152]{1,0:T(8,128)(2,1)S(1)}, bf16[32,1152]{1,0:T(8,128)(2,1)S(1)}, u32[]{:S(2)}, u32[]{:S(2)}) collective-permute-start(bf16[32,1152]{1,0:T(8,128)(2,1)S(1)} %shard_map.107), channel_id=1, source_target_pairs={{0,4},{4,0},{8,12},{12,8},{16,20},{20,16},{24,28},{28,24},{1,5},{5... | collective-permute-start | bytes 221192 | tf_op jit(solution)/shard_map/ppermute | solution.py:24
  57.6 4.4 %collective-permute-start.24 = (bf16[32,1152]{1,0:T(8,128)(2,1)S(1)}, bf16[32,1152]{1,0:T(8,128)(2,1)S(1)}, u32[]{:S(2)}, u32[]{:S(2)}) collective-permute-start(bf16[32,1152]{1,0:T(8,128)(2,1)S(1)} %shard_map.110.refs_0_), channel_id=1, source_target_pairs={{0,2},{1,3},{2,0},{3,1},{4,6},{5,7},{6,4},{7,5},{8,10},{9,11},{10,... | collective-permute-start | bytes 221192 | tf_op jit(solution)/shard_map/ppermute | solution.py:24
  59.2 2.8 %collective-permute-start.23 = (bf16[32,1152]{1,0:T(8,128)(2,1)S(1)}, bf16[32,1152]{1,0:T(8,128)(2,1)S(1)}, u32[]{:S(2)}, u32[]{:S(2)}) collective-permute-start(bf16[32,1152]{1,0:T(8,128)(2,1)S(1)} %shard_map.110.refs_0_), channel_id=1, source_target_pairs={{0,1},{1,0},{2,3},{3,2},{4,5},{5,4},{6,7},{7,6},{8,9},{9,8},{10,11... | collective-permute-start | bytes 221192 | tf_op jit(solution)/shard_map/ppermute | solution.py:24
  62.1 1.3 %collective-permute-start.25 = (bf16[32,1152]{1,0:T(8,128)(2,1)S(1)}, bf16[32,1152]{1,0:T(8,128)(2,1)S(1)}, u32[]{:S(2)}, u32[]{:S(2)}) collective-permute-start(bf16[32,1152]{1,0:T(8,128)(2,1)S(1)} %collective-permute-done.24.refs_2_), channel_id=1, source_target_pairs={{0,1},{1,0},{2,3},{3,2},{4,5},{5,4},{6,7},{7,6},{8,9},{9,8},{10,11... | collective-permute-start | bytes 221192 | tf_op jit(solution)/shard_map/ppermute | solution.py:24

commit v3 on v2

--- a/solution.py
+++ b/solution.py
@@ -15,7 +15,8 @@
 VMEM = pl.BlockSpec(memory_space=pltpu.VMEM)
 SMEM = pl.BlockSpec(memory_space=pltpu.SMEM)
 HBM = pl.BlockSpec(memory_space=pltpu.HBM)
-CHUNKS = 4
+CHUNKS = 1
+OUT_CHUNKS = 4
 TP = 4
 
 
@@ -42,9 +43,9 @@
     return jnp.where(hit, 1.0, 0.0).astype(BF16)
 
 
-def chunks(width):
-    step = width // CHUNKS
-    return [(part, slice(part * step, (part + 1) * step)) for part in range(CHUNKS)]
+def chunks(width, count):
+    step = width // count
+    return [(part, slice(part * step, (part + 1) * step)) for part in range(count)]
 
 
 def scaled(values, gain):
@@ -60,7 +61,7 @@
     capacity, piece = own.shape
     width = tokens.shape[1]
     copies = [
-        pltpu.make_async_copy(tokens.at[:, at], tokens_v.at[:, at], sems.at[part]) for part, at in chunks(width)
+        pltpu.make_async_copy(tokens.at[:, at], tokens_v.at[:, at], sems.at[part]) for part, at in chunks(width, CHUNKS)
     ]
     small = [
         pltpu.make_async_copy(source, target, done.at[at])
@@ -73,11 +74,11 @@
     small[0].wait()
     count = counts[0]
     picked[...] = picker(chosen_v[...], count, tokens.shape[0])
-    hot = picked[...]
+    hot = picked[...].astype(F32).T.astype(BF16)
     square = jnp.zeros((capacity, 1), F32)
-    for part, at in chunks(width):
+    for part, at in chunks(width, CHUNKS):
         copies[part].wait()
-        values = dot_rows(hot, tokens_v[:, at])
+        values = dot_f32(hot, tokens_v[:, at])
         rows[:, at] = values.astype(BF16)
         square = square + jnp.sum(values * values, axis=1, keepdims=True)
     small[1].wait()
@@ -196,9 +197,9 @@
     values = joined[...]
     scale = lax.rsqrt(jnp.mean(values * values, axis=1, keepdims=True) + EPS) * weight[:, :1]
     hot = picked[...]
-    rows = gain.shape[0] // CHUNKS
+    rows = gain.shape[0] // OUT_CHUNKS
     copies = []
-    for part, at in chunks(width):
+    for part, at in chunks(width, OUT_CHUNKS):
         update = scaled(values[:, at] * scale, gain[part * rows : (part + 1) * rows, :]).astype(BF16)
         staged[:, at] = (tokens[:, at].astype(F32) + dot_f32(hot, update)).astype(BF16)
         copies.append(pltpu.make_async_copy(staged.at[:, at], out.at[:, at], sems.at[part]))
@@ -338,7 +339,7 @@
         scratch=(
             pltpu.VMEM((capacity, width), F32),
             pltpu.VMEM(tokens.shape, BF16),
-            pltpu.SemaphoreType.DMA((CHUNKS,)),
+            pltpu.SemaphoreType.DMA((OUT_CHUNKS,)),
         ),
         out_spec=HBM,
     )

time: 65 us -> 64.7 us (level)
  transfers between devices with their start and end apart: 26 -> 26, of which waited for: 13 -> 13; matrix products, arithmetic and copies ran while one was open for 0% -> 0% of each run, Pallas kernels for 9% -> 10%
where the time goes in v3:
time: 64.7 us; the launch traced here: 64.5 us
  starting transfers between devices  26.4 us (41%)
  waiting for transfers between devices  25.6 us (40%)
  Pallas kernels  11.5 us (18%)
  between operations  0.95 us (1%)
    ppermute x26, starting transfers between devices, swap(): return lax.ppermute(value, axis, [(i, i ^ bits) for i in range(size)])  26.4 us
    ppermute x26, waiting for transfers between devices, swap(): return lax.ppermute(value, axis, [(i, i ^ bits) for i in range(size)])  25.6 us
    pallas_call x21, Pallas kernels, call(): pl.pallas_call(kernel, out_shape=shapes, in_specs=[SMEM] * len(scalars) +...  11.5 us
  transfers between devices with their start and end apart: 26, of which 13 were waited for; matrix products, arithmetic and copies ran while one was open for 0% of the time, Pallas kernels for 10%

profile of v3, /device:TPU:0, one launch (start us, length us, event | category | flops | bytes accessed | tf_op | source)
XLA Modules:
  0.0 64.5 jit_solution(17017681712107867783)
XLA Ops:
  0.7 1.7 %shard_map.91 = (bf16[32,1152]{1,0:T(8,128)(2,1)S(1)}, bf16[32,4608]{1,0:T(8,128)(2,1)S(1)}, bf16[128,32]{1,0:T(8,128)(2,1)S(1)}, f32[36,128]{1,0:T(8,128)S(1)}) custom-call(s32[1]{0:T(128)S(6)} %copy.10.counts, s32[1]{0:T(128)} %bitcast.tp_at, s32[1]{0:T(128)} %bitcast.1.seq_at, s32[1,32]{1,0:T(1,128)} %chosen.1, bf16[128,4608]{1,0:T(8,128)(2,1)} %tokens.3, ...), custom_call_target="tpu_custom_call" | custom-call | tf_op jit(solution)/shard_map/pallas_call | solution.py:212
  2.4 5.1 %collective-permute-start = (bf16[32,1152]{1,0:T(8,128)(2,1)S(1)}, bf16[32,1152]{1,0:T(8,128)(2,1)S(1)}, u32[]{:S(2)}, u32[]{:S(2)}) collective-permute-start(bf16[32,1152]{1,0:T(8,128)(2,1)S(1)} %get-tuple-element.42.refs_0_), channel_id=1, source_target_pairs={{0,24},{4,28},{8,16},{12,20},{16,8},{20,12},{24,0},{28,4},{1,25},{... | collective-permute-start | bytes 221192 | tf_op jit(solution)/shard_map/ppermute | solution.py:25
  7.5 1.5 %collective-permute-start.1 = (bf16[32,1152]{1,0:T(8,128)(2,1)S(1)}, bf16[32,1152]{1,0:T(8,128)(2,1)S(1)}, u32[]{:S(2)}, u32[]{:S(2)}) collective-permute-start(bf16[32,1152]{1,0:T(8,128)(2,1)S(1)} %get-tuple-element.42.refs_0_), channel_id=1, source_target_pairs={{0,4},{4,0},{8,12},{12,8},{16,20},{20,16},{24,28},{28,24},{1,5},{5... | collective-permute-start | bytes 221192 | tf_op jit(solution)/shard_map/ppermute | solution.py:25
  9.0 0.8 %collective-permute-start.2 = (bf16[32,1152]{1,0:T(8,128)(2,1)S(1)}, bf16[32,1152]{1,0:T(8,128)(2,1)S(1)}, u32[]{:S(2)}, u32[]{:S(2)}) collective-permute-start(bf16[32,1152]{1,0:T(8,128)(2,1)S(1)} %get-tuple-element.42.refs_0_), channel_id=1, source_target_pairs={{0,8},{4,12},{8,0},{12,4},{16,24},{20,28},{24,16},{28,20},{1,9},{5... | collective-permute-start | bytes 221192 | tf_op jit(solution)/shard_map/ppermute | solution.py:25
  9.8 0.0 slice-start.2
  9.9 0.0 slice-start.5
  9.9 0.0 slice-start.7
  9.9 0.1 shard_map.92.weight
  10.0 0.1 collective-permute-done.refs_6_
  10.1 1.7 %collective-permute-start.6 = (bf16[32,1152]{1,0:T(8,128)(2,1)S(1)}, bf16[32,1152]{1,0:T(8,128)(2,1)S(1)}, u32[]{:S(2)}, u32[]{:S(2)}) collective-permute-start(bf16[32,1152]{1,0:T(8,128)(2,1)S(1)} %collective-permute-done.refs_6_), channel_id=1, source_target_pairs={{0,4},{4,0},{8,12},{12,8},{16,20},{20,16},{24,28},{28,24},{1,5},{5... | collective-permute-start | bytes 221192 | tf_op jit(solution)/shard_map/ppermute | solution.py:25
  11.9 0.4 collective-permute-done.1.refs_1_
  12.2 2.5 %collective-permute-start.3 = (bf16[32,1152]{1,0:T(8,128)(2,1)S(1)}, bf16[32,1152]{1,0:T(8,128)(2,1)S(1)}, u32[]{:S(2)}, u32[]{:S(2)}) collective-permute-start(bf16[32,1152]{1,0:T(8,128)(2,1)S(1)} %collective-permute-done.1.refs_1_), channel_id=1, source_target_pairs={{0,8},{4,12},{8,0},{12,4},{16,24},{20,28},{24,16},{28,20},{1,9},{5... | collective-permute-start | bytes 221192 | tf_op jit(solution)/shard_map/ppermute | solution.py:25
  14.7 0.0 collective-permute-done.4.refs_4_
  14.7 0.6 collective-permute-start.5
  15.3 1.7 %collective-permute-done.3.refs_3_ = bf16[32,1152]{1,0:T(8,128)(2,1)S(1)} collective-permute-done((bf16[32,1152]{1,0:T(8,128)(2,1)S(1)}, bf16[32,1152]{1,0:T(8,128)(2,1)S(1)}, u32[]{:S(2)}, u32[]{:S(2)}) %collective-permute-start.3) | collective-permute-done | bytes 73760 | tf_op jit(solution)/shard_map/ppermute | solution.py:25
  17.1 2.0 %collective-permute-done.5.refs_5_ = bf16[32,1152]{1,0:T(8,128)(2,1)S(1)} collective-permute-done((bf16[32,1152]{1,0:T(8,128)(2,1)S(1)}, bf16[32,1152]{1,0:T(8,128)(2,1)S(1)}, u32[]{:S(2)}, u32[]{:S(2)}) %collective-permute-start.5) | collective-permute-done | bytes 73760 | tf_op jit(solution)/shard_map/ppermute | solution.py:25
  19.1 0.5 shard_map.93
  19.6 0.1 collective-permute-start.9
  19.7 1.6 %collective-permute-start.8 = (bf16[128,640]{1,0:T(8,128)(2,1)S(1)}, bf16[128,640]{1,0:T(8,128)(2,1)S(1)}, u32[]{:S(2)}, u32[]{:S(2)}) collective-permute-start(bf16[128,640]{1,0:T(8,128)(2,1)S(1)} %get-tuple-element.48), channel_id=1, source_target_pairs={{0,2},{1,3},{2,0},{3,1},{4,6},{5,7},{6,4},{7,5},{8,10},{9,11},{10,... | collective-permute-start | bytes 491528 | tf_op jit(solution)/shard_map/ppermute | solution.py:25
  21.3 0.5 collective-permute-start.7
  21.8 0.0 collective-permute-done.9.second
  21.9 1.9 %shard_map.94 = (f32[128,1152]{1,0:T(8,128)S(1)}, f32[128,1152]{1,0:T(8,128)S(1)}) custom-call(s32[1]{0:T(128)} %bitcast.tp_at, bf16[128,1152]{1,0:T(8,128)(2,1)S(1)} %get-tuple-element.49.first, bf16[128,1152]{1,0:T(8,128)(2,1)S(1)} %collective-permute-done.9.second, bf16[4608,1152]{1,0:T(8,128)(2,1)S(1)} %bitcast.8, bf16[4608,1152]{1,0:T(8,128)(2,1)S(1)} %bitcast.10, ...), custom_call_target="tpu_custom_call" | custom-call | flops 1358954496 | tf_op jit(solution)/shard_map/pallas_call | solution.py:212
  23.8 3.1 %collective-permute-done.8.refs_0_ = bf16[128,640]{1,0:T(8,128)(2,1)S(1)} collective-permute-done((bf16[128,640]{1,0:T(8,128)(2,1)S(1)}, bf16[128,640]{1,0:T(8,128)(2,1)S(1)}, u32[]{:S(2)}, u32[]{:S(2)}) %collective-permute-start.8) | collective-permute-done | bytes 163872 | tf_op jit(solution)/shard_map/ppermute | solution.py:25
  26.9 0.7 %shard_map.95 = (f32[128,1152]{1,0:T(8,128)S(1)}, f32[128,1152]{1,0:T(8,128)S(1)}) custom-call(s32[1]{0:T(128)} %bitcast.tp_at, bf16[128,640]{1,0:T(8,128)(2,1)S(1)} %collective-permute-done.8.refs_0_, f32[128,1152]{1,0:T(8,128)S(1)} %get-tuple-element.53.refs_1_, f32[128,1152]{1,0:T(8,128)S(1)} %get-tuple-element.54.refs_2_, ...), custom_call_target="tpu_custom_call" | custom-call | flops 339738624 | tf_op jit(solution)/shard_map/pallas_call | solution.py:212
  27.6 1.6 %collective-permute-done.7.refs_1_ = bf16[128,512]{1,0:T(8,128)(2,1)S(1)} collective-permute-done((bf16[128,512]{1,0:T(8,128)(2,1)S(1)}, bf16[128,512]{1,0:T(8,128)(2,1)S(1)}, u32[]{:S(2)}, u32[]{:S(2)}) %collective-permute-start.7) | collective-permute-done | bytes 131104 | tf_op jit(solution)/shard_map/ppermute | solution.py:25
  29.1 0.0 collective-permute-start.10
  29.1 0.0 collective-permute-done.11.refs_0_
  29.1 1.0 %shard_map.96 = (f32[128,1152]{1,0:T(8,128)S(1)}, f32[128,1152]{1,0:T(8,128)S(1)}) custom-call(s32[1]{0:T(128)} %bitcast.tp_at, bf16[128,640]{1,0:T(8,128)(2,1)S(1)} %collective-permute-done.11.refs_0_, bf16[128,512]{1,0:T(8,128)(2,1)S(1)} %collective-permute-done.7.refs_1_, f32[128,1152]{1,0:T(8,128)S(1)} %get-tuple-element.58.refs_2_, ...), custom_call_target="tpu_custom_call" | custom-call | flops 339738624 | tf_op jit(solution)/shard_map/pallas_call | solution.py:212
  30.2 0.3 collective-permute-done.10.rows
  30.5 0.6 shard_map.97.hidden
  31.1 0.4 shard_map.100
  31.5 0.3 collective-permute-start.13
  31.8 0.6 shard_map.98
  32.4 0.4 collective-permute-start.12
  32.8 0.3 shard_map.103
  33.1 0.3 collective-permute-start.15
  33.4 0.4 shard_map.101.first
  33.8 0.0 collective-permute-done.13.refs_0_
  33.8 0.0 copy-start
  33.8 0.0 copy-start.1
  33.9 1.6 %collective-permute-start.14 = (bf16[128,640]{1,0:T(8,128)(2,1)S(1)}, bf16[128,640]{1,0:T(8,128)(2,1)S(1)}, u32[]{:S(2)}, u32[]{:S(2)}) collective-permute-start(bf16[128,640]{1,0:T(8,128)(2,1)S(1)} %shard_map.102), channel_id=1, source_target_pairs={{0,2},{1,3},{2,0},{3,1},{4,6},{5,7},{6,4},{7,5},{8,10},{9,11},{10,... | collective-permute-start | bytes 491528 | tf_op jit(solution)/shard_map/ppermute | solution.py:25
  35.5 0.3 shard_map.104.first
  35.8 0.0 collective-permute-done.15.refs_0_
  35.9 0.6 collective-permute-start.16
  36.4 0.6 shard_map.99.near
  37.0 6.1 %collective-permute-done.16.second = bf16[128,512]{1,0:T(8,128)(2,1)S(1)} collective-permute-done((bf16[128,512]{1,0:T(8,128)(2,1)S(1)}, bf16[128,512]{1,0:T(8,128)(2,1)S(1)}, u32[]{:S(2)}, u32[]{:S(2)}) %collective-permute-start.16) | collective-permute-done | bytes 131104 | tf_op jit(solution)/shard_map/ppermute | solution.py:25
  43.2 0.0 collective-permute-done.14.first
  43.2 0.4 shard_map.106
  43.6 0.1 collective-permute-start.17
  43.7 1.0 %collective-permute-start.21 = (bf16[32,1152]{1,0:T(8,128)(2,1)S(1)}, bf16[32,1152]{1,0:T(8,128)(2,1)S(1)}, u32[]{:S(2)}, u32[]{:S(2)}) collective-permute-start(bf16[32,1152]{1,0:T(8,128)(2,1)S(1)} %get-tuple-element.76), channel_id=1, source_target_pairs={{0,4},{4,0},{8,12},{12,8},{16,20},{20,16},{24,28},{28,24},{1,5},{5... | collective-permute-start | bytes 221192 | tf_op jit(solution)/shard_map/ppermute | solution.py:25
  44.8 1.0 %collective-permute-start.19 = (bf16[32,1152]{1,0:T(8,128)(2,1)S(1)}, bf16[32,1152]{1,0:T(8,128)(2,1)S(1)}, u32[]{:S(2)}, u32[]{:S(2)}) collective-permute-start(bf16[32,1152]{1,0:T(8,128)(2,1)S(1)} %get-tuple-element.74), channel_id=1, source_target_pairs={{0,4},{4,0},{8,12},{12,8},{16,20},{20,16},{24,28},{28,24},{1,5},{5... | collective-permute-start | bytes 221192 | tf_op jit(solution)/shard_map/ppermute | solution.py:25
  45.8 2.4 %collective-permute-done.21.refs_0_ = bf16[32,1152]{1,0:T(8,128)(2,1)S(1)} collective-permute-done((bf16[32,1152]{1,0:T(8,128)(2,1)S(1)}, bf16[32,1152]{1,0:T(8,128)(2,1)S(1)}, u32[]{:S(2)}, u32[]{:S(2)}) %collective-permute-start.21) | collective-permute-done | bytes 73760 | tf_op jit(solution)/shard_map/ppermute | solution.py:25
  48.2 2.8 %collective-permute-start.22 = (bf16[32,1152]{1,0:T(8,128)(2,1)S(1)}, bf16[32,1152]{1,0:T(8,128)(2,1)S(1)}, u32[]{:S(2)}, u32[]{:S(2)}) collective-permute-start(bf16[32,1152]{1,0:T(8,128)(2,1)S(1)} %shard_map.109), channel_id=1, source_target_pairs={{0,16},{4,20},{8,24},{12,28},{16,0},{20,4},{24,8},{28,12},{1,17},{... | collective-permute-start | bytes 221192 | tf_op jit(solution)/shard_map/ppermute | solution.py:25
  51.0 0.0 collective-permute-done.19.refs_0_
  51.0 1.6 %collective-permute-start.20 = (bf16[32,1152]{1,0:T(8,128)(2,1)S(1)}, bf16[32,1152]{1,0:T(8,128)(2,1)S(1)}, u32[]{:S(2)}, u32[]{:S(2)}) collective-permute-start(bf16[32,1152]{1,0:T(8,128)(2,1)S(1)} %shard_map.108), channel_id=1, source_target_pairs={{0,24},{4,28},{8,16},{12,20},{16,8},{20,12},{24,0},{28,4},{1,25},{... | collective-permute-start | bytes 221192 | tf_op jit(solution)/shard_map/ppermute | solution.py:25
  52.6 0.9 %collective-permute-start.18 = (bf16[32,1152]{1,0:T(8,128)(2,1)S(1)}, bf16[32,1152]{1,0:T(8,128)(2,1)S(1)}, u32[]{:S(2)}, u32[]{:S(2)}) collective-permute-start(bf16[32,1152]{1,0:T(8,128)(2,1)S(1)} %shard_map.107), channel_id=1, source_target_pairs={{0,4},{4,0},{8,12},{12,8},{16,20},{20,16},{24,28},{28,24},{1,5},{5... | collective-permute-start | bytes 221192 | tf_op jit(solution)/shard_map/ppermute | solution.py:25
  53.5 1.9 %collective-permute-done.22.refs_3_ = bf16[32,1152]{1,0:T(8,128)(2,1)S(1)} collective-permute-done((bf16[32,1152]{1,0:T(8,128)(2,1)S(1)}, bf16[32,1152]{1,0:T(8,128)(2,1)S(1)}, u32[]{:S(2)}, u32[]{:S(2)}) %collective-permute-start.22) | collective-permute-done | bytes 73760 | tf_op jit(solution)/shard_map/ppermute | solution.py:25
  55.4 1.9 %collective-permute-done.20.refs_2_ = bf16[32,1152]{1,0:T(8,128)(2,1)S(1)} collective-permute-done((bf16[32,1152]{1,0:T(8,128)(2,1)S(1)}, bf16[32,1152]{1,0:T(8,128)(2,1)S(1)}, u32[]{:S(2)}, u32[]{:S(2)}) %collective-permute-start.20) | collective-permute-done | bytes 73760 | tf_op jit(solution)/shard_map/ppermute | solution.py:25
  57.2 0.0 collective-permute-done.18.refs_1_
  57.2 0.1 shard_map.110.refs_0_
  57.3 1.6 %collective-permute-start.24 = (bf16[32,1152]{1,0:T(8,128)(2,1)S(1)}, bf16[32,1152]{1,0:T(8,128)(2,1)S(1)}, u32[]{:S(2)}, u32[]{:S(2)}) collective-permute-start(bf16[32,1152]{1,0:T(8,128)(2,1)S(1)} %shard_map.110.refs_0_), channel_id=1, source_target_pairs={{0,2},{1,3},{2,0},{3,1},{4,6},{5,7},{6,4},{7,5},{8,10},{9,11},{10,... | collective-permute-start | bytes 221192 | tf_op jit(solution)/shard_map/ppermute | solution.py:25
  58.9 2.8 %collective-permute-done.24.refs_2_ = bf16[32,1152]{1,0:T(8,128)(2,1)S(1)} collective-permute-done((bf16[32,1152]{1,0:T(8,128)(2,1)S(1)}, bf16[32,1152]{1,0:T(8,128)(2,1)S(1)}, u32[]{:S(2)}, u32[]{:S(2)}) %collective-permute-start.24) | collective-permute-done | bytes 73760 | tf_op jit(solution)/shard_map/ppermute | solution.py:25
  61.7 1.3 %collective-permute-done.25.refs_3_ = bf16[32,1152]{1,0:T(8,128)(2,1)S(1)} collective-permute-done((bf16[32,1152]{1,0:T(8,128)(2,1)S(1)}, bf16[32,1152]{1,0:T(8,128)(2,1)S(1)}, u32[]{:S(2)}, u32[]{:S(2)}) %collective-permute-start.25) | collective-permute-done | bytes 73760 | tf_op jit(solution)/shard_map/ppermute | solution.py:25
  63.0 1.6 %shard_map.111 = bf16[128,4608]{1,0:T(8,128)(2,1)} custom-call(s32[1]{0:T(128)} %bitcast.tp_at, bf16[128,32]{1,0:T(8,128)(2,1)S(1)} %get-tuple-element.41.picked, bf16[128,4608]{1,0:T(8,128)(2,1)S(1)} %copy-done, f32[32,128]{1,0:T(8,128)S(1)} %shard_map.92.weight, f32[36,128]{1,0:T(8,128)S(1)} %bitcast.11, bf16[32,1152]{1,0:T(8,128)(2,1)S(1)} %shard_map.110.refs_0_, ...), custom_call_target="tpu_custom_call" | custom-call | tf_op jit(solution)/shard_map/pallas_call | solution.py:212
  (34 shorter events, 0.2 us)
Async XLA Ops:
  2.4 7.7 %collective-permute-start = (bf16[32,1152]{1,0:T(8,128)(2,1)S(1)}, bf16[32,1152]{1,0:T(8,128)(2,1)S(1)}, u32[]{:S(2)}, u32[]{:S(2)}) collective-permute-start(bf16[32,1152]{1,0:T(8,128)(2,1)S(1)} %get-tuple-element.42.refs_0_), channel_id=1, source_target_pairs={{0,24},{4,28},{8,16},{12,20},{16,8},{20,12},{24,0},{28,4},{1,25},{... | collective-permute-start | bytes 221192 | tf_op jit(solution)/shard_map/ppermute | solution.py:25
  7.5 4.7 %collective-permute-start.1 = (bf16[32,1152]{1,0:T(8,128)(2,1)S(1)}, bf16[32,1152]{1,0:T(8,128)(2,1)S(1)}, u32[]{:S(2)}, u32[]{:S(2)}) collective-permute-start(bf16[32,1152]{1,0:T(8,128)(2,1)S(1)} %get-tuple-element.42.refs_0_), channel_id=1, source_target_pairs={{0,4},{4,0},{8,12},{12,8},{16,20},{20,16},{24,28},{28,24},{1,5},{5... | collective-permute-start | bytes 221192 | tf_op jit(solution)/shard_map/ppermute | solution.py:25
  9.0 5.7 %collective-permute-start.4 = (bf16[32,1152]{1,0:T(8,128)(2,1)S(1)}, bf16[32,1152]{1,0:T(8,128)(2,1)S(1)}, u32[]{:S(2)}, u32[]{:S(2)}) collective-permute-start(bf16[32,1152]{1,0:T(8,128)(2,1)S(1)} %get-tuple-element.42.refs_0_), channel_id=1, source_target_pairs={{0,16},{4,20},{8,24},{12,28},{16,0},{20,4},{24,8},{28,12},{1,17},{... | collective-permute-start | bytes 221192 | tf_op jit(solution)/shard_map/ppermute | solution.py:25
  9.0 6.3 %collective-permute-start.2 = (bf16[32,1152]{1,0:T(8,128)(2,1)S(1)}, bf16[32,1152]{1,0:T(8,128)(2,1)S(1)}, u32[]{:S(2)}, u32[]{:S(2)}) collective-permute-start(bf16[32,1152]{1,0:T(8,128)(2,1)S(1)} %get-tuple-element.42.refs_0_), channel_id=1, source_target_pairs={{0,8},{4,12},{8,0},{12,4},{16,24},{20,28},{24,16},{28,20},{1,9},{5... | collective-permute-start | bytes 221192 | tf_op jit(solution)/shard_map/ppermute | solution.py:25
  9.8 12.0 %slice-start = ((s8[10616832]{0:T(1024)(128)(4,1)}), s8[4194304]{0:T(1024)(128)(4,1)S(1)}, s32[]{:S(2)}) async-start(s8[10616832]{0:T(1024)(128)(4,1)} %bitcast.5), calls=%async_computation | async-start | bytes 8388608
  9.8 12.0 %slice-start.3 = ((s8[10616832]{0:T(1024)(128)(4,1)}), s8[4194304]{0:T(1024)(128)(4,1)S(1)}, s32[]{:S(2)}) async-start(s8[10616832]{0:T(1024)(128)(4,1)} %bitcast.7), calls=%async_computation.3 | async-start | bytes 8388608
  9.8 12.0 %slice-start.6 = ((s8[10616832]{0:T(1024)(128)(4,1)}), s8[4194304]{0:T(1024)(128)(4,1)S(1)}, s32[]{:S(2)}) async-start(s8[10616832]{0:T(1024)(128)(4,1)} %bitcast.9), calls=%async_computation.6 | async-start | bytes 8388608
  9.8 12.0 %slice-start.1 = ((s8[10616832]{0:T(1024)(128)(4,1)}), s8[4194304]{0:T(1024)(128)(4,1)S(1)}, s32[]{:S(2)}) async-start(s8[10616832]{0:T(1024)(128)(4,1)} %bitcast.5), calls=%async_computation.1 | async-start | bytes 8388608
  9.8 12.0 %slice-start.2 = ((s8[10616832]{0:T(1024)(128)(4,1)}), s8[2228224]{0:T(1024)(128)(4,1)S(1)}, s32[]{:S(2)}) async-start(s8[10616832]{0:T(1024)(128)(4,1)} %bitcast.5), calls=%async_computation.2 | async-start | bytes 4456448
  9.9 12.0 %slice-start.4 = ((s8[10616832]{0:T(1024)(128)(4,1)}), s8[4194304]{0:T(1024)(128)(4,1)S(1)}, s32[]{:S(2)}) async-start(s8[10616832]{0:T(1024)(128)(4,1)} %bitcast.7), calls=%async_computation.4 | async-start | bytes 8388608
  9.9 12.0 %slice-start.5 = ((s8[10616832]{0:T(1024)(128)(4,1)}), s8[2228224]{0:T(1024)(128)(4,1)S(1)}, s32[]{:S(2)}) async-start(s8[10616832]{0:T(1024)(128)(4,1)} %bitcast.7), calls=%async_computation.5 | async-start | bytes 4456448
  9.9 12.0 %slice-start.7 = ((s8[10616832]{0:T(1024)(128)(4,1)}), s8[4194304]{0:T(1024)(128)(4,1)S(1)}, s32[]{:S(2)}) async-start(s8[10616832]{0:T(1024)(128)(4,1)} %bitcast.9), calls=%async_computation.7 | async-start | bytes 8388608
  9.9 12.0 %slice-start.8 = ((s8[10616832]{0:T(1024)(128)(4,1)}), s8[2228224]{0:T(1024)(128)(4,1)S(1)}, s32[]{:S(2)}) async-start(s8[10616832]{0:T(1024)(128)(4,1)} %bitcast.9), calls=%async_computation.8 | async-start | bytes 4456448
  10.1 5.2 %collective-permute-start.6 = (bf16[32,1152]{1,0:T(8,128)(2,1)S(1)}, bf16[32,1152]{1,0:T(8,128)(2,1)S(1)}, u32[]{:S(2)}, u32[]{:S(2)}) collective-permute-start(bf16[32,1152]{1,0:T(8,128)(2,1)S(1)} %collective-permute-done.refs_6_), channel_id=1, source_target_pairs={{0,4},{4,0},{8,12},{12,8},{16,20},{20,16},{24,28},{28,24},{1,5},{5... | collective-permute-start | bytes 221192 | tf_op jit(solution)/shard_map/ppermute | solution.py:25
  12.2 4.8 %collective-permute-start.3 = (bf16[32,1152]{1,0:T(8,128)(2,1)S(1)}, bf16[32,1152]{1,0:T(8,128)(2,1)S(1)}, u32[]{:S(2)}, u32[]{:S(2)}) collective-permute-start(bf16[32,1152]{1,0:T(8,128)(2,1)S(1)} %collective-permute-done.1.refs_1_), channel_id=1, source_target_pairs={{0,8},{4,12},{8,0},{12,4},{16,24},{20,28},{24,16},{28,20},{1,9},{5... | collective-permute-start | bytes 221192 | tf_op jit(solution)/shard_map/ppermute | solution.py:25
  14.7 4.4 %collective-permute-start.5 = (bf16[32,1152]{1,0:T(8,128)(2,1)S(1)}, bf16[32,1152]{1,0:T(8,128)(2,1)S(1)}, u32[]{:S(2)}, u32[]{:S(2)}) collective-permute-start(bf16[32,1152]{1,0:T(8,128)(2,1)S(1)} %collective-permute-done.4.refs_4_), channel_id=1, source_target_pairs={{0,4},{4,0},{8,12},{12,8},{16,20},{20,16},{24,28},{28,24},{1,5},{5... | collective-permute-start | bytes 221192 | tf_op jit(solution)/shard_map/ppermute | solution.py:25
  19.6 2.2 %collective-permute-start.9 = (bf16[128,1152]{1,0:T(8,128)(2,1)S(1)}, bf16[128,1152]{1,0:T(8,128)(2,1)S(1)}, u32[]{:S(2)}, u32[]{:S(2)}) collective-permute-start(bf16[128,1152]{1,0:T(8,128)(2,1)S(1)} %get-tuple-element.49.first), channel_id=1, source_target_pairs={{0,1},{1,0},{2,3},{3,2},{4,5},{5,4},{6,7},{7,6},{8,9},{9,8},{10,11... | collective-permute-start | bytes 884744 | tf_op jit(solution)/shard_map/ppermute | solution.py:25
  19.7 7.1 %collective-permute-start.8 = (bf16[128,640]{1,0:T(8,128)(2,1)S(1)}, bf16[128,640]{1,0:T(8,128)(2,1)S(1)}, u32[]{:S(2)}, u32[]{:S(2)}) collective-permute-start(bf16[128,640]{1,0:T(8,128)(2,1)S(1)} %get-tuple-element.48), channel_id=1, source_target_pairs={{0,2},{1,3},{2,0},{3,1},{4,6},{5,7},{6,4},{7,5},{8,10},{9,11},{10,... | collective-permute-start | bytes 491528 | tf_op jit(solution)/shard_map/ppermute | solution.py:25
  21.3 7.8 %collective-permute-start.7 = (bf16[128,512]{1,0:T(8,128)(2,1)S(1)}, bf16[128,512]{1,0:T(8,128)(2,1)S(1)}, u32[]{:S(2)}, u32[]{:S(2)}) collective-permute-start(bf16[128,512]{1,0:T(8,128)(2,1)S(1)} %get-tuple-element.47), channel_id=1, source_target_pairs={{0,2},{1,3},{2,0},{3,1},{4,6},{5,7},{6,4},{7,5},{8,10},{9,11},{10,... | collective-permute-start | bytes 393224 | tf_op jit(solution)/shard_map/ppermute | solution.py:25
  26.9 2.3 %collective-permute-start.11 = (bf16[128,640]{1,0:T(8,128)(2,1)S(1)}, bf16[128,640]{1,0:T(8,128)(2,1)S(1)}, u32[]{:S(2)}, u32[]{:S(2)}) collective-permute-start(bf16[128,640]{1,0:T(8,128)(2,1)S(1)} %collective-permute-done.8.refs_0_), channel_id=1, source_target_pairs={{0,1},{1,0},{2,3},{3,2},{4,5},{5,4},{6,7},{7,6},{8,9},{9,8},{10,11... | collective-permute-start | bytes 491528 | tf_op jit(solution)/shard_map/ppermute | solution.py:25
  29.1 1.3 %collective-permute-start.10 = (bf16[128,512]{1,0:T(8,128)(2,1)S(1)}, bf16[128,512]{1,0:T(8,128)(2,1)S(1)}, u32[]{:S(2)}, u32[]{:S(2)}) collective-permute-start(bf16[128,512]{1,0:T(8,128)(2,1)S(1)} %collective-permute-done.7.refs_1_), channel_id=1, source_target_pairs={{0,1},{1,0},{2,3},{3,2},{4,5},{5,4},{6,7},{7,6},{8,9},{9,8},{10,11... | collective-permute-start | bytes 393224 | tf_op jit(solution)/shard_map/ppermute | solution.py:25
  31.5 2.3 %collective-permute-start.13 = (bf16[128,640]{1,0:T(8,128)(2,1)S(1)}, bf16[128,640]{1,0:T(8,128)(2,1)S(1)}, u32[]{:S(2)}, u32[]{:S(2)}) collective-permute-start(bf16[128,640]{1,0:T(8,128)(2,1)S(1)} %shard_map.100), channel_id=1, source_target_pairs={{0,1},{1,0},{2,3},{3,2},{4,5},{5,4},{6,7},{7,6},{8,9},{9,8},{10,11... | collective-permute-start | bytes 491528 | tf_op jit(solution)/shard_map/ppermute | solution.py:25
  32.4 4.0 %collective-permute-start.12 = (bf16[128,1152]{1,0:T(8,128)(2,1)S(1)}, bf16[128,1152]{1,0:T(8,128)(2,1)S(1)}, u32[]{:S(2)}, u32[]{:S(2)}) collective-permute-start(bf16[128,1152]{1,0:T(8,128)(2,1)S(1)} %shard_map.98), channel_id=1, source_target_pairs={{0,1},{1,0},{2,3},{3,2},{4,5},{5,4},{6,7},{7,6},{8,9},{9,8},{10,11... | collective-permute-start | bytes 884744 | tf_op jit(solution)/shard_map/ppermute | solution.py:25
  33.1 2.7 %collective-permute-start.15 = (bf16[128,512]{1,0:T(8,128)(2,1)S(1)}, bf16[128,512]{1,0:T(8,128)(2,1)S(1)}, u32[]{:S(2)}, u32[]{:S(2)}) collective-permute-start(bf16[128,512]{1,0:T(8,128)(2,1)S(1)} %shard_map.103), channel_id=1, source_target_pairs={{0,1},{1,0},{2,3},{3,2},{4,5},{5,4},{6,7},{7,6},{8,9},{9,8},{10,11... | collective-permute-start | bytes 393224 | tf_op jit(solution)/shard_map/ppermute | solution.py:25
  33.8 29.1 %copy-start = (bf16[128,4608]{1,0:T(8,128)(2,1)S(1)}, bf16[128,4608]{1,0:T(8,128)(2,1)}, u32[]{:S(2)}) copy-start(bf16[128,4608]{1,0:T(8,128)(2,1)} %tokens.3) | copy-start | bytes 3538948
  33.8 29.1 %copy-start.1 = (f32[4608]{0:T(1024)S(1)}, f32[4608]{0:T(1024)}, u32[]{:S(2)}) copy-start(f32[4608]{0:T(1024)} %param.14) | copy-start | bytes 55300
  33.9 9.3 %collective-permute-start.14 = (bf16[128,640]{1,0:T(8,128)(2,1)S(1)}, bf16[128,640]{1,0:T(8,128)(2,1)S(1)}, u32[]{:S(2)}, u32[]{:S(2)}) collective-permute-start(bf16[128,640]{1,0:T(8,128)(2,1)S(1)} %shard_map.102), channel_id=1, source_target_pairs={{0,2},{1,3},{2,0},{3,1},{4,6},{5,7},{6,4},{7,5},{8,10},{9,11},{10,... | collective-permute-start | bytes 491528 | tf_op jit(solution)/shard_map/ppermute | solution.py:25
  35.9 7.3 %collective-permute-start.16 = (bf16[128,512]{1,0:T(8,128)(2,1)S(1)}, bf16[128,512]{1,0:T(8,128)(2,1)S(1)}, u32[]{:S(2)}, u32[]{:S(2)}) collective-permute-start(bf16[128,512]{1,0:T(8,128)(2,1)S(1)} %shard_map.105), channel_id=1, source_target_pairs={{0,2},{1,3},{2,0},{3,1},{4,6},{5,7},{6,4},{7,5},{8,10},{9,11},{10,... | collective-permute-start | bytes 393224 | tf_op jit(solution)/shard_map/ppermute | solution.py:25
  43.6 9.0 %collective-permute-start.17 = (bf16[64,1152]{1,0:T(8,128)(2,1)S(1)}, bf16[64,1152]{1,0:T(8,128)(2,1)S(1)}, u32[]{:S(2)}, u32[]{:S(2)}) collective-permute-start(bf16[64,1152]{1,0:T(8,128)(2,1)S(1)} %get-tuple-element.70), channel_id=1, source_target_pairs={{0,8},{4,12},{8,0},{12,4},{16,24},{20,28},{24,16},{28,20},{1,9},{5... | collective-permute-start | bytes 442376 | tf_op jit(solution)/shard_map/ppermute | solution.py:25
  43.7 4.4 %collective-permute-start.21 = (bf16[32,1152]{1,0:T(8,128)(2,1)S(1)}, bf16[32,1152]{1,0:T(8,128)(2,1)S(1)}, u32[]{:S(2)}, u32[]{:S(2)}) collective-permute-start(bf16[32,1152]{1,0:T(8,128)(2,1)S(1)} %get-tuple-element.76), channel_id=1, source_target_pairs={{0,4},{4,0},{8,12},{12,8},{16,20},{20,16},{24,28},{28,24},{1,5},{5... | collective-permute-start | bytes 221192 | tf_op jit(solution)/shard_map/ppermute | solution.py:25
  44.8 6.2 %collective-permute-start.19 = (bf16[32,1152]{1,0:T(8,128)(2,1)S(1)}, bf16[32,1152]{1,0:T(8,128)(2,1)S(1)}, u32[]{:S(2)}, u32[]{:S(2)}) collective-permute-start(bf16[32,1152]{1,0:T(8,128)(2,1)S(1)} %get-tuple-element.74), channel_id=1, source_target_pairs={{0,4},{4,0},{8,12},{12,8},{16,20},{20,16},{24,28},{28,24},{1,5},{5... | collective-permute-start | bytes 221192 | tf_op jit(solution)/shard_map/ppermute | solution.py:25
  48.2 7.1 %collective-permute-start.22 = (bf16[32,1152]{1,0:T(8,128)(2,1)S(1)}, bf16[32,1152]{1,0:T(8,128)(2,1)S(1)}, u32[]{:S(2)}, u32[]{:S(2)}) collective-permute-start(bf16[32,1152]{1,0:T(8,128)(2,1)S(1)} %shard_map.109), channel_id=1, source_target_pairs={{0,16},{4,20},{8,24},{12,28},{16,0},{20,4},{24,8},{28,12},{1,17},{... | collective-permute-start | bytes 221192 | tf_op jit(solution)/shard_map/ppermute | solution.py:25
  51.0 6.2 %collective-permute-start.20 = (bf16[32,1152]{1,0:T(8,128)(2,1)S(1)}, bf16[32,1152]{1,0:T(8,128)(2,1)S(1)}, u32[]{:S(2)}, u32[]{:S(2)}) collective-permute-start(bf16[32,1152]{1,0:T(8,128)(2,1)S(1)} %shard_map.108), channel_id=1, source_target_pairs={{0,24},{4,28},{8,16},{12,20},{16,8},{20,12},{24,0},{28,4},{1,25},{... | collective-permute-start | bytes 221192 | tf_op jit(solution)/shard_map/ppermute | solution.py:25
  52.6 4.6 %collective-permute-start.18 = (bf16[32,1152]{1,0:T(8,128)(2,1)S(1)}, bf16[32,1152]{1,0:T(8,128)(2,1)S(1)}, u32[]{:S(2)}, u32[]{:S(2)}) collective-permute-start(bf16[32,1152]{1,0:T(8,128)(2,1)S(1)} %shard_map.107), channel_id=1, source_target_pairs={{0,4},{4,0},{8,12},{12,8},{16,20},{20,16},{24,28},{28,24},{1,5},{5... | collective-permute-start | bytes 221192 | tf_op jit(solution)/shard_map/ppermute | solution.py:25
  57.3 4.4 %collective-permute-start.24 = (bf16[32,1152]{1,0:T(8,128)(2,1)S(1)}, bf16[32,1152]{1,0:T(8,128)(2,1)S(1)}, u32[]{:S(2)}, u32[]{:S(2)}) collective-permute-start(bf16[32,1152]{1,0:T(8,128)(2,1)S(1)} %shard_map.110.refs_0_), channel_id=1, source_target_pairs={{0,2},{1,3},{2,0},{3,1},{4,6},{5,7},{6,4},{7,5},{8,10},{9,11},{10,... | collective-permute-start | bytes 221192 | tf_op jit(solution)/shard_map/ppermute | solution.py:25
  58.9 2.9 %collective-permute-start.23 = (bf16[32,1152]{1,0:T(8,128)(2,1)S(1)}, bf16[32,1152]{1,0:T(8,128)(2,1)S(1)}, u32[]{:S(2)}, u32[]{:S(2)}) collective-permute-start(bf16[32,1152]{1,0:T(8,128)(2,1)S(1)} %shard_map.110.refs_0_), channel_id=1, source_target_pairs={{0,1},{1,0},{2,3},{3,2},{4,5},{5,4},{6,7},{7,6},{8,9},{9,8},{10,11... | collective-permute-start | bytes 221192 | tf_op jit(solution)/shard_map/ppermute | solution.py:25
  61.7 1.3 %collective-permute-start.25 = (bf16[32,1152]{1,0:T(8,128)(2,1)S(1)}, bf16[32,1152]{1,0:T(8,128)(2,1)S(1)}, u32[]{:S(2)}, u32[]{:S(2)}) collective-permute-start(bf16[32,1152]{1,0:T(8,128)(2,1)S(1)} %collective-permute-done.24.refs_2_), channel_id=1, source_target_pairs={{0,1},{1,0},{2,3},{3,2},{4,5},{5,4},{6,7},{7,6},{8,9},{9,8},{10,11... | collective-permute-start | bytes 221192 | tf_op jit(solution)/shard_map/ppermute | solution.py:25

commit v4 on v3

--- a/solution.py
+++ b/solution.py
@@ -16,7 +16,6 @@
 SMEM = pl.BlockSpec(memory_space=pltpu.SMEM)
 HBM = pl.BlockSpec(memory_space=pltpu.HBM)
 CHUNKS = 1
-OUT_CHUNKS = 4
 TP = 4
 
 
@@ -103,13 +102,16 @@
     held = jnp.concatenate([ref[...] for ref in pieces], 0)
     count = held.shape[0]
     live = held[:, :LANES].astype(F32) < DEAD / 2
-    live_bf16 = jnp.where(live, 1.0, 0.0).astype(BF16)
-    block = min(count, 2 * LANES)
+    amount = jnp.where(live, 1, 0)
+    sizes = [
+        jnp.sum(amount[k * capacity : (k + 1) * capacity, :], axis=0, keepdims=True) for k in range(len(pieces))
+    ]
     firsts = []
-    for top in range(0, count, block):
-        shard = seq_at[0] ^ ((iota((block, count), 0) + top) // capacity)
-        before = (seq_at[0] ^ (iota((block, count), 1) // capacity)) < shard
-        firsts.append(dot_f32(jnp.where(before, 1.0, 0.0).astype(BF16), live_bf16).astype(jnp.int32))
+    for k in range(len(pieces)):
+        first = jnp.zeros((1, LANES), jnp.int32)
+        for j in range(len(pieces)):
+            first = first + jnp.where((seq_at[0] ^ j) < (seq_at[0] ^ k), sizes[j], 0)
+        firsts.append(jnp.broadcast_to(first, (capacity, LANES)))
     first = jnp.concatenate(firsts, 0)
     target = first + (iota((count, LANES), 0) % capacity)
     for part in range(places.shape[1] // LANES):
@@ -161,12 +163,11 @@
 
 def window_kernel(near, first, second, places, *windows):
     total = near[...] + jnp.concatenate([first[...], second[...]], 1).astype(F32)
-    total = total.astype(BF16)
-    first = 0
+    picked = dot_f32(places[...], total.astype(BF16)).astype(BF16)
+    start = 0
     for window in windows:
-        count = window.shape[0]
-        window[...] = dot_f32(places[first : first + count, :], total).astype(BF16)
-        first += count
+        window[...] = picked[start : start + window.shape[0], :]
+        start += window.shape[0]
 
 
 def add_up(values, refs):
@@ -189,20 +190,21 @@
 
 
 def finish_rows_kernel(tp_at, picked, tokens, weight, gain, *refs):
-    parts, (out, joined, staged, sems) = refs[:-4], refs[-4:]
-    width = tokens.shape[1]
-    piece = width // len(parts)
-    for far, part in enumerate(parts):
-        joined[:, pl.ds(pl.multiple_of((tp_at[0] ^ far) * piece, LANES), piece)] = part[...].astype(F32)
-    values = joined[...]
-    scale = lax.rsqrt(jnp.mean(values * values, axis=1, keepdims=True) + EPS) * weight[:, :1]
+    parts, (out, staged, sems) = refs[:-3], refs[-3:]
+    wide = parts[0].shape[1]
+    tiles = wide // LANES
+    values = [part[...].astype(F32) for part in parts]
+    square = sum(jnp.sum(value * value, axis=1, keepdims=True) for value in values)
+    scale = lax.rsqrt(square / tokens.shape[1] + EPS) * weight[:, :1]
     hot = picked[...]
-    rows = gain.shape[0] // OUT_CHUNKS
     copies = []
-    for part, at in chunks(width, OUT_CHUNKS):
-        update = scaled(values[:, at] * scale, gain[part * rows : (part + 1) * rows, :]).astype(BF16)
+    for far, value in enumerate(values):
+        place = (tp_at[0] ^ far) * tiles
+        at = pl.ds(pl.multiple_of(place * LANES, LANES), wide)
+        gains = jnp.concatenate([gain[pl.ds(place + i, 1), :] for i in range(tiles)], 1)
+        update = (value * scale * gains).astype(BF16)
         staged[:, at] = (tokens[:, at].astype(F32) + dot_f32(hot, update)).astype(BF16)
-        copies.append(pltpu.make_async_copy(staged.at[:, at], out.at[:, at], sems.at[part]))
+        copies.append(pltpu.make_async_copy(staged.at[:, at], out.at[:, at], sems.at[far]))
         copies[-1].start()
     for copy in copies:
         copy.wait()
@@ -336,11 +338,7 @@
         array(tok_rows, width),
         (tp_at,),
         (picked, tokens, weight, post_gain.reshape(-1, LANES), final, other_near, other_far, last),
-        scratch=(
-            pltpu.VMEM((capacity, width), F32),
-            pltpu.VMEM(tokens.shape, BF16),
-            pltpu.SemaphoreType.DMA((OUT_CHUNKS,)),
-        ),
+        scratch=(pltpu.VMEM(tokens.shape, BF16), pltpu.SemaphoreType.DMA((TP,))),
         out_spec=HBM,
     )
 

time: 64.7 us -> 64.4 us (level)
  no operation moved by 1% of the time
where the time goes in v4:
time: 64.4 us; the launch traced here: 64.2 us
  starting transfers between devices  26.5 us (41%)
  waiting for transfers between devices  25.6 us (40%)
  Pallas kernels  11.2 us (17%)
  between operations  0.96 us (1%)
    ppermute x26, starting transfers between devices, swap(): return lax.ppermute(value, axis, [(i, i ^ bits) for i in range(size)])  26.5 us
    ppermute x26, waiting for transfers between devices, swap(): return lax.ppermute(value, axis, [(i, i ^ bits) for i in range(size)])  25.6 us
    pallas_call x21, Pallas kernels, call(): pl.pallas_call(kernel, out_shape=shapes, in_specs=[SMEM] * len(scalars) +...  11.2 us
  transfers between devices with their start and end apart: 26, of which 13 were waited for; matrix products, arithmetic and copies ran while one was open for 0% of the time, Pallas kernels for 10%

profile of v4, /device:TPU:0, one launch (start us, length us, event | category | flops | bytes accessed | tf_op | source)
XLA Modules:
  0.0 64.2 jit_solution(16489557447502066708)
XLA Ops:
  0.7 1.7 %shard_map.91 = (bf16[32,1152]{1,0:T(8,128)(2,1)S(1)}, bf16[32,4608]{1,0:T(8,128)(2,1)S(1)}, bf16[128,32]{1,0:T(8,128)(2,1)S(1)}, f32[36,128]{1,0:T(8,128)S(1)}) custom-call(s32[1]{0:T(128)S(6)} %copy.10.counts, s32[1]{0:T(128)} %bitcast.tp_at, s32[1]{0:T(128)} %bitcast.1.seq_at, s32[1,32]{1,0:T(1,128)} %chosen.1, bf16[128,4608]{1,0:T(8,128)(2,1)} %tokens.3, ...), custom_call_target="tpu_custom_call" | custom-call | tf_op jit(solution)/shard_map/pallas_call | solution.py:214
  2.4 5.1 %collective-permute-start = (bf16[32,1152]{1,0:T(8,128)(2,1)S(1)}, bf16[32,1152]{1,0:T(8,128)(2,1)S(1)}, u32[]{:S(2)}, u32[]{:S(2)}) collective-permute-start(bf16[32,1152]{1,0:T(8,128)(2,1)S(1)} %get-tuple-element.42.refs_0_), channel_id=1, source_target_pairs={{0,24},{4,28},{8,16},{12,20},{16,8},{20,12},{24,0},{28,4},{1,25},{... | collective-permute-start | bytes 221192 | tf_op jit(solution)/shard_map/ppermute | solution.py:24
  7.5 1.5 %collective-permute-start.1 = (bf16[32,1152]{1,0:T(8,128)(2,1)S(1)}, bf16[32,1152]{1,0:T(8,128)(2,1)S(1)}, u32[]{:S(2)}, u32[]{:S(2)}) collective-permute-start(bf16[32,1152]{1,0:T(8,128)(2,1)S(1)} %get-tuple-element.42.refs_0_), channel_id=1, source_target_pairs={{0,4},{4,0},{8,12},{12,8},{16,20},{20,16},{24,28},{28,24},{1,5},{5... | collective-permute-start | bytes 221192 | tf_op jit(solution)/shard_map/ppermute | solution.py:24
  9.0 0.0 collective-permute-start.4
  9.0 0.8 %collective-permute-start.2 = (bf16[32,1152]{1,0:T(8,128)(2,1)S(1)}, bf16[32,1152]{1,0:T(8,128)(2,1)S(1)}, u32[]{:S(2)}, u32[]{:S(2)}) collective-permute-start(bf16[32,1152]{1,0:T(8,128)(2,1)S(1)} %get-tuple-element.42.refs_0_), channel_id=1, source_target_pairs={{0,8},{4,12},{8,0},{12,4},{16,24},{20,28},{24,16},{28,20},{1,9},{5... | collective-permute-start | bytes 221192 | tf_op jit(solution)/shard_map/ppermute | solution.py:24
  9.8 0.0 slice-start.2
  9.9 0.0 slice-start.5
  9.9 0.0 slice-start.7
  9.9 0.1 shard_map.92.weight
  10.0 0.1 collective-permute-done.refs_6_
  10.1 1.7 %collective-permute-start.6 = (bf16[32,1152]{1,0:T(8,128)(2,1)S(1)}, bf16[32,1152]{1,0:T(8,128)(2,1)S(1)}, u32[]{:S(2)}, u32[]{:S(2)}) collective-permute-start(bf16[32,1152]{1,0:T(8,128)(2,1)S(1)} %collective-permute-done.refs_6_), channel_id=1, source_target_pairs={{0,4},{4,0},{8,12},{12,8},{16,20},{20,16},{24,28},{28,24},{1,5},{5... | collective-permute-start | bytes 221192 | tf_op jit(solution)/shard_map/ppermute | solution.py:24
  11.9 0.4 collective-permute-done.1.refs_1_
  12.2 2.5 %collective-permute-start.3 = (bf16[32,1152]{1,0:T(8,128)(2,1)S(1)}, bf16[32,1152]{1,0:T(8,128)(2,1)S(1)}, u32[]{:S(2)}, u32[]{:S(2)}) collective-permute-start(bf16[32,1152]{1,0:T(8,128)(2,1)S(1)} %collective-permute-done.1.refs_1_), channel_id=1, source_target_pairs={{0,8},{4,12},{8,0},{12,4},{16,24},{20,28},{24,16},{28,20},{1,9},{5... | collective-permute-start | bytes 221192 | tf_op jit(solution)/shard_map/ppermute | solution.py:24
  14.7 0.0 collective-permute-done.4.refs_4_
  14.7 0.6 collective-permute-start.5
  15.3 1.7 %collective-permute-done.3.refs_3_ = bf16[32,1152]{1,0:T(8,128)(2,1)S(1)} collective-permute-done((bf16[32,1152]{1,0:T(8,128)(2,1)S(1)}, bf16[32,1152]{1,0:T(8,128)(2,1)S(1)}, u32[]{:S(2)}, u32[]{:S(2)}) %collective-permute-start.3) | collective-permute-done | bytes 73760 | tf_op jit(solution)/shard_map/ppermute | solution.py:24
  17.1 2.0 %collective-permute-done.5.refs_5_ = bf16[32,1152]{1,0:T(8,128)(2,1)S(1)} collective-permute-done((bf16[32,1152]{1,0:T(8,128)(2,1)S(1)}, bf16[32,1152]{1,0:T(8,128)(2,1)S(1)}, u32[]{:S(2)}, u32[]{:S(2)}) %collective-permute-start.5) | collective-permute-done | bytes 73760 | tf_op jit(solution)/shard_map/ppermute | solution.py:24
  19.1 0.4 shard_map.93
  19.5 0.1 collective-permute-start.9
  19.6 1.6 %collective-permute-start.8 = (bf16[128,640]{1,0:T(8,128)(2,1)S(1)}, bf16[128,640]{1,0:T(8,128)(2,1)S(1)}, u32[]{:S(2)}, u32[]{:S(2)}) collective-permute-start(bf16[128,640]{1,0:T(8,128)(2,1)S(1)} %get-tuple-element.48), channel_id=1, source_target_pairs={{0,2},{1,3},{2,0},{3,1},{4,6},{5,7},{6,4},{7,5},{8,10},{9,11},{10,... | collective-permute-start | bytes 491528 | tf_op jit(solution)/shard_map/ppermute | solution.py:24
  21.2 0.5 collective-permute-start.7
  21.7 0.0 collective-permute-done.9.second
  21.8 1.9 %shard_map.94 = (f32[128,1152]{1,0:T(8,128)S(1)}, f32[128,1152]{1,0:T(8,128)S(1)}) custom-call(s32[1]{0:T(128)} %bitcast.tp_at, bf16[128,1152]{1,0:T(8,128)(2,1)S(1)} %get-tuple-element.49.first, bf16[128,1152]{1,0:T(8,128)(2,1)S(1)} %collective-permute-done.9.second, bf16[4608,1152]{1,0:T(8,128)(2,1)S(1)} %bitcast.8, bf16[4608,1152]{1,0:T(8,128)(2,1)S(1)} %bitcast.10, ...), custom_call_target="tpu_custom_call" | custom-call | flops 1358954496 | tf_op jit(solution)/shard_map/pallas_call | solution.py:214
  23.6 3.1 %collective-permute-done.8.refs_0_ = bf16[128,640]{1,0:T(8,128)(2,1)S(1)} collective-permute-done((bf16[128,640]{1,0:T(8,128)(2,1)S(1)}, bf16[128,640]{1,0:T(8,128)(2,1)S(1)}, u32[]{:S(2)}, u32[]{:S(2)}) %collective-permute-start.8) | collective-permute-done | bytes 163872 | tf_op jit(solution)/shard_map/ppermute | solution.py:24
  26.7 0.0 collective-permute-start.11
  26.7 0.7 %shard_map.95 = (f32[128,1152]{1,0:T(8,128)S(1)}, f32[128,1152]{1,0:T(8,128)S(1)}) custom-call(s32[1]{0:T(128)} %bitcast.tp_at, bf16[128,640]{1,0:T(8,128)(2,1)S(1)} %collective-permute-done.8.refs_0_, f32[128,1152]{1,0:T(8,128)S(1)} %get-tuple-element.53.refs_1_, f32[128,1152]{1,0:T(8,128)S(1)} %get-tuple-element.54.refs_2_, ...), custom_call_target="tpu_custom_call" | custom-call | flops 339738624 | tf_op jit(solution)/shard_map/pallas_call | solution.py:214
  27.4 1.6 %collective-permute-done.7.refs_1_ = bf16[128,512]{1,0:T(8,128)(2,1)S(1)} collective-permute-done((bf16[128,512]{1,0:T(8,128)(2,1)S(1)}, bf16[128,512]{1,0:T(8,128)(2,1)S(1)}, u32[]{:S(2)}, u32[]{:S(2)}) %collective-permute-start.7) | collective-permute-done | bytes 131104 | tf_op jit(solution)/shard_map/ppermute | solution.py:24
  29.0 0.0 collective-permute-start.10
  29.0 0.0 collective-permute-done.11.refs_0_
  29.0 1.0 %shard_map.96 = (f32[128,1152]{1,0:T(8,128)S(1)}, f32[128,1152]{1,0:T(8,128)S(1)}) custom-call(s32[1]{0:T(128)} %bitcast.tp_at, bf16[128,640]{1,0:T(8,128)(2,1)S(1)} %collective-permute-done.11.refs_0_, bf16[128,512]{1,0:T(8,128)(2,1)S(1)} %collective-permute-done.7.refs_1_, f32[128,1152]{1,0:T(8,128)S(1)} %get-tuple-element.58.refs_2_, ...), custom_call_target="tpu_custom_call" | custom-call | flops 339738624 | tf_op jit(solution)/shard_map/pallas_call | solution.py:214
  30.0 0.3 collective-permute-done.10.rows
  30.3 0.6 shard_map.97.hidden
  30.9 0.4 shard_map.100
  31.3 0.3 collective-permute-start.13
  31.6 0.6 shard_map.98
  32.2 0.4 collective-permute-start.12
  32.6 0.3 shard_map.103
  32.9 0.3 collective-permute-start.15
  33.2 0.4 shard_map.101.first
  33.7 0.0 copy-start
  33.7 0.0 copy-start.1
  33.7 1.6 %collective-permute-start.14 = (bf16[128,640]{1,0:T(8,128)(2,1)S(1)}, bf16[128,640]{1,0:T(8,128)(2,1)S(1)}, u32[]{:S(2)}, u32[]{:S(2)}) collective-permute-start(bf16[128,640]{1,0:T(8,128)(2,1)S(1)} %shard_map.102), channel_id=1, source_target_pairs={{0,2},{1,3},{2,0},{3,1},{4,6},{5,7},{6,4},{7,5},{8,10},{9,11},{10,... | collective-permute-start | bytes 491528 | tf_op jit(solution)/shard_map/ppermute | solution.py:24
  35.3 0.3 shard_map.104.first
  35.7 0.6 collective-permute-start.16
  36.3 0.6 shard_map.99.near
  36.9 6.1 %collective-permute-done.16.second = bf16[128,512]{1,0:T(8,128)(2,1)S(1)} collective-permute-done((bf16[128,512]{1,0:T(8,128)(2,1)S(1)}, bf16[128,512]{1,0:T(8,128)(2,1)S(1)}, u32[]{:S(2)}, u32[]{:S(2)}) %collective-permute-start.16) | collective-permute-done | bytes 131104 | tf_op jit(solution)/shard_map/ppermute | solution.py:24
  43.0 0.3 shard_map.106
  43.3 0.1 collective-permute-start.17
  43.5 1.0 %collective-permute-start.21 = (bf16[32,1152]{1,0:T(8,128)(2,1)S(1)}, bf16[32,1152]{1,0:T(8,128)(2,1)S(1)}, u32[]{:S(2)}, u32[]{:S(2)}) collective-permute-start(bf16[32,1152]{1,0:T(8,128)(2,1)S(1)} %get-tuple-element.76), channel_id=1, source_target_pairs={{0,4},{4,0},{8,12},{12,8},{16,20},{20,16},{24,28},{28,24},{1,5},{5... | collective-permute-start | bytes 221192 | tf_op jit(solution)/shard_map/ppermute | solution.py:24
  44.5 1.0 %collective-permute-start.19 = (bf16[32,1152]{1,0:T(8,128)(2,1)S(1)}, bf16[32,1152]{1,0:T(8,128)(2,1)S(1)}, u32[]{:S(2)}, u32[]{:S(2)}) collective-permute-start(bf16[32,1152]{1,0:T(8,128)(2,1)S(1)} %get-tuple-element.74), channel_id=1, source_target_pairs={{0,4},{4,0},{8,12},{12,8},{16,20},{20,16},{24,28},{28,24},{1,5},{5... | collective-permute-start | bytes 221192 | tf_op jit(solution)/shard_map/ppermute | solution.py:24
  45.5 2.4 %collective-permute-done.21.refs_0_ = bf16[32,1152]{1,0:T(8,128)(2,1)S(1)} collective-permute-done((bf16[32,1152]{1,0:T(8,128)(2,1)S(1)}, bf16[32,1152]{1,0:T(8,128)(2,1)S(1)}, u32[]{:S(2)}, u32[]{:S(2)}) %collective-permute-start.21) | collective-permute-done | bytes 73760 | tf_op jit(solution)/shard_map/ppermute | solution.py:24
  47.9 2.8 %collective-permute-start.22 = (bf16[32,1152]{1,0:T(8,128)(2,1)S(1)}, bf16[32,1152]{1,0:T(8,128)(2,1)S(1)}, u32[]{:S(2)}, u32[]{:S(2)}) collective-permute-start(bf16[32,1152]{1,0:T(8,128)(2,1)S(1)} %shard_map.109), channel_id=1, source_target_pairs={{0,16},{4,20},{8,24},{12,28},{16,0},{20,4},{24,8},{28,12},{1,17},{... | collective-permute-start | bytes 221192 | tf_op jit(solution)/shard_map/ppermute | solution.py:24
  50.7 1.6 %collective-permute-start.20 = (bf16[32,1152]{1,0:T(8,128)(2,1)S(1)}, bf16[32,1152]{1,0:T(8,128)(2,1)S(1)}, u32[]{:S(2)}, u32[]{:S(2)}) collective-permute-start(bf16[32,1152]{1,0:T(8,128)(2,1)S(1)} %shard_map.108), channel_id=1, source_target_pairs={{0,24},{4,28},{8,16},{12,20},{16,8},{20,12},{24,0},{28,4},{1,25},{... | collective-permute-start | bytes 221192 | tf_op jit(solution)/shard_map/ppermute | solution.py:24
  52.4 0.9 %collective-permute-start.18 = (bf16[32,1152]{1,0:T(8,128)(2,1)S(1)}, bf16[32,1152]{1,0:T(8,128)(2,1)S(1)}, u32[]{:S(2)}, u32[]{:S(2)}) collective-permute-start(bf16[32,1152]{1,0:T(8,128)(2,1)S(1)} %shard_map.107), channel_id=1, source_target_pairs={{0,4},{4,0},{8,12},{12,8},{16,20},{20,16},{24,28},{28,24},{1,5},{5... | collective-permute-start | bytes 221192 | tf_op jit(solution)/shard_map/ppermute | solution.py:24
  53.2 1.8 %collective-permute-done.22.refs_3_ = bf16[32,1152]{1,0:T(8,128)(2,1)S(1)} collective-permute-done((bf16[32,1152]{1,0:T(8,128)(2,1)S(1)}, bf16[32,1152]{1,0:T(8,128)(2,1)S(1)}, u32[]{:S(2)}, u32[]{:S(2)}) %collective-permute-start.22) | collective-permute-done | bytes 73760 | tf_op jit(solution)/shard_map/ppermute | solution.py:24
  55.1 1.9 %collective-permute-done.20.refs_2_ = bf16[32,1152]{1,0:T(8,128)(2,1)S(1)} collective-permute-done((bf16[32,1152]{1,0:T(8,128)(2,1)S(1)}, bf16[32,1152]{1,0:T(8,128)(2,1)S(1)}, u32[]{:S(2)}, u32[]{:S(2)}) %collective-permute-start.20) | collective-permute-done | bytes 73760 | tf_op jit(solution)/shard_map/ppermute | solution.py:24
  57.0 0.1 shard_map.110.refs_0_
  57.0 1.6 %collective-permute-start.24 = (bf16[32,1152]{1,0:T(8,128)(2,1)S(1)}, bf16[32,1152]{1,0:T(8,128)(2,1)S(1)}, u32[]{:S(2)}, u32[]{:S(2)}) collective-permute-start(bf16[32,1152]{1,0:T(8,128)(2,1)S(1)} %shard_map.110.refs_0_), channel_id=1, source_target_pairs={{0,2},{1,3},{2,0},{3,1},{4,6},{5,7},{6,4},{7,5},{8,10},{9,11},{10,... | collective-permute-start | bytes 221192 | tf_op jit(solution)/shard_map/ppermute | solution.py:24
  58.6 0.0 collective-permute-start.23
  58.6 2.8 %collective-permute-done.24.refs_2_ = bf16[32,1152]{1,0:T(8,128)(2,1)S(1)} collective-permute-done((bf16[32,1152]{1,0:T(8,128)(2,1)S(1)}, bf16[32,1152]{1,0:T(8,128)(2,1)S(1)}, u32[]{:S(2)}, u32[]{:S(2)}) %collective-permute-start.24) | collective-permute-done | bytes 73760 | tf_op jit(solution)/shard_map/ppermute | solution.py:24
  61.4 0.0 collective-permute-start.25
  61.4 0.0 collective-permute-done.23.refs_1_
  61.4 1.3 %collective-permute-done.25.refs_3_ = bf16[32,1152]{1,0:T(8,128)(2,1)S(1)} collective-permute-done((bf16[32,1152]{1,0:T(8,128)(2,1)S(1)}, bf16[32,1152]{1,0:T(8,128)(2,1)S(1)}, u32[]{:S(2)}, u32[]{:S(2)}) %collective-permute-start.25) | collective-permute-done | bytes 73760 | tf_op jit(solution)/shard_map/ppermute | solution.py:24
  62.7 1.5 %shard_map.111 = bf16[128,4608]{1,0:T(8,128)(2,1)} custom-call(s32[1]{0:T(128)} %bitcast.tp_at, bf16[128,32]{1,0:T(8,128)(2,1)S(1)} %get-tuple-element.41.picked, bf16[128,4608]{1,0:T(8,128)(2,1)S(1)} %copy-done, f32[32,128]{1,0:T(8,128)S(1)} %shard_map.92.weight, f32[36,128]{1,0:T(8,128)S(1)} %bitcast.11, bf16[32,1152]{1,0:T(8,128)(2,1)S(1)} %shard_map.110.refs_0_, ...), custom_call_target="tpu_custom_call" | custom-call | tf_op jit(solution)/shard_map/pallas_call | solution.py:214
  (34 shorter events, 0.2 us)
Async XLA Ops:
  2.4 7.7 %collective-permute-start = (bf16[32,1152]{1,0:T(8,128)(2,1)S(1)}, bf16[32,1152]{1,0:T(8,128)(2,1)S(1)}, u32[]{:S(2)}, u32[]{:S(2)}) collective-permute-start(bf16[32,1152]{1,0:T(8,128)(2,1)S(1)} %get-tuple-element.42.refs_0_), channel_id=1, source_target_pairs={{0,24},{4,28},{8,16},{12,20},{16,8},{20,12},{24,0},{28,4},{1,25},{... | collective-permute-start | bytes 221192 | tf_op jit(solution)/shard_map/ppermute | solution.py:24
  7.5 4.7 %collective-permute-start.1 = (bf16[32,1152]{1,0:T(8,128)(2,1)S(1)}, bf16[32,1152]{1,0:T(8,128)(2,1)S(1)}, u32[]{:S(2)}, u32[]{:S(2)}) collective-permute-start(bf16[32,1152]{1,0:T(8,128)(2,1)S(1)} %get-tuple-element.42.refs_0_), channel_id=1, source_target_pairs={{0,4},{4,0},{8,12},{12,8},{16,20},{20,16},{24,28},{28,24},{1,5},{5... | collective-permute-start | bytes 221192 | tf_op jit(solution)/shard_map/ppermute | solution.py:24
  9.0 5.7 %collective-permute-start.4 = (bf16[32,1152]{1,0:T(8,128)(2,1)S(1)}, bf16[32,1152]{1,0:T(8,128)(2,1)S(1)}, u32[]{:S(2)}, u32[]{:S(2)}) collective-permute-start(bf16[32,1152]{1,0:T(8,128)(2,1)S(1)} %get-tuple-element.42.refs_0_), channel_id=1, source_target_pairs={{0,16},{4,20},{8,24},{12,28},{16,0},{20,4},{24,8},{28,12},{1,17},{... | collective-permute-start | bytes 221192 | tf_op jit(solution)/shard_map/ppermute | solution.py:24
  9.0 6.3 %collective-permute-start.2 = (bf16[32,1152]{1,0:T(8,128)(2,1)S(1)}, bf16[32,1152]{1,0:T(8,128)(2,1)S(1)}, u32[]{:S(2)}, u32[]{:S(2)}) collective-permute-start(bf16[32,1152]{1,0:T(8,128)(2,1)S(1)} %get-tuple-element.42.refs_0_), channel_id=1, source_target_pairs={{0,8},{4,12},{8,0},{12,4},{16,24},{20,28},{24,16},{28,20},{1,9},{5... | collective-permute-start | bytes 221192 | tf_op jit(solution)/shard_map/ppermute | solution.py:24
  9.8 11.8 %slice-start = ((s8[10616832]{0:T(1024)(128)(4,1)}), s8[4194304]{0:T(1024)(128)(4,1)S(1)}, s32[]{:S(2)}) async-start(s8[10616832]{0:T(1024)(128)(4,1)} %bitcast.5), calls=%async_computation | async-start | bytes 8388608
  9.8 11.8 %slice-start.3 = ((s8[10616832]{0:T(1024)(128)(4,1)}), s8[4194304]{0:T(1024)(128)(4,1)S(1)}, s32[]{:S(2)}) async-start(s8[10616832]{0:T(1024)(128)(4,1)} %bitcast.7), calls=%async_computation.3 | async-start | bytes 8388608
  9.8 11.8 %slice-start.6 = ((s8[10616832]{0:T(1024)(128)(4,1)}), s8[4194304]{0:T(1024)(128)(4,1)S(1)}, s32[]{:S(2)}) async-start(s8[10616832]{0:T(1024)(128)(4,1)} %bitcast.9), calls=%async_computation.6 | async-start | bytes 8388608
  9.8 11.9 %slice-start.1 = ((s8[10616832]{0:T(1024)(128)(4,1)}), s8[4194304]{0:T(1024)(128)(4,1)S(1)}, s32[]{:S(2)}) async-start(s8[10616832]{0:T(1024)(128)(4,1)} %bitcast.5), calls=%async_computation.1 | async-start | bytes 8388608
  9.8 11.9 %slice-start.2 = ((s8[10616832]{0:T(1024)(128)(4,1)}), s8[2228224]{0:T(1024)(128)(4,1)S(1)}, s32[]{:S(2)}) async-start(s8[10616832]{0:T(1024)(128)(4,1)} %bitcast.5), calls=%async_computation.2 | async-start | bytes 4456448
  9.9 11.9 %slice-start.4 = ((s8[10616832]{0:T(1024)(128)(4,1)}), s8[4194304]{0:T(1024)(128)(4,1)S(1)}, s32[]{:S(2)}) async-start(s8[10616832]{0:T(1024)(128)(4,1)} %bitcast.7), calls=%async_computation.4 | async-start | bytes 8388608
  9.9 11.9 %slice-start.5 = ((s8[10616832]{0:T(1024)(128)(4,1)}), s8[2228224]{0:T(1024)(128)(4,1)S(1)}, s32[]{:S(2)}) async-start(s8[10616832]{0:T(1024)(128)(4,1)} %bitcast.7), calls=%async_computation.5 | async-start | bytes 4456448
  9.9 11.9 %slice-start.7 = ((s8[10616832]{0:T(1024)(128)(4,1)}), s8[4194304]{0:T(1024)(128)(4,1)S(1)}, s32[]{:S(2)}) async-start(s8[10616832]{0:T(1024)(128)(4,1)} %bitcast.9), calls=%async_computation.7 | async-start | bytes 8388608
  9.9 11.9 %slice-start.8 = ((s8[10616832]{0:T(1024)(128)(4,1)}), s8[2228224]{0:T(1024)(128)(4,1)S(1)}, s32[]{:S(2)}) async-start(s8[10616832]{0:T(1024)(128)(4,1)} %bitcast.9), calls=%async_computation.8 | async-start | bytes 4456448
  10.1 5.2 %collective-permute-start.6 = (bf16[32,1152]{1,0:T(8,128)(2,1)S(1)}, bf16[32,1152]{1,0:T(8,128)(2,1)S(1)}, u32[]{:S(2)}, u32[]{:S(2)}) collective-permute-start(bf16[32,1152]{1,0:T(8,128)(2,1)S(1)} %collective-permute-done.refs_6_), channel_id=1, source_target_pairs={{0,4},{4,0},{8,12},{12,8},{16,20},{20,16},{24,28},{28,24},{1,5},{5... | collective-permute-start | bytes 221192 | tf_op jit(solution)/shard_map/ppermute | solution.py:24
  12.2 4.8 %collective-permute-start.3 = (bf16[32,1152]{1,0:T(8,128)(2,1)S(1)}, bf16[32,1152]{1,0:T(8,128)(2,1)S(1)}, u32[]{:S(2)}, u32[]{:S(2)}) collective-permute-start(bf16[32,1152]{1,0:T(8,128)(2,1)S(1)} %collective-permute-done.1.refs_1_), channel_id=1, source_target_pairs={{0,8},{4,12},{8,0},{12,4},{16,24},{20,28},{24,16},{28,20},{1,9},{5... | collective-permute-start | bytes 221192 | tf_op jit(solution)/shard_map/ppermute | solution.py:24
  14.7 4.4 %collective-permute-start.5 = (bf16[32,1152]{1,0:T(8,128)(2,1)S(1)}, bf16[32,1152]{1,0:T(8,128)(2,1)S(1)}, u32[]{:S(2)}, u32[]{:S(2)}) collective-permute-start(bf16[32,1152]{1,0:T(8,128)(2,1)S(1)} %collective-permute-done.4.refs_4_), channel_id=1, source_target_pairs={{0,4},{4,0},{8,12},{12,8},{16,20},{20,16},{24,28},{28,24},{1,5},{5... | collective-permute-start | bytes 221192 | tf_op jit(solution)/shard_map/ppermute | solution.py:24
  19.5 2.2 %collective-permute-start.9 = (bf16[128,1152]{1,0:T(8,128)(2,1)S(1)}, bf16[128,1152]{1,0:T(8,128)(2,1)S(1)}, u32[]{:S(2)}, u32[]{:S(2)}) collective-permute-start(bf16[128,1152]{1,0:T(8,128)(2,1)S(1)} %get-tuple-element.49.first), channel_id=1, source_target_pairs={{0,1},{1,0},{2,3},{3,2},{4,5},{5,4},{6,7},{7,6},{8,9},{9,8},{10,11... | collective-permute-start | bytes 884744 | tf_op jit(solution)/shard_map/ppermute | solution.py:24
  19.6 7.1 %collective-permute-start.8 = (bf16[128,640]{1,0:T(8,128)(2,1)S(1)}, bf16[128,640]{1,0:T(8,128)(2,1)S(1)}, u32[]{:S(2)}, u32[]{:S(2)}) collective-permute-start(bf16[128,640]{1,0:T(8,128)(2,1)S(1)} %get-tuple-element.48), channel_id=1, source_target_pairs={{0,2},{1,3},{2,0},{3,1},{4,6},{5,7},{6,4},{7,5},{8,10},{9,11},{10,... | collective-permute-start | bytes 491528 | tf_op jit(solution)/shard_map/ppermute | solution.py:24
  21.2 7.8 %collective-permute-start.7 = (bf16[128,512]{1,0:T(8,128)(2,1)S(1)}, bf16[128,512]{1,0:T(8,128)(2,1)S(1)}, u32[]{:S(2)}, u32[]{:S(2)}) collective-permute-start(bf16[128,512]{1,0:T(8,128)(2,1)S(1)} %get-tuple-element.47), channel_id=1, source_target_pairs={{0,2},{1,3},{2,0},{3,1},{4,6},{5,7},{6,4},{7,5},{8,10},{9,11},{10,... | collective-permute-start | bytes 393224 | tf_op jit(solution)/shard_map/ppermute | solution.py:24
  26.7 2.3 %collective-permute-start.11 = (bf16[128,640]{1,0:T(8,128)(2,1)S(1)}, bf16[128,640]{1,0:T(8,128)(2,1)S(1)}, u32[]{:S(2)}, u32[]{:S(2)}) collective-permute-start(bf16[128,640]{1,0:T(8,128)(2,1)S(1)} %collective-permute-done.8.refs_0_), channel_id=1, source_target_pairs={{0,1},{1,0},{2,3},{3,2},{4,5},{5,4},{6,7},{7,6},{8,9},{9,8},{10,11... | collective-permute-start | bytes 491528 | tf_op jit(solution)/shard_map/ppermute | solution.py:24
  29.0 1.3 %collective-permute-start.10 = (bf16[128,512]{1,0:T(8,128)(2,1)S(1)}, bf16[128,512]{1,0:T(8,128)(2,1)S(1)}, u32[]{:S(2)}, u32[]{:S(2)}) collective-permute-start(bf16[128,512]{1,0:T(8,128)(2,1)S(1)} %collective-permute-done.7.refs_1_), channel_id=1, source_target_pairs={{0,1},{1,0},{2,3},{3,2},{4,5},{5,4},{6,7},{7,6},{8,9},{9,8},{10,11... | collective-permute-start | bytes 393224 | tf_op jit(solution)/shard_map/ppermute | solution.py:24
  31.3 2.3 %collective-permute-start.13 = (bf16[128,640]{1,0:T(8,128)(2,1)S(1)}, bf16[128,640]{1,0:T(8,128)(2,1)S(1)}, u32[]{:S(2)}, u32[]{:S(2)}) collective-permute-start(bf16[128,640]{1,0:T(8,128)(2,1)S(1)} %shard_map.100), channel_id=1, source_target_pairs={{0,1},{1,0},{2,3},{3,2},{4,5},{5,4},{6,7},{7,6},{8,9},{9,8},{10,11... | collective-permute-start | bytes 491528 | tf_op jit(solution)/shard_map/ppermute | solution.py:24
  32.2 4.0 %collective-permute-start.12 = (bf16[128,1152]{1,0:T(8,128)(2,1)S(1)}, bf16[128,1152]{1,0:T(8,128)(2,1)S(1)}, u32[]{:S(2)}, u32[]{:S(2)}) collective-permute-start(bf16[128,1152]{1,0:T(8,128)(2,1)S(1)} %shard_map.98), channel_id=1, source_target_pairs={{0,1},{1,0},{2,3},{3,2},{4,5},{5,4},{6,7},{7,6},{8,9},{9,8},{10,11... | collective-permute-start | bytes 884744 | tf_op jit(solution)/shard_map/ppermute | solution.py:24
  32.9 2.7 %collective-permute-start.15 = (bf16[128,512]{1,0:T(8,128)(2,1)S(1)}, bf16[128,512]{1,0:T(8,128)(2,1)S(1)}, u32[]{:S(2)}, u32[]{:S(2)}) collective-permute-start(bf16[128,512]{1,0:T(8,128)(2,1)S(1)} %shard_map.103), channel_id=1, source_target_pairs={{0,1},{1,0},{2,3},{3,2},{4,5},{5,4},{6,7},{7,6},{8,9},{9,8},{10,11... | collective-permute-start | bytes 393224 | tf_op jit(solution)/shard_map/ppermute | solution.py:24
  33.7 29.0 %copy-start = (bf16[128,4608]{1,0:T(8,128)(2,1)S(1)}, bf16[128,4608]{1,0:T(8,128)(2,1)}, u32[]{:S(2)}) copy-start(bf16[128,4608]{1,0:T(8,128)(2,1)} %tokens.3) | copy-start | bytes 3538948
  33.7 29.0 %copy-start.1 = (f32[4608]{0:T(1024)S(1)}, f32[4608]{0:T(1024)}, u32[]{:S(2)}) copy-start(f32[4608]{0:T(1024)} %param.14) | copy-start | bytes 55300
  33.7 9.3 %collective-permute-start.14 = (bf16[128,640]{1,0:T(8,128)(2,1)S(1)}, bf16[128,640]{1,0:T(8,128)(2,1)S(1)}, u32[]{:S(2)}, u32[]{:S(2)}) collective-permute-start(bf16[128,640]{1,0:T(8,128)(2,1)S(1)} %shard_map.102), channel_id=1, source_target_pairs={{0,2},{1,3},{2,0},{3,1},{4,6},{5,7},{6,4},{7,5},{8,10},{9,11},{10,... | collective-permute-start | bytes 491528 | tf_op jit(solution)/shard_map/ppermute | solution.py:24
  35.7 7.3 %collective-permute-start.16 = (bf16[128,512]{1,0:T(8,128)(2,1)S(1)}, bf16[128,512]{1,0:T(8,128)(2,1)S(1)}, u32[]{:S(2)}, u32[]{:S(2)}) collective-permute-start(bf16[128,512]{1,0:T(8,128)(2,1)S(1)} %shard_map.105), channel_id=1, source_target_pairs={{0,2},{1,3},{2,0},{3,1},{4,6},{5,7},{6,4},{7,5},{8,10},{9,11},{10,... | collective-permute-start | bytes 393224 | tf_op jit(solution)/shard_map/ppermute | solution.py:24
  43.3 9.0 %collective-permute-start.17 = (bf16[64,1152]{1,0:T(8,128)(2,1)S(1)}, bf16[64,1152]{1,0:T(8,128)(2,1)S(1)}, u32[]{:S(2)}, u32[]{:S(2)}) collective-permute-start(bf16[64,1152]{1,0:T(8,128)(2,1)S(1)} %get-tuple-element.70), channel_id=1, source_target_pairs={{0,8},{4,12},{8,0},{12,4},{16,24},{20,28},{24,16},{28,20},{1,9},{5... | collective-permute-start | bytes 442376 | tf_op jit(solution)/shard_map/ppermute | solution.py:24
  43.5 4.4 %collective-permute-start.21 = (bf16[32,1152]{1,0:T(8,128)(2,1)S(1)}, bf16[32,1152]{1,0:T(8,128)(2,1)S(1)}, u32[]{:S(2)}, u32[]{:S(2)}) collective-permute-start(bf16[32,1152]{1,0:T(8,128)(2,1)S(1)} %get-tuple-element.76), channel_id=1, source_target_pairs={{0,4},{4,0},{8,12},{12,8},{16,20},{20,16},{24,28},{28,24},{1,5},{5... | collective-permute-start | bytes 221192 | tf_op jit(solution)/shard_map/ppermute | solution.py:24
  44.5 6.2 %collective-permute-start.19 = (bf16[32,1152]{1,0:T(8,128)(2,1)S(1)}, bf16[32,1152]{1,0:T(8,128)(2,1)S(1)}, u32[]{:S(2)}, u32[]{:S(2)}) collective-permute-start(bf16[32,1152]{1,0:T(8,128)(2,1)S(1)} %get-tuple-element.74), channel_id=1, source_target_pairs={{0,4},{4,0},{8,12},{12,8},{16,20},{20,16},{24,28},{28,24},{1,5},{5... | collective-permute-start | bytes 221192 | tf_op jit(solution)/shard_map/ppermute | solution.py:24
  47.9 7.1 %collective-permute-start.22 = (bf16[32,1152]{1,0:T(8,128)(2,1)S(1)}, bf16[32,1152]{1,0:T(8,128)(2,1)S(1)}, u32[]{:S(2)}, u32[]{:S(2)}) collective-permute-start(bf16[32,1152]{1,0:T(8,128)(2,1)S(1)} %shard_map.109), channel_id=1, source_target_pairs={{0,16},{4,20},{8,24},{12,28},{16,0},{20,4},{24,8},{28,12},{1,17},{... | collective-permute-start | bytes 221192 | tf_op jit(solution)/shard_map/ppermute | solution.py:24
  50.7 6.2 %collective-permute-start.20 = (bf16[32,1152]{1,0:T(8,128)(2,1)S(1)}, bf16[32,1152]{1,0:T(8,128)(2,1)S(1)}, u32[]{:S(2)}, u32[]{:S(2)}) collective-permute-start(bf16[32,1152]{1,0:T(8,128)(2,1)S(1)} %shard_map.108), channel_id=1, source_target_pairs={{0,24},{4,28},{8,16},{12,20},{16,8},{20,12},{24,0},{28,4},{1,25},{... | collective-permute-start | bytes 221192 | tf_op jit(solution)/shard_map/ppermute | solution.py:24
  52.4 4.6 %collective-permute-start.18 = (bf16[32,1152]{1,0:T(8,128)(2,1)S(1)}, bf16[32,1152]{1,0:T(8,128)(2,1)S(1)}, u32[]{:S(2)}, u32[]{:S(2)}) collective-permute-start(bf16[32,1152]{1,0:T(8,128)(2,1)S(1)} %shard_map.107), channel_id=1, source_target_pairs={{0,4},{4,0},{8,12},{12,8},{16,20},{20,16},{24,28},{28,24},{1,5},{5... | collective-permute-start | bytes 221192 | tf_op jit(solution)/shard_map/ppermute | solution.py:24
  57.0 4.4 %collective-permute-start.24 = (bf16[32,1152]{1,0:T(8,128)(2,1)S(1)}, bf16[32,1152]{1,0:T(8,128)(2,1)S(1)}, u32[]{:S(2)}, u32[]{:S(2)}) collective-permute-start(bf16[32,1152]{1,0:T(8,128)(2,1)S(1)} %shard_map.110.refs_0_), channel_id=1, source_target_pairs={{0,2},{1,3},{2,0},{3,1},{4,6},{5,7},{6,4},{7,5},{8,10},{9,11},{10,... | collective-permute-start | bytes 221192 | tf_op jit(solution)/shard_map/ppermute | solution.py:24
  58.6 2.9 %collective-permute-start.23 = (bf16[32,1152]{1,0:T(8,128)(2,1)S(1)}, bf16[32,1152]{1,0:T(8,128)(2,1)S(1)}, u32[]{:S(2)}, u32[]{:S(2)}) collective-permute-start(bf16[32,1152]{1,0:T(8,128)(2,1)S(1)} %shard_map.110.refs_0_), channel_id=1, source_target_pairs={{0,1},{1,0},{2,3},{3,2},{4,5},{5,4},{6,7},{7,6},{8,9},{9,8},{10,11... | collective-permute-start | bytes 221192 | tf_op jit(solution)/shard_map/ppermute | solution.py:24
  61.4 1.3 %collective-permute-start.25 = (bf16[32,1152]{1,0:T(8,128)(2,1)S(1)}, bf16[32,1152]{1,0:T(8,128)(2,1)S(1)}, u32[]{:S(2)}, u32[]{:S(2)}) collective-permute-start(bf16[32,1152]{1,0:T(8,128)(2,1)S(1)} %collective-permute-done.24.refs_2_), channel_id=1, source_target_pairs={{0,1},{1,0},{2,3},{3,2},{4,5},{5,4},{6,7},{7,6},{8,9},{9,8},{10,11... | collective-permute-start | bytes 221192 | tf_op jit(solution)/shard_map/ppermute | solution.py:24
